TPU v7x, 32 devices: a whole 2x2x4 slice. The times are simulated.
32 devices in a mesh: seq: 8 (over y, x, core), wshard: 4 (over z).
Axes of the slice: x: 2, y: 2, z: 4, core: 2. Of those that a mesh axis runs over, the one named last changes fastest.
Arguments:
- block_in: bfloat16 [4, 2048, 1536], P('wshard', 'seq'), may hold values from -6 to 6
- cotangent: bfloat16 [4, 2048, 1536], P('wshard', 'seq'), may hold values from -6 to 6
- in_weight: float32 [1536, 6448], P(('seq', 'wshard')), may hold values from -0.15625 to 0.15625
- out_weight: float32 [3072, 1536], P(('seq', 'wshard')), may hold values from -0.109375 to 0.109375
- in_gain: float32 [1536], replicated, may hold values from 0.5 to 1.5
- out_gain: float32 [3072], replicated, may hold values from 0.5 to 1.5
- conv_inner: float32 [5, 3072], replicated, may hold values from -3 to 3
- conv_shared: float32 [5, 256], replicated, may hold values from -3 to 3
- head_params: float32 [3, 48], replicated, may hold values from -5 to 1.5, as said below
- first_in_weight: float32 [1536, 6448], P(('seq', 'wshard')), may hold values from -6 to 6
- first_out_weight: float32 [3072, 1536], P(('seq', 'wshard')), may hold values from -6 to 6
- first_in_gain: float32 [1536], replicated, may hold values from -6 to 6
- first_out_gain: float32 [3072], replicated, may hold values from -6 to 6
- first_conv_inner: float32 [5, 3072], replicated, may hold values from -6 to 6
- first_conv_shared: float32 [5, 256], replicated, may hold values from -6 to 6
- first_head_params: float32 [3, 48], replicated, may hold values from -6 to 6
- second_in_weight: float32 [1536, 6448], P(('seq', 'wshard')), may hold values from 0.01 to 1
- second_out_weight: float32 [3072, 1536], P(('seq', 'wshard')), may hold values from 0.01 to 1
- second_in_gain: float32 [1536], replicated, may hold values from 16.384 to 1638.4
- second_out_gain: float32 [3072], replicated, may hold values from 0.01 to 1
- second_conv_inner: float32 [5, 3072], replicated, may hold values from 0.01 to 1
- second_conv_shared: float32 [5, 256], replicated, may hold values from 0.01 to 1
- second_head_params: float32 [3, 48], replicated, may hold values from 0.01 to 1
Outputs:
- block_out: float32 [4, 2048, 1536], P('wshard', 'seq')
- grad_in: float32 [4, 2048, 1536], P('wshard', 'seq')
- grad_in_weight: float32 [1536, 6448], P(('seq', 'wshard'))
- grad_out_weight: float32 [3072, 1536], P(('seq', 'wshard'))
- grad_in_gain: float32 [1536], replicated
- grad_out_gain: float32 [3072], replicated
- grad_conv_inner: float32 [5, 3072], replicated
- grad_conv_shared: float32 [5, 256], replicated
- grad_head_params: float32 [3, 48], replicated
- new_in_weight: float32 [1536, 6448], P(('seq', 'wshard'))
- new_out_weight: float32 [3072, 1536], P(('seq', 'wshard'))
- updated_input_gain: float32 [1536], replicated
- new_out_gain: float32 [3072], replicated
- new_conv_inner: float32 [5, 3072], replicated
- new_conv_shared: float32 [5, 256], replicated
- new_head_params: float32 [3, 48], replicated
- new_first_in_weight: float32 [1536, 6448], P(('seq', 'wshard'))
- new_first_out_weight: float32 [3072, 1536], P(('seq', 'wshard'))
- new_first_in_gain: float32 [1536], replicated
- new_first_out_gain: float32 [3072], replicated
- new_first_conv_inner: float32 [5, 3072], replicated
- new_first_conv_shared: float32 [5, 256], replicated
- updated_head_first_moment: float32 [3, 48], replicated
- new_second_in_weight: float32 [1536, 6448], P(('seq', 'wshard'))
- new_second_out_weight: float32 [3072, 1536], P(('seq', 'wshard'))
- new_second_in_gain: float32 [1536], replicated
- new_second_out_gain: float32 [3072], replicated
- new_second_conv_inner: float32 [5, 3072], replicated
- new_second_conv_shared: float32 [5, 256], replicated
- new_second_head_params: float32 [2, 48], replicated
- new_second_skip: float32 [48], replicated
Inputs may be any that keep to these rules, and one draw needn't show every extreme that they name: `head_params`: row 0 holds step biases, row 1 logarithms of decay rates, row 2 skip gains.
All inputs are finite; a program needn't handle non-finite values.
Results may differ from a plain program's by a relative error of at most 0.02.
The roundings to bfloat16 on the way count: a program that leaves them out, or rounds other values in their place, can miss the bound.
Values may be sent and summed in bfloat16 or wider, within the bound.
A program may use at most 256 MiB of HBM per device.

v0:
```python
import jax
import jax.numpy as jnp
from jax import lax
from jax.sharding import PartitionSpec as P

P_SIZE = 64
N_STATE = 128
BLOCK_LEN = 256
E = 3072


norm_eps = 1e-05
beta_one = 0.9
beta_two = 0.95
adam_eps = 1e-08
adam_step = 3.0
weight_learning_rate = 0.01
matrix_decay = 0.1
small_rate = 0.1


def causal_conv(values, taps):
    length = values.shape[1]
    width = taps.shape[0] - 1
    padded = jnp.pad(values, ((0, 0), (width - 1, 0), (0, 0)))
    total = taps[width] + taps[0] * padded[:, 0:length]
    for shift in range(1, width):
        total = total + taps[shift] * padded[:, shift : shift + length]
    return total


def block_step(state, inputs):
    inner_part, step_part, learning_rate_piece, b_part, c_part = inputs
    high = lax.Precision.HIGHEST
    cumul = jnp.cumsum(learning_rate_piece, axis=1)
    scores = jnp.einsum("sin,sjn->sij", c_part, b_part, precision=high)
    rows = lax.broadcasted_iota(jnp.int32, (BLOCK_LEN, BLOCK_LEN), 0)
    cols = lax.broadcasted_iota(jnp.int32, (BLOCK_LEN, BLOCK_LEN), 1)
    lower = (rows >= cols)[None, :, :, None]
    spread = cumul[:, :, None, :] - cumul[:, None, :, :]
    decay = jnp.where(lower, jnp.exp(jnp.where(lower, spread, 0.0)), 0.0)
    weights = scores[..., None] * decay * step_part[:, None, :, :]
    within = jnp.einsum("sijh,sjhp->sihp", weights, inner_part, precision=high)
    carried = (
        jnp.einsum("sin,shpn->sihp", c_part, state, precision=high) * jnp.exp(cumul)[..., None]
    )
    tail = jnp.exp(cumul[:, -1:, :] - cumul) * step_part
    fresh = jnp.einsum("sjn,sjh,sjhp->shpn", b_part, tail, inner_part, precision=high)
    new_state = jnp.exp(cumul[:, -1, :])[:, :, None, None] * state + fresh
    return (new_state, within + carried)


def state_space(inner, step, rate, b_mat, c_mat):
    batch, length, heads, head_size = inner.shape
    blocks = length // BLOCK_LEN

    def blockify(values):
        return jnp.moveaxis(values.reshape((batch, blocks, BLOCK_LEN) + values.shape[2:]), 1, 0)

    start = jnp.zeros((batch, heads, head_size, b_mat.shape[2]), dtype=inner.dtype)
    _, outputs = lax.scan(
        jax.checkpoint(block_step),
        start,
        (blockify(inner), blockify(step), blockify(rate), blockify(b_mat), blockify(c_mat)),
    )
    return jnp.moveaxis(outputs, 0, 1).reshape(batch, length, heads, head_size)


def mixer(gate_inner, shared, step_raw, conv_local, conv_common, head_local):
    batch, length = (gate_inner.shape[0], gate_inner.shape[1])
    heads = step_raw.shape[2]
    parts = gate_inner.reshape(batch, length, heads, 2, P_SIZE)
    gate_vals = parts[:, :, :, 0, :].reshape(batch, length, heads * P_SIZE)
    inner_vals = parts[:, :, :, 1, :].reshape(batch, length, heads * P_SIZE)
    inner_act = jax.nn.silu(causal_conv(inner_vals, conv_local))
    shared_act = jax.nn.silu(causal_conv(shared, conv_common))
    half = shared.shape[2] // 2
    step = jax.nn.softplus(step_raw + head_local[0])
    rate = -step * jnp.exp(head_local[1])
    inner_heads = inner_act.reshape(batch, length, heads, P_SIZE)
    output = state_space(inner_heads, step, rate, shared_act[..., :half], shared_act[..., half:])
    output = output + head_local[2][:, None] * inner_heads
    return output.reshape(batch, length, heads * P_SIZE) * jax.nn.silu(gate_vals)


def adamw(param, grad, first, second_moment, rate, decay):
    first_new = beta_one * first + (1.0 - beta_one) * grad
    second_new = beta_two * second_moment + (1.0 - beta_two) * grad * grad
    corrected = (
        first_new
        / (1.0 - beta_one**adam_step)
        / (jnp.sqrt(second_new / (1.0 - beta_two**adam_step)) + adam_eps)
    )
    return (param - rate * (corrected + decay * param), first_new, second_new)


def local(
    block_in,
    cotangent,
    in_weight,
    out_weight,
    in_gain,
    out_gain,
    conv_inner,
    conv_shared,
    head_params,
    first_in_weight,
    first_out_weight,
    first_in_gain,
    first_out_gain,
    first_conv_inner,
    first_conv_shared,
    first_head_params,
    second_in_weight,
    second_out_weight,
    second_in_gain,
    second_out_gain,
    second_conv_inner,
    second_conv_shared,
    second_head_params,
):
    seq_index = lax.axis_index("seq")
    inputs = block_in.astype(jnp.float32)
    rms_in = lax.rsqrt(jnp.mean(inputs * inputs, axis=-1, keepdims=True) + norm_eps)
    normed = (inputs * rms_in * in_gain).astype(jnp.bfloat16)
    in_w16 = in_weight.astype(jnp.bfloat16)
    out_w16 = out_weight.astype(jnp.bfloat16)
    column_list = normed
    projected = jnp.einsum(
        "fbe,ek->fbk",
        column_list,
        lax.all_gather(in_w16, ("seq", "wshard"), axis=0, tiled=True),
        preferred_element_type=jnp.float32,
    ).astype(jnp.bfloat16)
    gate_inner = projected[:, :, : 2 * E]
    shared = projected[:, :, 2 * E : 2 * E + 2 * N_STATE]
    step_raw = projected[:, :, 2 * E + 2 * N_STATE :]
    head_gate, head_step = (
        lax.all_to_all(gate_inner, "seq", split_axis=2, concat_axis=1, tiled=True),
        lax.all_to_all(step_raw, "seq", split_axis=2, concat_axis=1, tiled=True),
    )
    head_shared = lax.all_gather(shared, "seq", axis=1, tiled=True)
    heads_dev = head_step.shape[2]
    inner_start = seq_index * (heads_dev * P_SIZE)
    conv_local = lax.dynamic_slice_in_dim(conv_inner, inner_start, heads_dev * P_SIZE, 1)
    head_local = lax.dynamic_slice_in_dim(head_params, seq_index * heads_dev, heads_dev, 1)
    gated, mixer_back = jax.vjp(
        mixer,
        head_gate.astype(jnp.float32),
        head_shared.astype(jnp.float32),
        head_step.astype(jnp.float32),
        conv_local,
        conv_shared,
        head_local,
    )
    gated32 = lax.all_to_all(
        gated.astype(jnp.bfloat16), "seq", split_axis=1, concat_axis=2, tiled=True
    ).astype(jnp.float32)
    rms_out = lax.rsqrt(jnp.mean(gated32 * gated32, axis=-1, keepdims=True) + norm_eps)
    gnormed = (gated32 * rms_out * out_gain).astype(jnp.bfloat16)
    column_list = gnormed
    mixed = jnp.einsum(
        "brg,ga->bra",
        column_list,
        lax.all_gather(out_w16, ("seq", "wshard"), axis=0, tiled=True),
        preferred_element_type=jnp.float32,
    )
    d_gnormed = jnp.einsum(
        "oum,am->oua",
        cotangent,
        lax.all_gather(out_w16, ("seq", "wshard"), axis=0, tiled=True),
        preferred_element_type=jnp.float32,
    )
    block_out = inputs + mixed
    d_out_gain = jnp.sum(d_gnormed * gated32 * rms_out, axis=(0, 1))
    scaled = d_gnormed * out_gain
    d_gated = (
        rms_out * scaled - gated32 * rms_out**3 * jnp.mean(scaled * gated32, axis=-1, keepdims=True)
    ).astype(jnp.bfloat16)
    head_cotan = lax.all_to_all(d_gated, "seq", split_axis=2, concat_axis=1, tiled=True).astype(
        jnp.float32
    )
    d_gate, d_shared, d_step, d_conv_local, d_common, d_head_local = mixer_back(head_cotan)
    tok_gate, tok_step = (
        lax.all_to_all(d_gate.astype(jnp.bfloat16), "seq", split_axis=1, concat_axis=2, tiled=True),
        lax.all_to_all(d_step.astype(jnp.bfloat16), "seq", split_axis=1, concat_axis=2, tiled=True),
    )
    shared_sum = lax.psum_scatter(
        d_shared.astype(jnp.bfloat16), "seq", scatter_dimension=1, tiled=True
    )
    projected_gradient = jnp.concatenate([tok_gate, shared_sum, tok_step], axis=2)
    d_normed = jnp.einsum(
        "ozu,hu->ozh",
        projected_gradient,
        lax.all_gather(in_w16, ("seq", "wshard"), axis=0, tiled=True),
        preferred_element_type=jnp.float32,
    )
    d_in_gain = jnp.sum(d_normed * inputs * rms_in, axis=(0, 1))
    scaled_in = d_normed * in_gain
    grad_in = (
        cotangent.astype(jnp.float32)
        + rms_in * scaled_in
        - inputs * rms_in**3 * jnp.mean(scaled_in * inputs, axis=-1, keepdims=True)
    )
    d_conv_full = lax.dynamic_update_slice_in_dim(
        jnp.zeros_like(conv_inner), d_conv_local, inner_start, 1
    )
    d_head_full = lax.dynamic_update_slice_in_dim(
        jnp.zeros_like(head_params), d_head_local, seq_index * heads_dev, 1
    )
    grad_in_gain, grad_out_gain, grad_conv_inner, grad_conv_shared, grad_head_params = lax.psum(
        (d_in_gain, d_out_gain, d_conv_full, d_common, d_head_full), ("seq", "wshard")
    )
    column_list = normed
    grad_in_weight = lax.psum_scatter(
        jnp.einsum(
            "nkm,nkc->mc", column_list, projected_gradient, preferred_element_type=jnp.float32
        ),
        ("seq", "wshard"),
        scatter_dimension=0,
        tiled=True,
    )
    column_list = gnormed
    grad_out_weight = lax.psum_scatter(
        jnp.einsum("kcb,kch->bh", column_list, cotangent, preferred_element_type=jnp.float32),
        ("seq", "wshard"),
        scatter_dimension=0,
        tiled=True,
    )
    new_in_weight, new_first_in_weight, new_second_in_weight = adamw(
        in_weight,
        grad_in_weight,
        first_in_weight,
        second_in_weight,
        weight_learning_rate,
        matrix_decay,
    )
    new_out_weight, new_first_out_weight, new_second_out_weight = adamw(
        out_weight,
        grad_out_weight,
        first_out_weight,
        second_out_weight,
        weight_learning_rate,
        matrix_decay,
    )
    updated_input_gain, new_first_in_gain, new_second_in_gain = adamw(
        in_gain, grad_in_gain, first_in_gain, second_in_gain, small_rate, 0.0
    )
    new_out_gain, new_first_out_gain, new_second_out_gain = adamw(
        out_gain, grad_out_gain, first_out_gain, second_out_gain, small_rate, 0.0
    )
    new_conv_inner, new_first_conv_inner, new_second_conv_inner = adamw(
        conv_inner, grad_conv_inner, first_conv_inner, second_conv_inner, small_rate, 0.0
    )
    new_conv_shared, new_first_conv_shared, new_second_conv_shared = adamw(
        conv_shared, grad_conv_shared, first_conv_shared, second_conv_shared, small_rate, 0.0
    )
    new_head_params, updated_head_first_moment, head_second_all = adamw(
        head_params, grad_head_params, first_head_params, second_head_params, small_rate, 0.0
    )
    return (
        block_out,
        grad_in,
        grad_in_weight,
        grad_out_weight,
        grad_in_gain,
        grad_out_gain,
        grad_conv_inner,
        grad_conv_shared,
        grad_head_params,
        new_in_weight,
        new_out_weight,
        updated_input_gain,
        new_out_gain,
        new_conv_inner,
        new_conv_shared,
        new_head_params,
        new_first_in_weight,
        new_first_out_weight,
        new_first_in_gain,
        new_first_out_gain,
        new_first_conv_inner,
        new_first_conv_shared,
        updated_head_first_moment,
        new_second_in_weight,
        new_second_out_weight,
        new_second_in_gain,
        new_second_out_gain,
        new_second_conv_inner,
        new_second_conv_shared,
        head_second_all[0:2],
        head_second_all[2],
    )


def solution(mesh):
    return jax.shard_map(
        local,
        mesh=mesh,
        in_specs=(
            P("wshard", "seq", None),
            P("wshard", "seq", None),
            P(("seq", "wshard"), None),
            P(("seq", "wshard"), None),
            P(),
            P(),
            P(),
            P(),
            P(),
            P(("seq", "wshard"), None),
            P(("seq", "wshard"), None),
            P(),
            P(),
            P(),
            P(),
            P(),
            P(("seq", "wshard"), None),
            P(("seq", "wshard"), None),
            P(),
            P(),
            P(),
            P(),
            P(),
        ),
        out_specs=(
            P("wshard", "seq", None),
            P("wshard", "seq", None),
            P(("seq", "wshard"), None),
            P(("seq", "wshard"), None),
            P(),
            P(),
            P(),
            P(),
            P(),
            P(("seq", "wshard"), None),
            P(("seq", "wshard"), None),
            P(),
            P(),
            P(),
            P(),
            P(),
            P(("seq", "wshard"), None),
            P(("seq", "wshard"), None),
            P(),
            P(),
            P(),
            P(),
            P(),
            P(("seq", "wshard"), None),
            P(("seq", "wshard"), None),
            P(),
            P(),
            P(),
            P(),
            P(),
            P(),
        ),
        check_vma=False,
    )
```

profile of v0, /device:TPU:0, one launch (start us, length us, event | category | flops | bytes accessed | tf_op | source)
XLA Modules:
  0.0 2023.6 jit_solution(13329375079531035761)
XLA Ops:
  11.6 132.1 %all-gather.4.cloned.1.call-done = bf16[1536,6448]{1,0:T(8,128)(2,1)} async-done(((bf16[48,6448]{1,0:T(8,128)(2,1)}), bf16[1536,6448]{1,0:T(8,128)(2,1)}) %all-gather.4.cloned.1.call-update) | async-done | bytes 19808272 | tf_op jit(solution)/shard_map/all_gather | solution.py:132
  143.6 14.0 fusion.107
  167.6 37.2 %copy.613 = bf16[1,256,6144]{1,0,2:T(2,128)(2,1)} copy(bf16[1,256,6144]{1,2,0:T(8,128)(2,1)S(1)} %slice.200) | data formatting | bytes 6291456 | tf_op jit(solution)/shard_map/slice | solution.py:135
  204.9 31.5 %reduce.89 = bf16[6144,256]{1,0:T(8,128)(2,1)S(1)} reduce(bf16[6144,1,256]{2,1,0:T(2,128)(2,1)} %bitcast.657, bf16[]{:T(256)} %broadcast.1020), dimensions={1}, to_apply=%bitcast.470.reduce_sub_computation | reduce | bytes 6291458
  240.0 4.6 all-to-all-start.1
  259.4 23.1 %all-to-all-done.1 = bf16[8,2,98304]{2,1,0:T(2,128)(2,1)S(1)} async-done(((bf16[8,2,98304]{2,1,0:T(2,128)(2,1)}), bf16[8,2,98304]{2,1,0:T(2,128)(2,1)S(1)}, u32[]{:S(2)}, u32[]{:S(2)}) %all-to-all-start.1) | async-done | bytes 3145760 | tf_op jit(solution)/shard_map/all_to_all | solution.py:139
  282.4 5.3 reshape.1694
  287.7 9.1 copy.611
  296.8 7.1 reshape.1633
  307.2 4.5 fusion.118
  317.7 185.0 %while.44 = (s32[]{:T(128)}, f32[1,6,64,128]{3,2,1,0:T(8,128)S(1)}, f32[8,1,256,6,64]{2,0,4,3,1:T(8,128)}, f32[8,1,6,64,128]{4,3,2,1,0:T(8,128)}, f32[8,1,256,6]...) while((s32[]{:T(128)}, f32[1,6,64,128]{3,2,1,0:T(8,128)S(1)}, ...), condition=%wide.region_4.5_spmd.clone.clone, body=%wide.region_1.4_spmd.clone.clone.sunk | while | flops 707349504 | bytes 5805416 | solution.py:61
  331.4 9.8 dynamic_update_slice.95
  354.5 9.8 dynamic_update_slice.95
  377.6 9.8 dynamic_update_slice.95
  400.6 9.8 dynamic_update_slice.95
  423.7 9.8 dynamic_update_slice.95
  446.7 9.8 dynamic_update_slice.95
  469.8 9.8 dynamic_update_slice.95
  492.8 9.8 dynamic_update_slice.95
  502.7 4.6 transpose.193
  507.3 4.8 multiply_convert_fusion.1
  512.0 8.5 copy.488
  520.5 35.5 %reduce.90 = bf16[2048,384]{1,0:T(8,128)(2,1)} reduce(bf16[2048,1,384]{2,1,0:T(2,128)(2,1)} %bitcast.669, bf16[]{:T(256)} %broadcast.1020), dimensions={1}, to_apply=%bitcast.432.reduce_sub_computation | reduce | bytes 3145730
  559.7 4.3 all-to-all-start.2
  564.1 20.9 %all-to-all-done.2 = bf16[8,2,49152]{2,1,0:T(2,128)(2,1)} async-done(((bf16[8,2,49152]{2,1,0:T(2,128)(2,1)}), bf16[8,2,49152]{2,1,0:T(2,128)(2,1)}, u32[]{:S(2)}, u32[]{:S(2)}) %all-to-all-start.2) | async-done | bytes 1572896 | tf_op jit(solution)/shard_map/all_to_all | solution.py:156
  585.1 6.5 reshape.1696
  600.2 10.7 fusion.139
  610.9 204.3 %reduce-scatter.8.cloned.1.call-done = f32[96,1536]{1,0:T(8,128)} async-done(((f32[3072,1536]{1,0:T(8,128)}), f32[96,1536]{1,0:T(8,128)}) %reduce-scatter.8.cloned.1.call-update) | async-done | bytes 589840 | tf_op jit(solution)/shard_map/reduce_scatter | solution.py:224
  822.5 76.8 %all-gather.8.cloned.1.call-done = bf16[3072,1536]{1,0:T(8,128)(2,1)} async-done(((bf16[96,1536]{1,0:T(8,128)(2,1)}), bf16[3072,1536]{1,0:T(8,128)(2,1)}) %all-gather.8.cloned.1.call-update) | async-done | bytes 9437200 | tf_op jit(solution)/shard_map/all_gather | solution.py:165
  899.3 8.4 multiply_reduce_fusion.7
  910.0 7.6 copy.491
  917.6 17.8 reduce.91
  947.2 17.2 all-to-all-done.3
  964.4 4.7 reshape.1698
  981.4 355.6 %while.43 = (s32[]{:T(128)}, f32[1,6,64,128]{3,2,1,0:T(8,128)S(1)}, f32[8,1,256,6,64]{2,0,4,3,1:T(8,128)}, f32[8,1,256,6]{3,2,1,0:T(8,128)}, f32[8,1,256,6]{2,0,...) while((s32[]{:T(128)}, f32[1,6,64,128]{3,2,1,0:T(8,128)S(1)}, ...), condition=%wide.region_19.20_spmd.clone, body=%wide.region_7.19_spmd.clone.sunk | while | flops 1670419456 | bytes 15714059 | solution.py:61
  999.2 9.8 dynamic_update_slice.91
  1009.9 7.6 reduce-window.74
  1043.6 9.8 dynamic_update_slice.91
  1054.3 7.6 reduce-window.74
  1088.0 9.8 dynamic_update_slice.91
  1098.7 7.6 reduce-window.74
  1132.4 9.8 dynamic_update_slice.91
  1143.1 7.6 reduce-window.74
  1176.8 9.8 dynamic_update_slice.91
  1187.5 7.6 reduce-window.74
  1221.2 9.8 dynamic_update_slice.91
  1231.9 7.6 reduce-window.74
  1265.6 9.8 dynamic_update_slice.91
  1276.3 7.6 reduce-window.74
  1310.0 9.8 dynamic_update_slice.91
  1320.7 7.6 reduce-window.74
  1341.8 11.5 reduce.92
  1358.1 4.8 transpose.194
  1369.0 12.4 multiply_reduce_fusion.6
  1392.1 15.7 copy.509
  1407.8 31.6 %reduce.93 = bf16[2048,768]{1,0:T(8,128)(2,1)S(1)} reduce(bf16[2048,1,768]{2,1,0:T(2,128)(2,1)} %bitcast.656, bf16[]{:T(256)} %broadcast.1020), dimensions={1}, to_apply=%bitcast.438.reduce_sub_computation | reduce | bytes 6291458
  1443.0 4.7 all-to-all-start.4
  1460.7 27.7 %all-to-all-done.4 = bf16[8,2,98304]{2,1,0:T(2,128)(2,1)} async-done(((bf16[8,2,98304]{2,1,0:T(2,128)(2,1)}), bf16[8,2,98304]{2,1,0:T(2,128)(2,1)}, u32[]{:S(2)}, u32[]{:S(2)}) %all-to-all-start.4) | async-done | bytes 3145760 | tf_op jit(solution)/shard_map/all_to_all | solution.py:185
  1488.4 7.8 reshape.1702
  1502.4 12.5 fusion.132
  1515.0 18.5 fusion.135
  1535.5 7.8 convert_add_fusion
  1545.1 94.3 %all-reduce.32.cloned.1.call-done = (f32[1536]{0:T(1024)}, f32[3072]{0:T(1024)}, f32[5,3072]{1,0:T(8,128)}, f32[5,256]{1,0:T(8,128)}, f32[3,48]{1,0:T(4,128)}) async-done(((f32[1536]{0:T(1024)}, f32[3072]{0:T(1024)}, f32[5,3072]{1,0:T(8,128)}, f32[5,256]{1,0:T(8,128)}, f32[3,48]{1,0:T(4,128)}), (f32[1536]{0:T(1024)}, f32[3072]{0:T(1024)}, f32[5,3072]{1,0:T(8,128)}, f32[5,256]{1,0:T(8,128)}, ...) | async-done | bytes 85584 | tf_op jit(solution)/shard_map/psum | solution.py:211
  1647.4 361.7 %reduce-scatter.6.cloned.1.call-done = f32[48,6448]{1,0:T(8,128)} async-done(((f32[1536,6448]{1,0:T(8,128)}), f32[48,6448]{1,0:T(8,128)}) %reduce-scatter.6.cloned.1.call-update) | async-done | bytes 1238032 | tf_op jit(solution)/shard_map/reduce_scatter | solution.py:215
  (923 shorter events, 474.9 us)
Async XLA Ops:
  7.2 136.4 %copy-start.11 = (bf16[1,256,1536]{2,1,0:T(8,128)(2,1)S(1)}, bf16[1,256,1536]{2,1,0:T(8,128)(2,1)}, u32[]{:S(2)}) copy-start(bf16[1,256,1536]{2,1,0:T(8,128)(2,1)} %param.27) | copy-start | bytes 2359300
  7.2 136.4 %copy-start.26 = (f32[1536]{0:T(1024)S(1)}, f32[1536]{0:T(1024)}, u32[]{:S(2)}) copy-start(f32[1536]{0:T(1024)} %param.31) | copy-start | bytes 18436
  7.2 136.4 %all-gather.4.cloned.1.call-start = ((), (), s32[]{:S(2)}) async-start(), calls=%async_computation.9 | async-start | bytes 20680704 | tf_op jit(solution)/shard_map/all_gather | solution.py:132
  9.6 238.6 %all-gather.6.cloned.1.call-start = ((), (), s32[]{:S(2)}) async-start(), calls=%async_computation.10 | async-start | bytes 1179648 | tf_op jit(solution)/shard_map/all_gather | solution.py:142
  11.6 146.1 %copy-start.48 = (f32[256]{0:T(256)}, f32[256]{0:T(256)S(1)}, u32[]{:S(2)}) copy-start(f32[256]{0:T(256)S(1)} %get-tuple-element.934) | copy-start | bytes 3076
  162.0 78.0 %all-to-all-start = ((bf16[8,2,768]{2,1,0:T(2,128)(2,1)}), bf16[8,2,768]{2,1,0:T(2,128)(2,1)S(1)}, u32[]{:S(2)}, u32[]{:S(2)}) async-start(bf16[8,2,768]{2,1,0:T(2,128)(2,1)} %reshape.1691), calls=%async_computation | async-start | bytes 49152 | tf_op jit(solution)/shard_map/all_to_all | solution.py:140
  240.0 42.4 %all-to-all-start.1 = ((bf16[8,2,98304]{2,1,0:T(2,128)(2,1)}), bf16[8,2,98304]{2,1,0:T(2,128)(2,1)S(1)}, u32[]{:S(2)}, u32[]{:S(2)}) async-start(bf16[8,2,98304]{2,1,0:T(2,128)(2,1)} %reshape.1693), calls=%async_computation.1 | async-start | bytes 6291456 | tf_op jit(solution)/shard_map/all_to_all | solution.py:139
  244.9 262.4 %copy-start.46 = (f32[384]{0:T(512)}, f32[384]{0:T(512)S(1)}, u32[]{:S(2)}) copy-start(f32[384]{0:T(512)S(1)} %mul.1143) | copy-start | bytes 4612
  245.9 61.3 %copy-start.38 = (f32[384]{0:T(512)}, f32[384]{0:T(512)S(1)}, u32[]{:S(2)}) copy-start(f32[384]{0:T(512)S(1)} %get-tuple-element.804) | copy-start | bytes 4612
  245.9 61.3 %copy-start.40 = (f32[384]{0:T(512)}, f32[384]{0:T(512)S(1)}, u32[]{:S(2)}) copy-start(f32[384]{0:T(512)S(1)} %get-tuple-element.805) | copy-start | bytes 4612
  245.9 61.3 %copy-start.42 = (f32[384]{0:T(512)}, f32[384]{0:T(512)S(1)}, u32[]{:S(2)}) copy-start(f32[384]{0:T(512)S(1)} %get-tuple-element.806) | copy-start | bytes 4612
  245.9 61.3 %copy-start.44 = (f32[384]{0:T(512)}, f32[384]{0:T(512)S(1)}, u32[]{:S(2)}) copy-start(f32[384]{0:T(512)S(1)} %get-tuple-element.807) | copy-start | bytes 4612
  307.2 636.9 %copy-start = (f32[1,2048,6,1,64]{1,4,3,2,0:T(8,128)}, f32[1,2048,6,1,64]{1,4,3,2,0:T(8,128)S(1)}, u32[]{:S(2)}) copy-start(f32[1,2048,6,1,64]{1,4,3,2,0:T(8,128)S(1)} %get-tuple-element.912) | copy-start | bytes 9437188
  559.7 25.3 %all-to-all-start.2 = ((bf16[8,2,49152]{2,1,0:T(2,128)(2,1)}), bf16[8,2,49152]{2,1,0:T(2,128)(2,1)}, u32[]{:S(2)}, u32[]{:S(2)}) async-start(bf16[8,2,49152]{2,1,0:T(2,128)(2,1)} %reshape.1695), calls=%async_computation.2 | async-start | bytes 3145728 | tf_op jit(solution)/shard_map/all_to_all | solution.py:156
  564.1 251.1 %reduce-scatter.8.cloned.1.call-start = ((), (), s32[]{:S(2)}) async-start(), calls=%async_computation.14 | async-start | bytes 19464192 | tf_op jit(solution)/shard_map/reduce_scatter | solution.py:224
  595.9 311.8 %copy-start.60 = (f32[256]{0:T(256)}, f32[256]{0:T(256)S(1)}, u32[]{:S(2)}) copy-start(f32[256]{0:T(256)S(1)} %get-tuple-element.936) | copy-start | bytes 3076
  610.9 288.4 %all-gather.8.cloned.1.call-start = ((), (), s32[]{:S(2)}) async-start(), calls=%async_computation.11 | async-start | bytes 9732096 | tf_op jit(solution)/shard_map/all_gather | solution.py:165
  939.1 25.3 %all-to-all-start.3 = ((bf16[8,2,49152]{2,1,0:T(2,128)(2,1)}), bf16[8,2,49152]{2,1,0:T(2,128)(2,1)}, u32[]{:S(2)}, u32[]{:S(2)}) async-start(bf16[8,2,49152]{2,1,0:T(2,128)(2,1)} %reshape.1697), calls=%async_computation.3 | async-start | bytes 3145728 | tf_op jit(solution)/shard_map/all_to_all | solution.py:180
  996.4 12.7 copy-start.24
  998.7 27.5 %copy-start.14 = (f32[1,6,64,128]{3,2,1,0:T(8,128)S(1)}, f32[1,6,64,128]{3,2,1,0:T(8,128)}, u32[]{:S(2)}) copy-start(f32[1,6,64,128]{3,2,1,0:T(8,128)} %fusion.229) | copy-start | bytes 589828 | tf_op jit(solution)/shard_map/transpose(jvp())/while
  1040.8 12.7 copy-start.24
  1043.1 27.5 %copy-start.14 = (f32[1,6,64,128]{3,2,1,0:T(8,128)S(1)}, f32[1,6,64,128]{3,2,1,0:T(8,128)}, u32[]{:S(2)}) copy-start(f32[1,6,64,128]{3,2,1,0:T(8,128)} %fusion.229) | copy-start | bytes 589828 | tf_op jit(solution)/shard_map/transpose(jvp())/while
  1085.2 12.7 copy-start.24
  1087.5 27.5 %copy-start.14 = (f32[1,6,64,128]{3,2,1,0:T(8,128)S(1)}, f32[1,6,64,128]{3,2,1,0:T(8,128)}, u32[]{:S(2)}) copy-start(f32[1,6,64,128]{3,2,1,0:T(8,128)} %fusion.229) | copy-start | bytes 589828 | tf_op jit(solution)/shard_map/transpose(jvp())/while
  1129.6 12.7 copy-start.24
  1131.9 27.5 %copy-start.14 = (f32[1,6,64,128]{3,2,1,0:T(8,128)S(1)}, f32[1,6,64,128]{3,2,1,0:T(8,128)}, u32[]{:S(2)}) copy-start(f32[1,6,64,128]{3,2,1,0:T(8,128)} %fusion.229) | copy-start | bytes 589828 | tf_op jit(solution)/shard_map/transpose(jvp())/while
  1174.0 12.7 copy-start.24
  1176.3 27.5 %copy-start.14 = (f32[1,6,64,128]{3,2,1,0:T(8,128)S(1)}, f32[1,6,64,128]{3,2,1,0:T(8,128)}, u32[]{:S(2)}) copy-start(f32[1,6,64,128]{3,2,1,0:T(8,128)} %fusion.229) | copy-start | bytes 589828 | tf_op jit(solution)/shard_map/transpose(jvp())/while
  1218.4 12.7 copy-start.24
  1220.8 27.5 %copy-start.14 = (f32[1,6,64,128]{3,2,1,0:T(8,128)S(1)}, f32[1,6,64,128]{3,2,1,0:T(8,128)}, u32[]{:S(2)}) copy-start(f32[1,6,64,128]{3,2,1,0:T(8,128)} %fusion.229) | copy-start | bytes 589828 | tf_op jit(solution)/shard_map/transpose(jvp())/while
  1262.8 12.7 copy-start.24
  1265.2 27.5 %copy-start.14 = (f32[1,6,64,128]{3,2,1,0:T(8,128)S(1)}, f32[1,6,64,128]{3,2,1,0:T(8,128)}, u32[]{:S(2)}) copy-start(f32[1,6,64,128]{3,2,1,0:T(8,128)} %fusion.229) | copy-start | bytes 589828 | tf_op jit(solution)/shard_map/transpose(jvp())/while
  1307.2 12.7 copy-start.24
  1309.6 27.5 %copy-start.14 = (f32[1,6,64,128]{3,2,1,0:T(8,128)S(1)}, f32[1,6,64,128]{3,2,1,0:T(8,128)}, u32[]{:S(2)}) copy-start(f32[1,6,64,128]{3,2,1,0:T(8,128)} %fusion.229) | copy-start | bytes 589828 | tf_op jit(solution)/shard_map/transpose(jvp())/while
  1354.7 88.3 %all-to-all-start.5 = ((bf16[8,2,768]{2,1,0:T(2,128)(2,1)}), bf16[8,2,768]{2,1,0:T(2,128)(2,1)S(1)}, u32[]{:S(2)}, u32[]{:S(2)}) async-start(bf16[8,2,768]{2,1,0:T(2,128)(2,1)} %reshape.1699), calls=%async_computation.6 | async-start | bytes 49152 | tf_op jit(solution)/shard_map/all_to_all | solution.py:186
  1369.0 12.4 copy-start.41
  1443.0 45.4 %all-to-all-start.4 = ((bf16[8,2,98304]{2,1,0:T(2,128)(2,1)}), bf16[8,2,98304]{2,1,0:T(2,128)(2,1)}, u32[]{:S(2)}, u32[]{:S(2)}) async-start(bf16[8,2,98304]{2,1,0:T(2,128)(2,1)} %reshape.1701), calls=%async_computation.4 | async-start | bytes 6291456 | tf_op jit(solution)/shard_map/all_to_all | solution.py:185
  1447.7 54.6 %reduce-scatter.4.cloned.1.call-start = ((), (), s32[]{:S(2)}) async-start(), calls=%async_computation.12 | async-start | bytes 1179648 | tf_op jit(solution)/shard_map/reduce_scatter | solution.py:188
  1455.5 184.0 %all-reduce.32.cloned.1.call-start = ((), (), s32[]{:S(2)}) async-start(), calls=%async_computation.15 | async-start | bytes 258048 | tf_op jit(solution)/shard_map/psum | solution.py:211
  1458.2 38.1 %copy-start.66 = (f32[3,48]{1,0:T(4,128)}, f32[3,48]{1,0:T(4,128)S(1)}, u32[]{:S(2)}) copy-start(f32[3,48]{1,0:T(4,128)S(1)} %dynamic_update_slice.68) | copy-start | bytes 1732
  1458.8 37.4 %copy-start.20 = (f32[5,3072]{1,0:T(8,128)}, f32[5,3072]{1,0:T(8,128)S(1)}, u32[]{:S(2)}) copy-start(f32[5,3072]{1,0:T(8,128)S(1)} %add_dynamic-update-slice_fusion) | copy-start | bytes 184324
  1502.4 12.6 copy-start.9
  1502.4 12.6 copy-start.25
  1514.9 494.2 %reduce-scatter.6.cloned.1.call-start = ((), (), s32[]{:S(2)}) async-start(), calls=%async_computation.13 | async-start | bytes 41361408 | tf_op jit(solution)/shard_map/reduce_scatter | solution.py:215
  1543.3 96.2 %copy-start.72 = (f32[3,48]{1,0:T(4,128)S(1)}, f32[3,48]{1,0:T(4,128)}, u32[]{:S(2)}) copy-start(f32[3,48]{1,0:T(4,128)} %param.35) | copy-start | bytes 1732
  1543.3 96.2 %copy-start.77 = (f32[3,48]{1,0:T(4,128)S(1)}, f32[3,48]{1,0:T(4,128)}, u32[]{:S(2)}) copy-start(f32[3,48]{1,0:T(4,128)} %param.42) | copy-start | bytes 1732
  1543.3 96.2 %copy-start.78 = (f32[3,48]{1,0:T(4,128)S(1)}, f32[3,48]{1,0:T(4,128)}, u32[]{:S(2)}) copy-start(f32[3,48]{1,0:T(4,128)} %param.49) | copy-start | bytes 1732
  1543.3 98.4 %copy-start.67 = (f32[1536]{0:T(1024)S(1)}, f32[1536]{0:T(1024)}, u32[]{:S(2)}) copy-start(f32[1536]{0:T(1024)} %param.38) | copy-start | bytes 18436
  1543.3 98.4 %copy-start.68 = (f32[1536]{0:T(1024)S(1)}, f32[1536]{0:T(1024)}, u32[]{:S(2)}) copy-start(f32[1536]{0:T(1024)} %param.45) | copy-start | bytes 18436
  1543.3 99.8 %copy-start.37 = (f32[5,256]{1,0:T(8,128)S(1)}, f32[5,256]{1,0:T(8,128)}, u32[]{:S(2)}) copy-start(f32[5,256]{1,0:T(8,128)} %param.34) | copy-start | bytes 15364
  1543.3 99.7 %copy-start.69 = (f32[5,256]{1,0:T(8,128)S(1)}, f32[5,256]{1,0:T(8,128)}, u32[]{:S(2)}) copy-start(f32[5,256]{1,0:T(8,128)} %param.41) | copy-start | bytes 15364
  1543.3 99.7 %copy-start.70 = (f32[5,256]{1,0:T(8,128)S(1)}, f32[5,256]{1,0:T(8,128)}, u32[]{:S(2)}) copy-start(f32[5,256]{1,0:T(8,128)} %param.48) | copy-start | bytes 15364
  1543.3 101.0 %copy-start.50 = (f32[3072]{0:T(1024)S(1)}, f32[3072]{0:T(1024)}, u32[]{:S(2)}) copy-start(f32[3072]{0:T(1024)} %param.39) | copy-start | bytes 36868
  1543.4 101.0 %copy-start.51 = (f32[3072]{0:T(1024)S(1)}, f32[3072]{0:T(1024)}, u32[]{:S(2)}) copy-start(f32[3072]{0:T(1024)} %param.46) | copy-start | bytes 36868
  1543.4 102.4 %copy-start.28 = (f32[5,3072]{1,0:T(8,128)S(1)}, f32[5,3072]{1,0:T(8,128)}, u32[]{:S(2)}) copy-start(f32[5,3072]{1,0:T(8,128)} %param.33) | copy-start | bytes 184324
  1543.4 102.4 %copy-start.31 = (f32[5,3072]{1,0:T(8,128)S(1)}, f32[5,3072]{1,0:T(8,128)}, u32[]{:S(2)}) copy-start(f32[5,3072]{1,0:T(8,128)} %param.40) | copy-start | bytes 184324
  1543.4 102.3 %copy-start.32 = (f32[5,3072]{1,0:T(8,128)S(1)}, f32[5,3072]{1,0:T(8,128)}, u32[]{:S(2)}) copy-start(f32[5,3072]{1,0:T(8,128)} %param.47) | copy-start | bytes 184324
  1543.4 465.7 %copy-start.13 = (f32[48,6448]{1,0:T(8,128)S(1)}, f32[48,6448]{1,0:T(8,128)}, u32[]{:S(2)}) copy-start(f32[48,6448]{1,0:T(8,128)} %param.29) | copy-start | bytes 3714052
  1543.4 465.7 %copy-start.18 = (f32[48,6448]{1,0:T(8,128)S(1)}, f32[48,6448]{1,0:T(8,128)}, u32[]{:S(2)}) copy-start(f32[48,6448]{1,0:T(8,128)} %param.36) | copy-start | bytes 3714052
  1647.4 365.9 %copy-start.35 = (f32[1536]{0:T(1024)S(1)}, f32[1536]{0:T(1024)}, u32[]{:S(2)}) copy-start(f32[1536]{0:T(1024)} %get-tuple-element.1242) | copy-start | bytes 18436
  1647.4 366.5 %copy-start.33 = (f32[3072]{0:T(1024)S(1)}, f32[3072]{0:T(1024)}, u32[]{:S(2)}) copy-start(f32[3072]{0:T(1024)} %get-tuple-element.1243) | copy-start | bytes 36868
  1647.4 367.1 %copy-start.21 = (f32[5,3072]{1,0:T(8,128)S(1)}, f32[5,3072]{1,0:T(8,128)}, u32[]{:S(2)}) copy-start(f32[5,3072]{1,0:T(8,128)} %get-tuple-element.1244) | copy-start | bytes 184324
  1647.4 367.8 %copy-start.34 = (f32[5,256]{1,0:T(8,128)S(1)}, f32[5,256]{1,0:T(8,128)}, u32[]{:S(2)}) copy-start(f32[5,256]{1,0:T(8,128)} %get-tuple-element.1245) | copy-start | bytes 15364
  1647.4 368.4 %copy-start.73 = (f32[3,48]{1,0:T(4,128)S(1)}, f32[3,48]{1,0:T(4,128)}, u32[]{:S(2)}) copy-start(f32[3,48]{1,0:T(4,128)} %get-tuple-element.1246) | copy-start | bytes 1732
  (56 other events, 249.7 us)
Sparse Core Ops, SparseCore 0:
  11.4 132.1 all-gather.3
  159.4 21.6 all-gather.5
  611.0 204.1 reduce-scatter.7
  818.7 80.5 all-gather.7
  1455.6 38.7 reduce-scatter.3
  1515.0 124.3 all-reduce.31
  1646.4 362.6 reduce-scatter.5
where the time goes:
time: 2040 us; the launch traced here: 2020 us
  waiting for transfers between devices  958 us (47%)
  local copies, waits for them, and re-layouts  484 us (24%)
  other arithmetic  326 us (16%)
  matrix products  211 us (10%)
  starting transfers between devices  25.1 us (1%)
    reduce_scatter x1, waiting for transfers between devices, local(): lax.psum_scatter(jnp.einsum('nkm,nkc->mc', column_list, projected_gradien...  362 us
    dynamic_update_slice x56, local copies, waits for them, and re-layouts, state_space(): lax.scan(jax.checkpoint(block_step), start, (blockify(inner), blockify(st...  215 us
    reduce_scatter x1, waiting for transfers between devices, local(): lax.psum_scatter(jnp.einsum('kcb,kch->bh', column_list, cotangent, prefer...  204 us
    all_gather x1, waiting for transfers between devices, local(): lax.all_gather(in_w16, ('seq', 'wshard'), axis=0, tiled=True)  132 us
    unnamed x10, other arithmetic  132 us
    psum x1, waiting for transfers between devices, local(): lax.psum((d_in_gain, d_out_gain, d_conv_full, d_common, d_head_full), ('s...  94.3 us
    another operation x49, other arithmetic  93.2 us
    all_gather x1, waiting for transfers between devices, local(): lax.all_gather(out_w16, ('seq', 'wshard'), axis=0, tiled=True)  76.8 us
  transfers between devices with their start and end apart: 13, of which 9 were waited for; matrix products, arithmetic and copies ran while one was open for 12% of the time, Pallas kernels for 0%

commit v1 on v0

v1 whole, which is shorter than its diff:
```python
import functools

import jax
import jax.numpy as jnp
from jax import lax
from jax.experimental import pallas as pl
from jax.experimental.pallas import tpu as pltpu
from jax.sharding import PartitionSpec as P

P_SIZE = 64
N_STATE = 128
LANES = 128
CHUNK = 128

norm_eps = 1e-05
beta_one = 0.9
beta_two = 0.95
adam_eps = 1e-08
adam_step = 3.0
weight_learning_rate = 0.01
matrix_decay = 0.1
small_rate = 0.1

f32 = jnp.float32
bf16 = jnp.bfloat16
NN = (((1,), (0,)), ((), ()))
NT = (((1,), (1,)), ((), ()))
TN = (((0,), (0,)), ((), ()))


def mm(a, b, dims):
    return lax.dot_general(a, b, dims, preferred_element_type=f32)


def mm_high(a, b):
    return lax.dot_general(
        a, b, NN, precision=lax.Precision.HIGHEST, preferred_element_type=f32
    )


def two_parts(a):
    hi = a.astype(bf16)
    return hi, (a - hi.astype(f32)).astype(bf16)


def mm3(a, b, dims):
    return mm(a[0], b[0], dims) + (mm(a[0], b[1], dims) + mm(a[1], b[0], dims))


def low_half(rows):
    return lax.broadcasted_iota(jnp.int32, (rows, LANES), 1) < P_SIZE


def split_pairs(values, heads):
    low = low_half(values.shape[0])
    gates, inners = [], []
    for h in range(0, heads, 2):
        a = values[:, h * LANES : (h + 1) * LANES]
        a_r = pltpu.roll(a, P_SIZE, 1)
        if h + 1 < heads:
            b = values[:, (h + 1) * LANES : (h + 2) * LANES]
            b_r = pltpu.roll(b, P_SIZE, 1)
            gates.append(jnp.where(low, a, b_r))
            inners.append(jnp.where(low, a_r, b))
        else:
            gates.append(a[:, :P_SIZE])
            inners.append(a_r[:, :P_SIZE])
    return jnp.concatenate(gates, axis=1), jnp.concatenate(inners, axis=1)


def join_pairs(gate, inner, heads):
    low = low_half(gate.shape[0])
    out = []
    for h in range(0, heads, 2):
        if h + 1 < heads:
            g = gate[:, h * P_SIZE : (h + 2) * P_SIZE]
            x = inner[:, h * P_SIZE : (h + 2) * P_SIZE]
            out.append(jnp.where(low, g, pltpu.roll(x, P_SIZE, 1)))
            out.append(jnp.where(low, pltpu.roll(g, P_SIZE, 1), x))
        else:
            out.append(
                jnp.concatenate(
                    [gate[:, h * P_SIZE :], inner[:, h * P_SIZE :]], axis=1
                )
            )
    return jnp.concatenate(out, axis=1)


def expand(cols, heads):
    rows = cols.shape[0]
    low = low_half(rows)
    out = []
    for h in range(0, heads, 2):
        if h + 1 < heads:
            one = jnp.broadcast_to(cols[:, h : h + 1], (rows, LANES))
            two = jnp.broadcast_to(cols[:, h + 1 : h + 2], (rows, LANES))
            out.append(jnp.where(low, one, two))
        else:
            out.append(jnp.broadcast_to(cols[:, h : h + 1], (rows, P_SIZE)))
    return jnp.concatenate(out, axis=1)


def pair_of(values, h, heads):
    first = h - h % 2
    return values[:, first * P_SIZE : min(first + 2, heads) * P_SIZE]


def merge_pairs(parts, heads):
    low = low_half(parts[0].shape[0])
    out = []
    for h in range(0, heads, 2):
        if h + 1 < heads:
            out.append(jnp.where(low, parts[h], parts[h + 1]))
        else:
            out.append(parts[h])
    return jnp.concatenate(out, axis=1)


def chunk_common(heads, main, small, cat, head_ref, taps_ref):
    rows = main.shape[0]
    gate, inner = split_pairs(main, heads)
    raw = jnp.concatenate([small[:, : 2 * N_STATE], inner], axis=1)
    cat[8 : 8 + rows] = raw
    conv = taps_ref[4:5] + taps_ref[0:1] * cat[5 : 5 + rows]
    for k in range(1, 4):
        conv = conv + taps_ref[k : k + 1] * cat[5 + k : 5 + k + rows]
    step_in = small[:, 2 * N_STATE :] + head_ref[0:1]
    dt = jnp.maximum(step_in, 0.0) + jnp.log1p(jnp.exp(-jnp.abs(step_in)))
    neg_rate = -jnp.exp(head_ref[1:2])
    decay_log = neg_rate * dt
    r = lax.broadcasted_iota(jnp.int32, (rows, rows), 0)
    c = lax.broadcasted_iota(jnp.int32, (rows, rows), 1)
    tri = jnp.where(r >= c, 1.0, 0.0).astype(f32)
    cumul = mm_high(tri, decay_log)
    return gate, conv, step_in, dt, neg_rate, decay_log, cumul, r, c


def fwd_kernel(
    heads, main_ref, small_ref, head_ref, taps_ref, gated_ref, y_ref, states_ref, state, cat
):
    rows = main_ref.shape[0]

    @pl.when(pl.program_id(0) == 0)
    def _():
        state[...] = jnp.zeros_like(state)
        cat[0:8] = jnp.zeros((8, cat.shape[1]), f32)

    gate, conv, _, dt, _, _, cumul, r, c = chunk_common(
        heads,
        main_ref[...].astype(f32),
        small_ref[...].astype(f32),
        cat,
        head_ref,
        taps_ref,
    )
    cat[0:8] = cat[rows : rows + 8]
    act = conv * jax.nn.sigmoid(conv)
    b2 = two_parts(act[:, :N_STATE])
    c2 = two_parts(act[:, N_STATE : 2 * N_STATE])
    inner = act[:, 2 * N_STATE :]
    scaled = inner * expand(dt, heads)
    scaled2 = two_parts(scaled)
    scores = mm3(c2, b2, NT)
    lower = r >= c
    cumul_t = cumul.T
    parts = []
    for h in range(heads):
        spread = cumul[:, h : h + 1] - cumul_t[h : h + 1, :]
        weights = two_parts(scores * jnp.exp(jnp.where(lower, spread, -1e30)))
        own = tuple(pair_of(part, h, heads) for part in scaled2)
        parts.append(mm3(weights, own, NN))
    s2 = two_parts(state[...])
    states_ref[0] = state[...]
    last = cumul[rows - 1 : rows]
    y = merge_pairs(parts, heads) + expand(jnp.exp(cumul), heads) * mm3(c2, s2, NN)
    y_ref[...] = y
    tail = expand(jnp.exp(last - cumul), heads)
    fresh = mm3(b2, two_parts(tail * scaled), TN)
    state[...] = expand(jnp.exp(last), heads) * state[...] + fresh
    full = y + expand(head_ref[2:3], heads) * inner
    gated_ref[...] = (full * (gate * jax.nn.sigmoid(gate))).astype(bf16)


def mixer_forward(main, small, head, taps, heads):
    length = main.shape[0]
    width = heads * P_SIZE
    count = length // CHUNK
    all_w = width + 2 * N_STATE
    return pl.pallas_call(
        functools.partial(fwd_kernel, heads),
        grid=(count,),
        in_specs=[
            pl.BlockSpec((CHUNK, 2 * width), lambda i: (i, 0)),
            pl.BlockSpec((CHUNK, 3 * LANES), lambda i: (i, 0)),
            pl.BlockSpec((8, LANES), lambda i: (0, 0)),
            pl.BlockSpec((8, all_w), lambda i: (0, 0)),
        ],
        out_specs=[
            pl.BlockSpec((CHUNK, width), lambda i: (i, 0)),
            pl.BlockSpec((CHUNK, width), lambda i: (i, 0)),
            pl.BlockSpec((1, N_STATE, width), lambda i: (i, 0, 0)),
        ],
        out_shape=[
            jax.ShapeDtypeStruct((length, width), bf16),
            jax.ShapeDtypeStruct((length, width), f32),
            jax.ShapeDtypeStruct((count, N_STATE, width), f32),
        ],
        scratch_shapes=[
            pltpu.VMEM((N_STATE, width), f32),
            pltpu.VMEM((CHUNK + 8, all_w), f32),
        ],
        name="mixer_forward",
    )(main, small, head, taps)


def bwd_kernel(
    heads,
    count,
    main_ref,
    small_ref,
    main_prev,
    small_prev,
    head_ref,
    taps_ref,
    y_ref,
    states_ref,
    dgated_ref,
    dmain_ref,
    dshared_ref,
    dstep_ref,
    dtaps_ref,
    dhead_ref,
    dstate,
    cat,
    dcat,
):
    rows, width = y_ref.shape
    step = pl.program_id(0)

    @pl.when(step == 0)
    def _():
        dstate[...] = jnp.zeros_like(dstate)
        dcat[rows : rows + 8] = jnp.zeros((8, dcat.shape[1]), f32)
        dtaps_ref[...] = jnp.zeros_like(dtaps_ref)
        dhead_ref[...] = jnp.zeros_like(dhead_ref)

    _, inner_prev = split_pairs(main_prev[8:16].astype(f32), heads)
    prev = jnp.concatenate(
        [small_prev[8:16].astype(f32)[:, : 2 * N_STATE], inner_prev], axis=1
    )
    cat[0:8] = jnp.where(step == count - 1, 0.0, prev)
    gate, conv, step_in, dt, neg_rate, decay_log, cumul, r, c = chunk_common(
        heads,
        main_ref[...].astype(f32),
        small_ref[...].astype(f32),
        cat,
        head_ref,
        taps_ref,
    )
    sig = jax.nn.sigmoid(conv)
    act = conv * sig
    dsilu = sig * (1.0 + conv * (1.0 - sig))
    b2 = two_parts(act[:, :N_STATE])
    c2 = two_parts(act[:, N_STATE : 2 * N_STATE])
    inner = act[:, 2 * N_STATE :]
    dt_x = expand(dt, heads)
    scaled = inner * dt_x
    scaled2 = two_parts(scaled)
    skip = expand(head_ref[2:3], heads)
    y = y_ref[...]
    sgate = jax.nn.sigmoid(gate)
    dgated = dgated_ref[...].astype(f32)
    dgate = dgated * (y + skip * inner) * (sgate * (1.0 + gate * (1.0 - sgate)))
    dy = dgated * (gate * sgate)
    dy2 = two_parts(dy)

    scores_t = mm3(b2, c2, NT)
    upper = c >= r
    cumul_t = cumul.T
    low = low_half(rows)
    parts = []
    dscores_t = None
    for h in range(heads):
        spread = cumul_t[h : h + 1, :] - cumul[:, h : h + 1]
        decay = jnp.exp(jnp.where(upper, spread, -1e30))
        weights = two_parts(scores_t * decay)
        dy_pair = tuple(pair_of(part, h, heads) for part in dy2)
        parts.append(mm3(weights, dy_pair, NN))
        own = pair_of(scaled, h, heads)
        if own.shape[1] == LANES:
            own = jnp.where(low == (h % 2 == 0), own, 0.0)
        term = mm3(two_parts(own), dy_pair, NT) * decay
        dscores_t = term if dscores_t is None else dscores_t + term
    s_in = states_ref[0]
    s2 = two_parts(s_in)
    ds = dstate[...]
    ds2 = two_parts(ds)
    last = cumul[rows - 1 : rows]
    tail = expand(jnp.exp(last - cumul), heads)
    ecum = expand(jnp.exp(cumul), heads)
    elast = expand(jnp.exp(last), heads)
    tail_b = tail * mm3(b2, ds2, NN)
    z = merge_pairs(parts, heads) + tail_b
    extra = jnp.sum(tail_b * scaled, axis=0, keepdims=True) + elast * jnp.sum(
        ds * s_in, axis=0, keepdims=True
    )
    at_end = lax.broadcasted_iota(jnp.int32, (rows, width), 0) == rows - 1
    u = dy * y - scaled * z + jnp.where(at_end, extra, 0.0)
    pick = (
        lax.broadcasted_iota(jnp.int32, (width, LANES), 0) // P_SIZE
        == lax.broadcasted_iota(jnp.int32, (width, LANES), 1)
    ).astype(f32)
    dcumul = mm_high(u, pick)
    suffix = jnp.where(c >= r, 1.0, 0.0).astype(f32)
    ddecay = mm_high(suffix, dcumul)
    dstep = (mm_high(inner * z, pick) + neg_rate * ddecay) * jax.nn.sigmoid(step_in)
    dstep_ref[...] = dstep.astype(bf16)
    dhead_ref[0:1] += jnp.sum(dstep, axis=0, keepdims=True)
    dhead_ref[1:2] += jnp.sum(decay_log * ddecay, axis=0, keepdims=True)

    dinner = dt_x * z + skip * dy
    dscores2 = two_parts(dscores_t)
    edy2 = two_parts(ecum * dy)
    db = mm3(dscores2, c2, NN) + mm3(two_parts(tail * scaled), ds2, NT)
    dc = mm3(dscores2, b2, TN) + mm3(edy2, s2, NT)
    dstate[...] = elast * ds + mm3(c2, edy2, TN)

    dconv = jnp.concatenate([db, dc, dinner], axis=1) * dsilu
    dcat[0:rows] = dconv
    draw = taps_ref[3:4] * dconv
    for k in range(3):
        draw = draw + taps_ref[k : k + 1] * dcat[3 - k : 3 - k + rows]
    for k in range(4):
        dtaps_ref[k : k + 1] += jnp.sum(
            dconv * cat[5 + k : 5 + k + rows], axis=0, keepdims=True
        )
    dtaps_ref[4:5] += jnp.sum(dconv, axis=0, keepdims=True)
    dtaps_ref[5:6, 2 * N_STATE :] += jnp.sum(dy * inner, axis=0, keepdims=True)
    dcat[rows : rows + 8] = dconv[0:8]
    dshared_ref[...] = draw[:, : 2 * N_STATE].T.astype(bf16)
    dmain_ref[...] = join_pairs(dgate, draw[:, 2 * N_STATE :], heads).astype(bf16)


def mixer_backward(main, small, head, taps, y, states, dgated, heads):
    length, width = y.shape
    count = length // CHUNK
    all_w = width + 2 * N_STATE
    per = CHUNK // 16

    def at(i):
        return (count - 1 - i, 0)

    def before(i):
        return (jnp.maximum((count - 1 - i) * per - 1, 0), 0)

    def fixed(i):
        return (0, 0)

    return pl.pallas_call(
        functools.partial(bwd_kernel, heads, count),
        grid=(count,),
        in_specs=[
            pl.BlockSpec((CHUNK, 2 * width), at),
            pl.BlockSpec((CHUNK, 3 * LANES), at),
            pl.BlockSpec((16, 2 * width), before),
            pl.BlockSpec((16, 3 * LANES), before),
            pl.BlockSpec((8, LANES), fixed),
            pl.BlockSpec((8, all_w), fixed),
            pl.BlockSpec((CHUNK, width), at),
            pl.BlockSpec((1, N_STATE, width), lambda i: (count - 1 - i, 0, 0)),
            pl.BlockSpec((CHUNK, width), at),
        ],
        out_specs=[
            pl.BlockSpec((CHUNK, 2 * width), at),
            pl.BlockSpec((2 * N_STATE, CHUNK), lambda i: (0, count - 1 - i)),
            pl.BlockSpec((CHUNK, LANES), at),
            pl.BlockSpec((8, all_w), fixed),
            pl.BlockSpec((8, LANES), fixed),
        ],
        out_shape=[
            jax.ShapeDtypeStruct((length, 2 * width), bf16),
            jax.ShapeDtypeStruct((2 * N_STATE, length), bf16),
            jax.ShapeDtypeStruct((length, LANES), bf16),
            jax.ShapeDtypeStruct((8, all_w), f32),
            jax.ShapeDtypeStruct((8, LANES), f32),
        ],
        scratch_shapes=[
            pltpu.VMEM((N_STATE, width), f32),
            pltpu.VMEM((CHUNK + 8, all_w), f32),
            pltpu.VMEM((CHUNK + 8, all_w), f32),
        ],
        name="mixer_backward",
    )(main, small, main, small, head, taps, y, states, dgated)


MESH = pl.DeviceIdType.MESH


def greet(peers, count):
    barrier = pltpu.get_barrier_semaphore()
    for peer in peers:
        pl.semaphore_signal(barrier, inc=1, device_id=peer, device_id_type=MESH)
    pl.semaphore_wait(barrier, count)


def wire(src, dst, send, recv, peer):
    return pltpu.make_async_remote_copy(
        src_ref=src,
        dst_ref=dst,
        send_sem=send,
        recv_sem=recv,
        device_id=peer,
        device_id_type=MESH,
    )


def weights_kernel(n_seq, n_wsh, main, small, outw, w_main, w_small, w_out, *sems):
    send_a, recv_a, send_b, recv_b, send_c, recv_c, send_d, recv_d, send_e, recv_e, own = sems
    s = lax.axis_index("seq")
    w = lax.axis_index("wshard")
    row = [(lax.rem(s + k, n_seq), w) for k in range(1, n_seq)]
    col = [(s, lax.rem(w + j, n_wsh)) for j in range(1, n_wsh)]
    greet(row + col, n_seq + n_wsh - 2)
    first = [
        wire(main.at[peer[0]], w_main.at[s, w], send_a.at[k], recv_a.at[k], peer)
        for k, peer in enumerate(row)
    ]
    spread = [
        wire(small, w_small.at[s, w], send_b.at[j], recv_b.at[j], peer)
        for j, peer in enumerate(col)
    ]
    outs = [
        wire(outw, w_out.at[w], send_c.at[j], recv_c.at[j], peer)
        for j, peer in enumerate(col)
    ]
    mine = [
        pltpu.make_async_copy(main.at[s], w_main.at[s, w], own.at[0]),
        pltpu.make_async_copy(small, w_small.at[s, w], own.at[1]),
        pltpu.make_async_copy(outw, w_out.at[w], own.at[2]),
    ]
    for copy in mine[:2] + first + spread:
        copy.start()
    mine[0].wait()
    for copy in first:
        copy.wait_recv()
    second = [
        wire(w_main.at[:, w], w_main.at[:, w], send_d.at[j], recv_d.at[j], peer)
        for j, peer in enumerate(col)
    ]
    for copy in second:
        copy.start()
    mine[1].wait()
    for copy in spread:
        copy.wait_recv()
    third = [
        wire(w_small.at[s], w_small.at[s], send_e.at[k], recv_e.at[k], peer)
        for k, peer in enumerate(row)
    ]
    for copy in third + [mine[2]] + outs:
        copy.start()
    mine[2].wait()
    for copy in first + spread:
        copy.wait_send()
    for copy in second + third + outs:
        copy.wait()


def spread_weights(main, small, outw, n_seq, n_wsh):
    rows_in, cols = main.shape[1:]
    anywhere = pl.BlockSpec(memory_space=pl.ANY)
    dma = pltpu.SemaphoreType.DMA
    a, c = n_seq - 1, n_wsh - 1
    return pl.pallas_call(
        functools.partial(weights_kernel, n_seq, n_wsh),
        in_specs=[anywhere] * 3,
        out_specs=[anywhere] * 3,
        out_shape=[
            jax.ShapeDtypeStruct((n_seq, n_wsh, rows_in, cols), bf16),
            jax.ShapeDtypeStruct((n_seq, n_wsh) + small.shape, bf16),
            jax.ShapeDtypeStruct((n_wsh,) + outw.shape, bf16),
        ],
        scratch_shapes=[
            dma((n,)) for n in (a, a, c, c, c, c, c, c, a, a, 3)
        ],
        compiler_params=pltpu.CompilerParams(collective_id=0, has_side_effects=True),
        cost_estimate=pl.CostEstimate(
            flops=0, bytes_accessed=200_000_000, transcendentals=0
        ),
        name="spread_weights",
    )(main, small, outw)


def swap_kernel(plan, n_seq, n_wsh, *refs):
    n = len(plan)
    ins, outs, sems = refs[:n], refs[n : 2 * n], refs[2 * n :]
    s = lax.axis_index("seq")
    w = lax.axis_index("wshard")
    total = n_seq * n_wsh
    me_all = s * n_wsh + w
    size = {"seq": n_seq, "wshard": n_wsh, "both": total}
    me_of = {"seq": s, "wshard": w, "both": me_all}

    def peer_at(axis, k):
        if axis == "seq":
            index = lax.rem(s + k, n_seq)
            return index, (index, w)
        if axis == "wshard":
            index = lax.rem(w + k, n_wsh)
            return index, (s, index)
        index = lax.rem(me_all + k, total)
        return index, (lax.div(index, n_wsh), lax.rem(index, n_wsh))

    def block(kind, ref, index):
        if kind == "all":
            return ref
        return ref.at[index] if kind == 0 else ref.at[:, index]

    def copy_of(i, k):
        kind, axis = plan[i]
        index, peer = peer_at(axis, k)
        return wire(
            block(kind, ins[i], index),
            outs[i].at[me_of[axis]],
            sems[3 * i].at[k],
            sems[3 * i + 1].at[k],
            peer,
        )

    widest = "both" if any(axis == "both" for _, axis in plan) else plan[0][1]
    barrier = pltpu.get_barrier_semaphore()

    def hail(k, _):
        pl.semaphore_signal(
            barrier, inc=1, device_id=peer_at(widest, k)[1], device_id_type=MESH
        )
        return 0

    lax.fori_loop(1, size[widest], hail, 0)
    pl.semaphore_wait(barrier, size[widest] - 1)
    own = []
    for i, (kind, axis) in enumerate(plan):
        me = me_of[axis]
        own.append(
            pltpu.make_async_copy(
                block(kind, ins[i], me), outs[i].at[me], sems[3 * i + 2].at[0]
            )
        )

        def begin(k, _, i=i):
            copy_of(i, k).start()
            return 0

        lax.fori_loop(1, size[axis], begin, 0)
    for copy in own:
        copy.start()
    for i, (kind, axis) in enumerate(plan):
        own[i].wait()

        def finish(k, _, i=i):
            copy_of(i, k).wait()
            return 0

        lax.fori_loop(1, size[axis], finish, 0)


def swap(arrays, plan, n_seq, n_wsh, collective_id, name):
    anywhere = pl.BlockSpec(memory_space=pl.ANY)
    size = {"seq": n_seq, "wshard": n_wsh, "both": n_seq * n_wsh}
    shapes, sems = [], []
    for x, (kind, axis) in zip(arrays, plan):
        n = size[axis]
        shape = x.shape
        if kind == 0:
            shape = shape[1:]
        elif kind == 1:
            shape = shape[:1] + shape[2:]
        shapes.append(jax.ShapeDtypeStruct((n,) + shape, x.dtype))
        sems += [
            pltpu.SemaphoreType.DMA((n,)),
            pltpu.SemaphoreType.DMA((n,)),
            pltpu.SemaphoreType.DMA((1,)),
        ]
    return pl.pallas_call(
        functools.partial(swap_kernel, plan, n_seq, n_wsh),
        in_specs=[anywhere] * len(arrays),
        out_specs=[anywhere] * len(arrays),
        out_shape=shapes,
        scratch_shapes=sems,
        compiler_params=pltpu.CompilerParams(
            collective_id=collective_id, has_side_effects=True
        ),
        name=name,
    )(*arrays)


def stats_kernel(n_seq, x_ref, out_ref, slots, send, recv):
    s = lax.axis_index("seq")
    w = lax.axis_index("wshard")
    row = [(lax.rem(s + k, n_seq), w) for k in range(1, n_seq)]
    greet(row, n_seq - 1)
    copies = [
        wire(x_ref, slots.at[s], send.at[k], recv.at[k], peer)
        for k, peer in enumerate(row)
    ]
    for copy in copies:
        copy.start()
    slots[s] = x_ref[...]
    for copy in copies:
        copy.wait()
    total = slots[0]
    for k in range(1, n_seq):
        total = total + slots[k]
    out_ref[...] = total


def sum_over_seq(x, n_seq):
    vmem = pl.BlockSpec(memory_space=pltpu.VMEM)
    dma = pltpu.SemaphoreType.DMA
    return pl.pallas_call(
        functools.partial(stats_kernel, n_seq),
        in_specs=[vmem],
        out_specs=vmem,
        out_shape=jax.ShapeDtypeStruct(x.shape, f32),
        scratch_shapes=[
            pltpu.VMEM((n_seq,) + x.shape, f32),
            dma((n_seq - 1,)),
            dma((n_seq - 1,)),
        ],
        compiler_params=pltpu.CompilerParams(collective_id=1, has_side_effects=True),
        name="sum_over_seq",
    )(x)


def adamw(param, grad, first, second_moment, rate, decay):
    first_new = beta_one * first + (1.0 - beta_one) * grad
    second_new = beta_two * second_moment + (1.0 - beta_two) * grad * grad
    corrected = (
        first_new
        / (1.0 - beta_one**adam_step)
        / (jnp.sqrt(second_new / (1.0 - beta_two**adam_step)) + adam_eps)
    )
    return (param - rate * (corrected + decay * param), first_new, second_new)


def local(
    block_in,
    cotangent,
    in_weight,
    out_weight,
    in_gain,
    out_gain,
    conv_inner,
    conv_shared,
    head_params,
    first_in_weight,
    first_out_weight,
    first_in_gain,
    first_out_gain,
    first_conv_inner,
    first_conv_shared,
    first_head_params,
    second_in_weight,
    second_out_weight,
    second_in_gain,
    second_out_gain,
    second_conv_inner,
    second_conv_shared,
    second_head_params,
):
    seq_index = lax.axis_index("seq")
    wsh_index = lax.axis_index("wshard")
    n_seq = lax.axis_size("seq")
    n_wsh = lax.axis_size("wshard")
    rows_in, cols_in = in_weight.shape
    rows_out = out_weight.shape[0]
    tokens, width_in = block_in.shape[1:]
    heads = head_params.shape[1] // n_seq
    width = heads * P_SIZE
    inner_all = out_gain.shape[0]
    share = 2 * N_STATE // n_seq

    inputs = block_in[0].astype(f32)
    rms_in = lax.rsqrt(jnp.mean(inputs * inputs, axis=-1, keepdims=True) + norm_eps)
    normed = (inputs * rms_in * in_gain).astype(bf16)
    normed_all = lax.all_gather(normed, "seq", axis=0, tiled=True)
    cot = cotangent[0]
    cot_all = lax.all_gather(cot, "seq", axis=0, tiled=True)
    in_w16 = in_weight.astype(bf16)
    main_send = in_w16[:, : 2 * inner_all].reshape(rows_in, n_seq, 2 * width)
    main_send = jnp.swapaxes(main_send, 0, 1)
    small_send = in_w16[:, 2 * inner_all :]
    small_send = jnp.pad(small_send, ((0, 0), (0, -small_send.shape[1] % LANES)))
    w_main, w_small, w_out = spread_weights(
        main_send, small_send, out_weight.astype(bf16), n_seq, n_wsh
    )
    w_main = w_main.reshape(width_in, 2 * width)
    w_small = w_small.reshape(width_in, small_send.shape[1])
    w_out = w_out.reshape(width, width_in)
    w_shared = w_small[:, : 2 * N_STATE]
    w_step = lax.dynamic_slice_in_dim(w_small, 2 * N_STATE + seq_index * heads, heads, 1)
    w_share = lax.dynamic_slice_in_dim(w_small, seq_index * share, share, 1)
    w_ext = jnp.pad(
        jnp.concatenate([w_share, w_step], axis=1), ((0, 0), (0, LANES - share - heads))
    )
    w_step = jnp.pad(w_step, ((0, 0), (0, LANES - heads)))

    main = mm(normed_all, w_main, NN).astype(bf16)
    small = mm(normed_all, jnp.concatenate([w_shared, w_step], axis=1), NN).astype(bf16)
    head_local = lax.dynamic_slice_in_dim(head_params, seq_index * heads, heads, 1)
    head = jnp.pad(head_local, ((0, 5), (0, LANES - heads)))
    conv_local = lax.dynamic_slice_in_dim(conv_inner, seq_index * width, width, 1)
    taps = jnp.pad(jnp.concatenate([conv_shared, conv_local], axis=1), ((0, 3), (0, 0)))
    gain_local = lax.dynamic_slice_in_dim(out_gain, seq_index * width, width, 0)
    gated, y, states = mixer_forward(main, small, head, taps, heads)
    d_gnormed = mm(cot_all, w_out, NT)
    gated32 = gated.astype(f32)
    scaled = d_gnormed * gain_local
    stats = jnp.stack(
        [jnp.sum(gated32 * gated32, axis=-1), jnp.sum(scaled * gated32, axis=-1)]
    )
    stats = sum_over_seq(stats.reshape(-1, LANES), n_seq).reshape(stats.shape)
    rms_out = lax.rsqrt(stats[0] / inner_all + norm_eps)[:, None]
    mean_sg = (stats[1] / inner_all)[:, None]
    gnormed = (gated32 * rms_out * gain_local).astype(bf16)
    d_gated = (rms_out * scaled - gated32 * rms_out**3 * mean_sg).astype(bf16)
    d_out_gain = jnp.sum(d_gnormed * gated32 * rms_out, axis=0)

    g_out = mm(gnormed, cot_all, TN)
    grad_out_weight = lax.dynamic_slice_in_dim(g_out, wsh_index * rows_out, rows_out, 0)
    for j in range(1, n_wsh):
        to = lax.rem(wsh_index + j, n_wsh)
        part = lax.dynamic_slice_in_dim(g_out, to * rows_out, rows_out, 0)
        grad_out_weight = grad_out_weight + lax.ppermute(
            part, "wshard", [(i, (i + j) % n_wsh) for i in range(n_wsh)]
        )
    mixed = lax.psum_scatter(
        mm(gnormed, w_out, NN).astype(bf16), "seq", scatter_dimension=0, tiled=True
    )
    block_out = (inputs + mixed.astype(f32))[None]
    dmain, dshared_t, dstep, dtaps, dhead = mixer_backward(
        main, small, head, taps, y, states, d_gated, heads
    )

    (shared_parts,) = swap(
        (dshared_t.reshape(n_seq, share, -1),), ((0, "seq"),), n_seq, n_wsh, 2, "swap_shared"
    )
    shared_sum = jnp.sum(shared_parts.astype(f32), axis=0).astype(bf16)
    d_ext = jnp.pad(
        jnp.concatenate([shared_sum.T, dstep[:, :heads]], axis=1),
        ((0, 0), (0, LANES - share - heads)),
    )
    d_normed = mm(dmain, w_main, NT) + mm(d_ext, w_ext, NT)
    d_normed = lax.psum_scatter(
        d_normed.astype(bf16), "seq", scatter_dimension=0, tiled=True
    ).astype(f32)

    g_main = mm(normed_all, dmain, TN).astype(bf16).reshape(n_seq, n_wsh, rows_in, 2 * width)
    g_ext = mm(normed_all, d_ext, TN).astype(bf16).reshape(n_seq, n_wsh, rows_in, LANES)
    g_main, g_ext = swap(
        (g_main, g_ext), ((1, "wshard"), (1, "wshard")), n_seq, n_wsh, 3, "swap_grads"
    )
    g_main = jnp.sum(g_main.astype(f32), axis=0).astype(bf16)
    g_ext = jnp.sum(g_ext.astype(f32), axis=0).astype(bf16)

    d_in_gain = jnp.sum(d_normed * inputs * rms_in, axis=0)
    scaled_in = d_normed * in_gain
    grad_in = (
        cot.astype(f32)
        + rms_in * scaled_in
        - inputs * rms_in**3 * jnp.mean(scaled_in * inputs, axis=-1, keepdims=True)
    )[None]

    d_skip = dtaps[5, 2 * N_STATE :].reshape(heads, P_SIZE).sum(-1)
    d_head = jnp.concatenate([dhead[:2, :heads], d_skip[None]], axis=0)
    pieces = (
        d_in_gain,
        dtaps[:5, : 2 * N_STATE],
        d_out_gain,
        dtaps[:5, 2 * N_STATE :],
        d_head,
    )
    flat = jnp.concatenate([p.reshape(-1) for p in pieces])
    flat = jnp.pad(flat, (0, -flat.shape[0] % (8 * LANES))).reshape(-1, LANES)
    g_main, g_ext, flat = swap(
        (g_main, g_ext, flat),
        ((0, "seq"), (0, "seq"), ("all", "both")),
        n_seq,
        n_wsh,
        4,
        "swap_last",
    )
    g_main = jnp.swapaxes(g_main, 0, 1).reshape(rows_in, 2 * inner_all)
    g_ext = jnp.swapaxes(g_ext, 0, 1)
    grad_in_weight = jnp.concatenate(
        [
            g_main,
            g_ext[:, :, :share].reshape(rows_in, 2 * N_STATE),
            g_ext[:, :, share : share + heads].reshape(rows_in, heads * n_seq),
        ],
        axis=1,
    ).astype(f32)
    flat = jnp.sum(flat.reshape(n_seq, n_wsh, -1), axis=1)
    sums, at = [], 0
    for p in pieces:
        sums.append(flat[:, at : at + p.size].reshape((n_seq,) + p.shape))
        at += p.size
    grad_in_gain = jnp.sum(sums[0], axis=0)
    grad_conv_shared = jnp.sum(sums[1], axis=0)
    grad_out_gain = sums[2].reshape(-1)
    grad_conv_inner = jnp.swapaxes(sums[3], 0, 1).reshape(conv_inner.shape)
    grad_head_params = jnp.swapaxes(sums[4], 0, 1).reshape(head_params.shape)
    new_in_weight, new_first_in_weight, new_second_in_weight = adamw(
        in_weight,
        grad_in_weight,
        first_in_weight,
        second_in_weight,
        weight_learning_rate,
        matrix_decay,
    )
    new_out_weight, new_first_out_weight, new_second_out_weight = adamw(
        out_weight,
        grad_out_weight,
        first_out_weight,
        second_out_weight,
        weight_learning_rate,
        matrix_decay,
    )
    updated_input_gain, new_first_in_gain, new_second_in_gain = adamw(
        in_gain, grad_in_gain, first_in_gain, second_in_gain, small_rate, 0.0
    )
    new_out_gain, new_first_out_gain, new_second_out_gain = adamw(
        out_gain, grad_out_gain, first_out_gain, second_out_gain, small_rate, 0.0
    )
    new_conv_inner, new_first_conv_inner, new_second_conv_inner = adamw(
        conv_inner, grad_conv_inner, first_conv_inner, second_conv_inner, small_rate, 0.0
    )
    new_conv_shared, new_first_conv_shared, new_second_conv_shared = adamw(
        conv_shared, grad_conv_shared, first_conv_shared, second_conv_shared, small_rate, 0.0
    )
    new_head_params, updated_head_first_moment, head_second_all = adamw(
        head_params, grad_head_params, first_head_params, second_head_params, small_rate, 0.0
    )
    return (
        block_out,
        grad_in,
        grad_in_weight,
        grad_out_weight,
        grad_in_gain,
        grad_out_gain,
        grad_conv_inner,
        grad_conv_shared,
        grad_head_params,
        new_in_weight,
        new_out_weight,
        updated_input_gain,
        new_out_gain,
        new_conv_inner,
        new_conv_shared,
        new_head_params,
        new_first_in_weight,
        new_first_out_weight,
        new_first_in_gain,
        new_first_out_gain,
        new_first_conv_inner,
        new_first_conv_shared,
        updated_head_first_moment,
        new_second_in_weight,
        new_second_out_weight,
        new_second_in_gain,
        new_second_out_gain,
        new_second_conv_inner,
        new_second_conv_shared,
        head_second_all[0:2],
        head_second_all[2],
    )


def solution(mesh):
    return jax.shard_map(
        local,
        mesh=mesh,
        in_specs=(
            P("wshard", "seq", None),
            P("wshard", "seq", None),
            P(("seq", "wshard"), None),
            P(("seq", "wshard"), None),
            P(),
            P(),
            P(),
            P(),
            P(),
            P(("seq", "wshard"), None),
            P(("seq", "wshard"), None),
            P(),
            P(),
            P(),
            P(),
            P(),
            P(("seq", "wshard"), None),
            P(("seq", "wshard"), None),
            P(),
            P(),
            P(),
            P(),
            P(),
        ),
        out_specs=(
            P("wshard", "seq", None),
            P("wshard", "seq", None),
            P(("seq", "wshard"), None),
            P(("seq", "wshard"), None),
            P(),
            P(),
            P(),
            P(),
            P(),
            P(("seq", "wshard"), None),
            P(("seq", "wshard"), None),
            P(),
            P(),
            P(),
            P(),
            P(),
            P(("seq", "wshard"), None),
            P(("seq", "wshard"), None),
            P(),
            P(),
            P(),
            P(),
            P(),
            P(("seq", "wshard"), None),
            P(("seq", "wshard"), None),
            P(),
            P(),
            P(),
            P(),
            P(),
            P(),
        ),
        check_vma=False,
    )
```

time: 2040 us -> 448 us (0.22)
  waiting for transfers between devices: 958 us -> 0.78 us
  local copies, waits for them, and re-layouts: 484 us -> 28.1 us
  Pallas kernels: 0 us -> 294 us
  other arithmetic: 326 us -> 39.5 us
  matrix products: 211 us -> 62.6 us
    reduce_scatter x3 -> x2, waiting for transfers between devices: 566 us -> 0.01 us  [the longest x1 0.01 us: local(): lax.psum_scatter(d_normed.astype(bf16), 'seq', scatter_dimension=0, tiled...]
    pallas_call x0 -> x7, Pallas kernels: none -> 294 us  [the longest x3 132 us: swap(): pl.pallas_call(functools.partial(swap_kernel, plan, n_seq, n_wsh), in_spe...]
    dynamic_update_slice x57 -> x0, local copies, waits for them, and re-layouts: 215 us -> none  [the longest x56 215 us: state_space(): lax.scan(jax.checkpoint(block_step), start, (blockify(inner), blockify(st...]
    all_gather x3 -> x2, waiting for transfers between devices: 209 us -> 0.01 us  [the longest x1 0.01 us: local(): cot_all = lax.all_gather(cot, 'seq', axis=0, tiled=True)]
    dot_general x118 -> x9, matrix products: 211 us -> 62.6 us  [mm(): return lax.dot_general(a, b, dims, preferred_element_type=f32)]
    unnamed x10 -> x1, other arithmetic: 132 us -> 0.01 us
    psum x1 -> x0, waiting for transfers between devices: 94.3 us -> none  [local(): lax.psum((d_in_gain, d_out_gain, d_conv_full, d_common, d_head_full), ('s...]
    another operation x57 -> x1, other arithmetic: 93.3 us -> 0.02 us  [local(): jnp.stack([jnp.sum(gated32 * gated32, axis=-1), jnp.sum(scaled * gated32,...]
  transfers between devices with their start and end apart: 13 -> 7, of which waited for: 9 -> 0; matrix products, arithmetic and copies ran while one was open for 12% -> 20% of each run, Pallas kernels for 0% -> 50%
where the time goes in v1:
time: 448 us; the launch traced here: 447 us
  Pallas kernels  294 us (66%)
  matrix products  62.6 us (14%)
  other arithmetic  39.5 us (9%)
  local copies, waits for them, and re-layouts  28.1 us (6%)
  between operations  14.4 us (3%)
  starting transfers between devices  7.36 us (2%)
    pallas_call x3, Pallas kernels, swap(): pl.pallas_call(functools.partial(swap_kernel, plan, n_seq, n_wsh), in_spe...  132 us
    pallas_call x1, Pallas kernels, spread_weights(): pl.pallas_call(functools.partial(weights_kernel, n_seq, n_wsh), in_specs=...  86.8 us
    dot_general x9, matrix products, mm(): return lax.dot_general(a, b, dims, preferred_element_type=f32)  62.6 us
    pallas_call x1, Pallas kernels, mixer_backward(): pl.pallas_call(functools.partial(bwd_kernel, heads, count), grid=(count,)...  46.1 us
    pallas_call x1, Pallas kernels, mixer_forward(): pl.pallas_call(functools.partial(fwd_kernel, heads), grid=(count,), in_sp...  20.3 us
    sub x7, other arithmetic, adamw(): return (param - rate * (corrected + decay * param), first_new, second_new)  14 us
  transfers between devices with their start and end apart: 7, of which 0 were waited for; matrix products, arithmetic and copies ran while one was open for 20% of the time, Pallas kernels for 50%

profile of v1, /device:TPU:0, one launch (start us, length us, event | category | flops | bytes accessed | tf_op | source)
XLA Modules:
  0.0 447.1 jit_solution(77473674748981319)
XLA Ops:
  7.2 1.4 fusion.18
  9.2 2.4 fusion.20
  11.6 0.7 all-gather.6.cloned.1.call-update
  12.5 0.9 copy-done.3
  13.5 0.7 convert_element_type.78.outw
  14.2 0.9 copy.91
  15.1 0.6 pad.28.small
  15.7 86.8 %spread_weights.1 = (bf16[8,4,48,768]{3,2,1,0:T(8,128)(2,1)}, bf16[8,4,48,384]{3,2,1,0:T(8,128)(2,1)}, bf16[4,96,1536]{2,1,0:T(8,128)(2,1)}) custom-call(bf16[8,48,768]{2,1,0:T(8,128)(2,1)} %bitcast.81, bf16[48,384]{1,0:T(8,128)(2,1)} %pad.28.small, bf16[96,1536]{1,0:T(8,128)(2,1)} %convert_element_type.78.outw), custom_call_target="tpu_custom_call" | custom-call | bytes 200000000 | tf_op jit(solution)/shard_map/spread_weights/pallas_call | solution.py:473
  102.5 2.2 slice.80
  104.9 0.8 copy.84
  105.7 0.9 constant_dynamic-slice_fusion.3
  106.6 1.9 copy.85
  108.5 0.8 dynamic_slice.30
  109.9 0.7 constant_dynamic-slice_fusion.4
  110.6 0.6 select_maximum_fusion.taps_ref
  111.2 7.7 %convolution_convert_fusion.3.small_ref.small_prev = bf16[2048,384]{1,0:T(8,128)(2,1)} fusion(bf16[2048,1536]{1,0:T(8,128)(2,1)} %all-gather.4.cloned.1.call-done, bf16[1536,6]{1,0:T(8,128)(2,1)S(1)} %constant_dynamic-slice_fusion.6, bf16[1536,256]{1,0:T(8,128)(2,1)} %slice.80), kind=kOutput, calls=%fused_computation.29 | convolution fusion | flops 2420244480 | bytes 8669184 | tf_op jit(solution)/shard_map/dot_general | solution.py:32
  119.0 6.5 %convolution_convert_fusion.2.main_ref.main_prev = bf16[2048,768]{1,0:T(8,128)(2,1)} fusion(bf16[2048,1536]{1,0:T(8,128)(2,1)S(1)} %copy-done.39, bf16[1536,768]{1,0:T(8,128)(2,1)S(1)} %bitcast.103), kind=kOutput, calls=%fused_computation.18 | convolution fusion | flops 4833411072 | bytes 11796480 | tf_op jit(solution)/shard_map/dot_general | solution.py:32
  125.4 20.3 %mixer_forward.1 = (bf16[2048,384]{1,0:T(8,128)(2,1)}, f32[2048,384]{1,0:T(8,128)}, f32[16,128,384]{2,1,0:T(8,128)}) custom-call(bf16[2048,768]{1,0:T(8,128)(2,1)} %convolution_convert_fusion.2.main_ref.main_prev, bf16[2048,384]{1,0:T(8,128)(2,1)} %convolution_convert_fusion.3.small_ref.small_prev, f32[8,128]{1,0:T(8,128)} %pad.30.head_ref, ...), custom_call_target="tpu_custom_call" | custom-call | tf_op jit(solution)/shard_map/mixer_forward/pallas_call | solution.py:189
  145.7 8.9 %fusion.4 = (f32[2048]{0:T(1024)S(1)}, f32[2048]{0:T(1024)S(1)}, f32[384,2048]{0,1:T(8,128)}) fusion(bf16[2048,384]{1,0:T(8,128)(2,1)} %get-tuple-element.49, f32[384]{0:T(512)S(1)} %dynamic_slice.30, bf16[384,1536]{1,0:T(8,128)(2,1)} %bitcast.104, bf16[1,2048,1536]{2,1,0:T(8,128)(2,1)} %all-gather.6.cloned.1.call-done), kind=kOutput, calls=%fused_computation.19 | convolution fusion | flops 2420633600 | bytes 12207616 | tf_op jit(solution)/shard_map/dot_general | solution.py:32
  154.6 0.6 reshape.184.x_ref
  155.3 8.8 %sum_over_seq.1 = f32[32,128]{1,0:T(8,128)} custom-call(f32[32,128]{1,0:T(8,128)} %reshape.184.x_ref), custom_call_target="tpu_custom_call" | custom-call | tf_op jit(solution)/shard_map/sum_over_seq/pallas_call | solution.py:619
  164.1 0.7 multiply_multiply_fusion.6
  164.8 0.7 multiply_bitcast_fusion
  165.5 4.2 fusion.12
  169.7 46.1 %mixer_backward.1 = (bf16[2048,768]{1,0:T(8,128)(2,1)}, bf16[256,2048]{1,0:T(8,128)(2,1)}, bf16[2048,128]{1,0:T(8,128)(2,1)}, f32[8,640]{1,0:T(8,128)}, f32[8,128]{1,0:T(8,128)}) custom-call(bf16[2048,768]{1,0:T(8,128)(2,1)} %convolution_convert_fusion.2.main_ref.main_prev, bf16[2048,384]{1,0:T(8,128)(2,1)} %convolution_convert_fusion.3.small_ref.small_prev, ...), custom_call_target="tpu_custom_call" | custom-call | tf_op jit(solution)/shard_map/mixer_backward/pallas_call | solution.py:359
  215.8 14.6 %swap_shared.1 = bf16[8,32,2048]{2,1,0:T(8,128)(2,1)} custom-call(bf16[8,32,2048]{2,1,0:T(8,128)(2,1)} %bitcast.87), custom_call_target="tpu_custom_call" | custom-call | tf_op jit(solution)/shard_map/swap_shared/pallas_call | solution.py:583
  230.5 1.4 reduce_sum.131
  231.9 1.9 copy.76
  233.8 7.9 %fusion.73 = f32[2048,1536]{1,0:T(8,128)S(1)} fusion(bf16[2048,768]{1,0:T(8,128)(2,1)} %get-tuple-element.53, bf16[1536,768]{1,0:T(8,128)(2,1)} %bitcast.102), kind=kOutput, calls=%fused_computation.132 | convolution fusion | flops 4831838208 | bytes 18087936 | tf_op jit(solution)/shard_map/dot_general | solution.py:32
  241.7 4.5 %add_convert_fusion = bf16[2048,1536]{1,0:T(8,128)(2,1)} fusion(f32[2048,1536]{1,0:T(8,128)S(1)} %fusion.73, bf16[1536,6]{0,1:T(8,128)(2,1)S(1)} %copy-done.18, bf16[1536,32]{0,1:T(8,128)(2,1)S(1)} %copy-done.10, bf16[2048,6]{0,1:T(8,128)(2,1)S(1)} %copy-done.15, bf16[2048,32]{0,1:T(8,128)(2,1)S(1)} %bitcast.90), kind=kOutput, calls=%fused_computation | convolution fusion | flops 814809088 | bytes 19146752 | tf_op jit(solution)/shard_map/dot_general | solution.py:32
  246.3 6.8 %convolution_convert_fusion = bf16[2048,1536]{1,0:T(8,128)(2,1)} fusion(bf16[384,1536]{1,0:T(8,128)(2,1)} %bitcast.105, bf16[2048,384]{1,0:T(8,128)(2,1)S(1)} %copy-done.6, f32[2048]{0:T(1024)S(1)} %get-tuple-element.98, f32[384]{0:T(512)} %copy-done.33), kind=kOutput, calls=%fused_computation.1 | convolution fusion | flops 2422210560 | bytes 9053696 | tf_op jit(solution)/shard_map/dot_general | solution.py:32
  253.1 1.3 slice.65
  254.4 1.3 slice.66
  255.7 1.3 slice.67
  257.0 1.3 slice_reduce_fusion.2
  258.3 1.4 reshape_squeeze.3
  259.6 1.3 reduce_sum.137
  261.0 5.6 %fusion = f32[384,1536]{1,0:T(8,128)S(1)} fusion(bf16[1,2048,1536]{2,1,0:T(8,128)(2,1)} %all-gather.6.cloned.1.call-done, bf16[2048,384]{1,0:T(8,128)(2,1)S(1)} %copy-done.6, f32[2048]{0:T(1024)S(1)} %get-tuple-element.98, f32[384]{0:T(512)} %copy-done.33), kind=kOutput, calls=%fused_computation.2 | convolution fusion | flops 2419064832 | bytes 10233344 | tf_op jit(solution)/shard_map/dot_general | solution.py:32
  266.6 1.3 constant_dynamic-slice_fusion.2
  267.8 0.8 copy-done.4
  268.7 5.7 %collective-permute-start = (f32[96,1536]{1,0:T(8,128)}, f32[96,1536]{1,0:T(8,128)}, u32[]{:S(2)}, u32[]{:S(2)}) collective-permute-start(f32[96,1536]{1,0:T(8,128)} %get-tuple-element.92), channel_id=1, source_target_pairs={{0,1},{1,2},{2,3},{3,0},{4,5},{5,6},{6,7},{7,4},{8,9},{9,10},{10,1... | collective-permute-start | bytes 1769480 | tf_op jit(solution)/shard_map/ppermute | solution.py:733
  274.3 0.8 collective-permute-start.2
  275.2 0.7 collective-permute-start.1
  275.9 9.3 %convolution_convert_fusion.1 = bf16[1536,768]{1,0:T(8,128)(2,1)} fusion(bf16[2048,1536]{1,0:T(8,128)(2,1)} %all-gather.4.cloned.1.call-done, bf16[2048,768]{1,0:T(8,128)(2,1)S(1)} %copy-done.40), kind=kOutput, calls=%fused_computation.17 | convolution fusion | flops 4833017856 | bytes 11796480 | tf_op jit(solution)/shard_map/dot_general | solution.py:32
  285.3 5.5 %convolution_convert_fusion.4 = bf16[1536,128]{1,0:T(8,128)(2,1)} fusion(bf16[2048,1536]{1,0:T(8,128)(2,1)} %all-gather.4.cloned.1.call-done, bf16[2048,6]{0,1:T(8,128)(2,1)S(1)} %copy-done.16, bf16[2048,32]{0,1:T(8,128)(2,1)S(1)} %bitcast.91), kind=kOutput, calls=%fused_computation.30 | convolution fusion | flops 807337984 | bytes 6840320 | tf_op jit(solution)/shard_map/dot_general | solution.py:32
  290.8 93.9 %swap_grads.1 = (bf16[4,8,48,768]{3,2,1,0:T(8,128)(2,1)}, bf16[4,8,48,128]{3,2,1,0:T(8,128)(2,1)}) custom-call(bf16[8,4,48,768]{3,2,1,0:T(8,128)(2,1)} %bitcast.82, bf16[8,4,48,128]{3,2,1,0:T(8,128)(2,1)} %bitcast.97), custom_call_target="tpu_custom_call" | custom-call | tf_op jit(solution)/shard_map/swap_grads/pallas_call | solution.py:583
  384.7 3.1 reduce_sum.133.refs_0_
  387.7 0.7 reduce_sum.134.refs_1_
  388.5 3.6 multiply_subtract_fusion.1
  392.1 2.2 fusion.25
  394.3 0.6 pad_bitcast_fusion.refs_2_
  394.9 23.8 %swap_last.1 = (bf16[8,48,768]{2,1,0:T(8,128)(2,1)}, bf16[8,48,128]{2,1,0:T(8,128)(2,1)}, f32[32,48,128]{2,1,0:T(8,128)}) custom-call(bf16[8,48,768]{2,1,0:T(8,128)(2,1)} %reduce_sum.133.refs_0_, bf16[8,48,128]{2,1,0:T(8,128)(2,1)} %reduce_sum.134.refs_1_, f32[48,128]{1,0:T(8,128)} %pad_bitcast_fusion.refs_2_), custom_call_target="tpu_custom_call" | custom-call | tf_op jit(solution)/shard_map/swap_last/pallas_call | solution.py:583
  418.8 1.4 reshape.195
  420.8 0.6 copy-done.7
  421.4 1.1 copy.88
  423.0 0.7 copy.81
  423.9 1.3 multiply_subtract_fusion.6
  425.9 1.3 broadcast_multiply_fusion
  427.7 1.3 multiply_subtract_fusion.4
  429.0 1.3 multiply_subtract_fusion.5
  430.4 1.4 multiply_subtract_fusion.3
  431.7 0.8 multiply_subtract_fusion.2
  432.6 4.3 multiply_subtract_fusion
  436.9 3.7 fusion.17
  (135 shorter events, 4.3 us)
Async XLA Ops:
  7.2 104.0 %all-gather.4.cloned.1.call-start = ((), (), s32[]{:S(2)}) async-start(), calls=%async_computation.2 | async-start | bytes 7077888 | tf_op jit(solution)/shard_map/all_gather | solution.py:685
  9.2 3.1 copy-start.29
  9.2 3.2 copy-start.1
  11.6 134.2 %all-gather.6.cloned.1.call-start = ((), (), s32[]{:S(2)}) async-start(), calls=%async_computation.5 | async-start | bytes 7077888 | tf_op jit(solution)/shard_map/all_gather | solution.py:687
  12.3 379.7 %reduce-scatter.5.cloned.1.call-start = ((), (), s32[]{:S(2)}) async-start(), calls=%async_computation.4 | async-start | bytes 7077888 | tf_op jit(solution)/shard_map/reduce_scatter | solution.py:753
  12.4 1.1 copy-start.3
  102.5 2.2 copy-start.5
  104.7 4.5 %copy-start.35 = (f32[3,48]{1,0:T(4,128)S(1)}, f32[3,48]{1,0:T(4,128)}, u32[]{:S(2)}) copy-start(f32[3,48]{1,0:T(4,128)} %param.31) | copy-start | bytes 1732
  104.7 5.9 %copy-start.23 = (f32[5,256]{1,0:T(8,128)S(1)}, f32[5,256]{1,0:T(8,128)}, u32[]{:S(2)}) copy-start(f32[5,256]{1,0:T(8,128)} %param.30) | copy-start | bytes 15364
  109.2 56.3 %copy-start.33 = (f32[384]{0:T(512)}, f32[384]{0:T(512)S(1)}, u32[]{:S(2)}) copy-start(f32[384]{0:T(512)S(1)} %dynamic_slice.30) | copy-start | bytes 4612
  111.2 7.7 %copy-start.39 = (bf16[2048,1536]{1,0:T(8,128)(2,1)S(1)}, bf16[2048,1536]{1,0:T(8,128)(2,1)}, u32[]{:S(2)}) copy-start(bf16[2048,1536]{1,0:T(8,128)(2,1)} %all-gather.4.cloned.1.call-done) | copy-start | bytes 18874372
  111.2 7.7 %copy-start.41 = (bf16[8,4,48,768]{3,2,1,0:T(8,128)(2,1)S(1)}, bf16[8,4,48,768]{3,2,1,0:T(8,128)(2,1)}, u32[]{:S(2)}) copy-start(bf16[8,4,48,768]{3,2,1,0:T(8,128)(2,1)} %get-tuple-element.47) | copy-start | bytes 7077892
  145.7 19.8 %copy-start.6 = (bf16[2048,384]{1,0:T(8,128)(2,1)S(1)}, bf16[2048,384]{1,0:T(8,128)(2,1)}, u32[]{:S(2)}) copy-start(bf16[2048,384]{1,0:T(8,128)(2,1)} %get-tuple-element.49) | copy-start | bytes 4718596
  233.8 7.9 %copy-start.10 = (bf16[1536,32]{0,1:T(8,128)(2,1)S(1)}, bf16[1536,32]{0,1:T(8,128)(2,1)}, u32[]{:S(2)}) copy-start(bf16[1536,32]{0,1:T(8,128)(2,1)} %copy.85) | copy-start | bytes 294916
  233.8 7.9 %copy-start.15 = (bf16[2048,6]{0,1:T(8,128)(2,1)S(1)}, bf16[2048,6]{0,1:T(8,128)(2,1)}, u32[]{:S(2)}) copy-start(bf16[2048,6]{0,1:T(8,128)(2,1)} %copy.76) | copy-start | bytes 73732
  233.8 7.9 %copy-start.18 = (bf16[1536,6]{0,1:T(8,128)(2,1)S(1)}, bf16[1536,6]{0,1:T(8,128)(2,1)}, u32[]{:S(2)}) copy-start(bf16[1536,6]{0,1:T(8,128)(2,1)} %copy.84) | copy-start | bytes 55300
  246.2 190.6 %reduce-scatter.3.cloned.1.call-start = ((), (), s32[]{:S(2)}) async-start(), calls=%async_computation.3 | async-start | bytes 7077888 | tf_op jit(solution)/shard_map/reduce_scatter | solution.py:736
  266.6 2.1 copy-start.4
  266.6 9.3 %copy-start.40 = (bf16[2048,768]{1,0:T(8,128)(2,1)S(1)}, bf16[2048,768]{1,0:T(8,128)(2,1)}, u32[]{:S(2)}) copy-start(bf16[2048,768]{1,0:T(8,128)(2,1)} %get-tuple-element.53) | copy-start | bytes 9437188
  268.7 119.8 %collective-permute-start = (f32[96,1536]{1,0:T(8,128)}, f32[96,1536]{1,0:T(8,128)}, u32[]{:S(2)}, u32[]{:S(2)}) collective-permute-start(f32[96,1536]{1,0:T(8,128)} %get-tuple-element.92), channel_id=1, source_target_pairs={{0,1},{1,2},{2,3},{3,0},{4,5},{5,6},{6,7},{7,4},{8,9},{9,10},{10,1... | collective-permute-start | bytes 1769480 | tf_op jit(solution)/shard_map/ppermute | solution.py:733
  274.3 114.1 %collective-permute-start.2 = (f32[96,1536]{1,0:T(8,128)}, f32[96,1536]{1,0:T(8,128)}, u32[]{:S(2)}, u32[]{:S(2)}) collective-permute-start(f32[96,1536]{1,0:T(8,128)} %get-tuple-element.93), channel_id=1, source_target_pairs={{0,3},{1,0},{2,1},{3,2},{4,7},{5,4},{6,5},{7,6},{8,11},{9,8},{10,9... | collective-permute-start | bytes 1769480 | tf_op jit(solution)/shard_map/ppermute | solution.py:733
  275.2 10.0 %copy-start.37 = (f32[2,6]{1,0:T(2,128)S(1)}, f32[2,6]{1,0:T(2,128)}, u32[]{:S(2)}) copy-start(f32[2,6]{1,0:T(2,128)} %slice.67) | copy-start | bytes 148
  275.2 10.0 %copy-start.38 = (f32[6]{0:T(128)S(1)}, f32[6]{0:T(128)}, u32[]{:S(2)}) copy-start(f32[6]{0:T(128)} %reduce_sum.137) | copy-start | bytes 76
  275.2 10.1 %copy-start.21 = (f32[5,384]{1,0:T(8,128)S(1)}, f32[5,384]{1,0:T(8,128)}, u32[]{:S(2)}) copy-start(f32[5,384]{1,0:T(8,128)} %slice.66) | copy-start | bytes 23044
  275.2 10.1 %copy-start.27 = (f32[5,256]{1,0:T(8,128)S(1)}, f32[5,256]{1,0:T(8,128)}, u32[]{:S(2)}) copy-start(f32[5,256]{1,0:T(8,128)} %slice.65) | copy-start | bytes 15364
  275.2 10.1 %copy-start.16 = (bf16[2048,6]{0,1:T(8,128)(2,1)S(1)}, bf16[2048,6]{0,1:T(8,128)(2,1)}, u32[]{:S(2)}) copy-start(bf16[2048,6]{0,1:T(8,128)(2,1)} %copy.76) | copy-start | bytes 73732
  275.2 113.3 %collective-permute-start.1 = (f32[96,1536]{1,0:T(8,128)}, f32[96,1536]{1,0:T(8,128)}, u32[]{:S(2)}, u32[]{:S(2)}) collective-permute-start(f32[96,1536]{1,0:T(8,128)} %get-tuple-element.94), channel_id=1, source_target_pairs={{0,2},{1,3},{2,0},{3,1},{4,6},{5,7},{6,4},{7,5},{8,10},{9,11},{10,... | collective-permute-start | bytes 1769480 | tf_op jit(solution)/shard_map/ppermute | solution.py:733
  384.6 3.1 copy-start.11
  384.7 3.8 copy-start.9
  388.4 3.6 copy-start
  388.4 3.6 copy-start.14
  388.4 3.7 copy-start.30
  392.0 2.2 copy-start.28
  392.0 2.2 copy-start.32
  418.8 3.8 copy-start.12
  420.2 7.4 %copy-start.24 = (f32[5,256]{1,0:T(8,128)S(1)}, f32[5,256]{1,0:T(8,128)}, u32[]{:S(2)}) copy-start(f32[5,256]{1,0:T(8,128)} %param.30) | copy-start | bytes 15364
  420.7 0.7 copy-start.7
  420.8 11.0 %copy-start.17 = (f32[5,3072]{1,0:T(8,128)S(1)}, f32[5,3072]{1,0:T(8,128)}, u32[]{:S(2)}) copy-start(f32[5,3072]{1,0:T(8,128)} %param.29) | copy-start | bytes 184324
  420.8 11.0 %copy-start.19 = (f32[5,3072]{1,0:T(8,128)S(1)}, f32[5,3072]{1,0:T(8,128)}, u32[]{:S(2)}) copy-start(f32[5,3072]{1,0:T(8,128)} %param.36) | copy-start | bytes 184324
  420.8 11.0 %copy-start.20 = (f32[5,3072]{1,0:T(8,128)S(1)}, f32[5,3072]{1,0:T(8,128)}, u32[]{:S(2)}) copy-start(f32[5,3072]{1,0:T(8,128)} %param.43) | copy-start | bytes 184324
  421.4 2.3 copy-start.8
  421.4 2.3 slice-start
  421.4 4.4 slice-start.1
  421.4 4.4 slice-start.2
  423.7 8.8 %copy-start.26 = (f32[5,256]{1,0:T(8,128)}, f32[5,256]{1,0:T(8,128)S(1)}, u32[]{:S(2)}) copy-start(f32[5,256]{1,0:T(8,128)S(1)} %reduce_sum.141) | copy-start | bytes 15364
  423.9 8.6 %copy-start.34 = (f32[3,48]{1,0:T(4,128)}, f32[3,48]{1,0:T(4,128)S(1)}, u32[]{:S(2)}) copy-start(f32[3,48]{1,0:T(4,128)S(1)} %reshape.200) | copy-start | bytes 1732
  425.8 6.7 %copy-start.22 = (f32[3072]{0:T(1024)}, f32[3072]{0:T(1024)S(1)}, u32[]{:S(2)}) copy-start(f32[3072]{0:T(1024)S(1)} %reshape.196) | copy-start | bytes 36868
  425.9 11.0 %copy-start.13 = (f32[1,5,8,384]{3,1,2,0:T(8,128)}, f32[1,5,8,384]{3,1,2,0:T(8,128)S(1)}, u32[]{:S(2)}) copy-start(f32[1,5,8,384]{3,1,2,0:T(8,128)S(1)} %copy.89) | copy-start | bytes 184324
  425.9 6.6 %copy-start.25 = (f32[1536]{0:T(1024)}, f32[1536]{0:T(1024)S(1)}, u32[]{:S(2)}) copy-start(f32[1536]{0:T(1024)S(1)} %slice_reduce_fusion) | copy-start | bytes 18436
  432.5 4.3 copy-start.2
  432.5 4.3 copy-start.31
  432.5 4.3 copy-start.36
Sparse Core Ops, SparseCore 0:
  11.7 61.2 all-gather.3
  74.9 45.3 all-gather.5
  246.3 66.3 reduce-scatter.4
  316.0 61.7 reduce-scatter.2

commit v2 on v1

--- a/solution.py
+++ b/solution.py
@@ -11,6 +11,7 @@
 N_STATE = 128
 LANES = 128
 CHUNK = 128
+STEP_ROWS = 16
 
 norm_eps = 1e-05
 beta_one = 0.9
@@ -314,7 +315,7 @@
     suffix = jnp.where(c >= r, 1.0, 0.0).astype(f32)
     ddecay = mm_high(suffix, dcumul)
     dstep = (mm_high(inner * z, pick) + neg_rate * ddecay) * jax.nn.sigmoid(step_in)
-    dstep_ref[...] = dstep.astype(bf16)
+    dstep_ref[...] = dstep.T[: dstep_ref.shape[0]].astype(bf16)
     dhead_ref[0:1] += jnp.sum(dstep, axis=0, keepdims=True)
     dhead_ref[1:2] += jnp.sum(decay_log * ddecay, axis=0, keepdims=True)
 
@@ -373,14 +374,14 @@
         out_specs=[
             pl.BlockSpec((CHUNK, 2 * width), at),
             pl.BlockSpec((2 * N_STATE, CHUNK), lambda i: (0, count - 1 - i)),
-            pl.BlockSpec((CHUNK, LANES), at),
+            pl.BlockSpec((STEP_ROWS, CHUNK), lambda i: (0, count - 1 - i)),
             pl.BlockSpec((8, all_w), fixed),
             pl.BlockSpec((8, LANES), fixed),
         ],
         out_shape=[
             jax.ShapeDtypeStruct((length, 2 * width), bf16),
             jax.ShapeDtypeStruct((2 * N_STATE, length), bf16),
-            jax.ShapeDtypeStruct((length, LANES), bf16),
+            jax.ShapeDtypeStruct((STEP_ROWS, length), bf16),
             jax.ShapeDtypeStruct((8, all_w), f32),
             jax.ShapeDtypeStruct((8, LANES), f32),
         ],
@@ -414,8 +415,8 @@
     )
 
 
-def weights_kernel(n_seq, n_wsh, main, small, outw, w_main, w_small, w_out, *sems):
-    send_a, recv_a, send_b, recv_b, send_c, recv_c, send_d, recv_d, send_e, recv_e, own = sems
+def weights_kernel(n_seq, n_wsh, main, small, w_main, w_small, *sems):
+    send_a, recv_a, send_b, recv_b, send_e, recv_e, send_r, recv_r, send_l, recv_l, own = sems
     s = lax.axis_index("seq")
     w = lax.axis_index("wshard")
     row = [(lax.rem(s + k, n_seq), w) for k in range(1, n_seq)]
@@ -429,65 +430,75 @@
         wire(small, w_small.at[s, w], send_b.at[j], recv_b.at[j], peer)
         for j, peer in enumerate(col)
     ]
-    outs = [
-        wire(outw, w_out.at[w], send_c.at[j], recv_c.at[j], peer)
-        for j, peer in enumerate(col)
+    third = [
+        wire(w_small.at[s], w_small.at[s], send_e.at[k], recv_e.at[k], peer)
+        for k, peer in enumerate(row)
     ]
     mine = [
         pltpu.make_async_copy(main.at[s], w_main.at[s, w], own.at[0]),
         pltpu.make_async_copy(small, w_small.at[s, w], own.at[1]),
-        pltpu.make_async_copy(outw, w_out.at[w], own.at[2]),
     ]
-    for copy in mine[:2] + first + spread:
+
+    def right(t):
+        block = w_main.at[:, jnp.maximum(w - t, 0)]
+        peer = (s, jnp.minimum(w + 1, n_wsh - 1))
+        return wire(block, block, send_r.at[t], recv_r.at[t], peer)
+
+    def left(t):
+        block = w_main.at[:, jnp.minimum(w + t, n_wsh - 1)]
+        peer = (s, jnp.maximum(w - 1, 0))
+        return wire(block, block, send_l.at[t], recv_l.at[t], peer)
+
+    for copy in mine + first + spread:
         copy.start()
     mine[0].wait()
     for copy in first:
         copy.wait_recv()
-    second = [
-        wire(w_main.at[:, w], w_main.at[:, w], send_d.at[j], recv_d.at[j], peer)
-        for j, peer in enumerate(col)
-    ]
-    for copy in second:
-        copy.start()
-    mine[1].wait()
-    for copy in spread:
-        copy.wait_recv()
-    third = [
-        wire(w_small.at[s], w_small.at[s], send_e.at[k], recv_e.at[k], peer)
-        for k, peer in enumerate(row)
-    ]
-    for copy in third + [mine[2]] + outs:
-        copy.start()
-    mine[2].wait()
+    last = n_wsh - 1
+    for t in range(n_wsh):
+        if t > 0:
+            pl.when(w >= t)(lambda t=t: right(t - 1).wait_recv())
+        if t < last:
+            pl.when((w >= t) & (w < last))(lambda t=t: right(t).start())
+        if t > 0:
+            pl.when(w + t <= last)(lambda t=t: left(t - 1).wait_recv())
+        if t < last:
+            pl.when((w + t <= last) & (w > 0))(lambda t=t: left(t).start())
+        if t == 0:
+            mine[1].wait()
+            for copy in spread:
+                copy.wait_recv()
+            for copy in third:
+                copy.start()
     for copy in first + spread:
         copy.wait_send()
-    for copy in second + third + outs:
+    for copy in third:
         copy.wait()
-
-
-def spread_weights(main, small, outw, n_seq, n_wsh):
+    for t in range(last):
+        pl.when((w >= t) & (w < last))(lambda t=t: right(t).wait_send())
+        pl.when((w + t <= last) & (w > 0))(lambda t=t: left(t).wait_send())
+
+
+def spread_weights(main, small, n_seq, n_wsh):
     rows_in, cols = main.shape[1:]
     anywhere = pl.BlockSpec(memory_space=pl.ANY)
     dma = pltpu.SemaphoreType.DMA
     a, c = n_seq - 1, n_wsh - 1
     return pl.pallas_call(
         functools.partial(weights_kernel, n_seq, n_wsh),
-        in_specs=[anywhere] * 3,
-        out_specs=[anywhere] * 3,
+        in_specs=[anywhere] * 2,
+        out_specs=[anywhere] * 2,
         out_shape=[
             jax.ShapeDtypeStruct((n_seq, n_wsh, rows_in, cols), bf16),
             jax.ShapeDtypeStruct((n_seq, n_wsh) + small.shape, bf16),
-            jax.ShapeDtypeStruct((n_wsh,) + outw.shape, bf16),
-        ],
-        scratch_shapes=[
-            dma((n,)) for n in (a, a, c, c, c, c, c, c, a, a, 3)
-        ],
+        ],
+        scratch_shapes=[dma((n,)) for n in (a, a, c, c, a, a, c, c, c, c, 2)],
         compiler_params=pltpu.CompilerParams(collective_id=0, has_side_effects=True),
         cost_estimate=pl.CostEstimate(
             flops=0, bytes_accessed=200_000_000, transcendentals=0
         ),
         name="spread_weights",
-    )(main, small, outw)
+    )(main, small)
 
 
 def swap_kernel(plan, n_seq, n_wsh, *refs):
@@ -690,22 +701,35 @@
     main_send = jnp.swapaxes(main_send, 0, 1)
     small_send = in_w16[:, 2 * inner_all :]
     small_send = jnp.pad(small_send, ((0, 0), (0, -small_send.shape[1] % LANES)))
-    w_main, w_small, w_out = spread_weights(
-        main_send, small_send, out_weight.astype(bf16), n_seq, n_wsh
-    )
+    w_main, w_small = spread_weights(main_send, small_send, n_seq, n_wsh)
+    out_w16, w_main = lax.optimization_barrier((out_weight.astype(bf16), w_main))
     w_main = w_main.reshape(width_in, 2 * width)
     w_small = w_small.reshape(width_in, small_send.shape[1])
+    w_out = jnp.zeros((n_wsh,) + out_w16.shape, bf16)
+    w_out = lax.dynamic_update_index_in_dim(w_out, out_w16, wsh_index, 0)
+    for j in range(1, n_wsh):
+        got = lax.ppermute(out_w16, "wshard", [(i, (i + j) % n_wsh) for i in range(n_wsh)])
+        w_out = lax.dynamic_update_index_in_dim(
+            w_out, got, lax.rem(wsh_index - j + n_wsh, n_wsh), 0
+        )
     w_out = w_out.reshape(width, width_in)
-    w_shared = w_small[:, : 2 * N_STATE]
-    w_step = lax.dynamic_slice_in_dim(w_small, 2 * N_STATE + seq_index * heads, heads, 1)
-    w_share = lax.dynamic_slice_in_dim(w_small, seq_index * share, share, 1)
-    w_ext = jnp.pad(
-        jnp.concatenate([w_share, w_step], axis=1), ((0, 0), (0, LANES - share - heads))
-    )
-    w_step = jnp.pad(w_step, ((0, 0), (0, LANES - heads)))
+
+    def pick(first, count, width_to):
+        col = lax.broadcasted_iota(jnp.int32, (w_small.shape[1], width_to), 0)
+        lane = lax.broadcasted_iota(jnp.int32, (w_small.shape[1], width_to), 1)
+        return jnp.where((col == lane + first) & (lane < count), 1.0, 0.0)
+
+    first_step = 2 * N_STATE + seq_index * heads
+    to_step = pick(first_step, heads, LANES)
+    to_fwd = jnp.concatenate([pick(0, 2 * N_STATE, 2 * N_STATE), to_step], axis=1)
+    to_ext = jnp.concatenate(
+        [pick(seq_index * share, share, share), to_step[:, :STEP_ROWS]], axis=1
+    )
+    w_fwd = mm(w_small, to_fwd.astype(bf16), NN).astype(bf16)
+    w_ext = mm(w_small, to_ext.astype(bf16), NN).astype(bf16)
 
     main = mm(normed_all, w_main, NN).astype(bf16)
-    small = mm(normed_all, jnp.concatenate([w_shared, w_step], axis=1), NN).astype(bf16)
+    small = mm(normed_all, w_fwd, NN).astype(bf16)
     head_local = lax.dynamic_slice_in_dim(head_params, seq_index * heads, heads, 1)
     head = jnp.pad(head_local, ((0, 5), (0, LANES - heads)))
     conv_local = lax.dynamic_slice_in_dim(conv_inner, seq_index * width, width, 1)
@@ -726,6 +750,10 @@
     d_out_gain = jnp.sum(d_gnormed * gated32 * rms_out, axis=0)
 
     g_out = mm(gnormed, cot_all, TN)
+    mixed = mm(gnormed, w_out, NN).astype(bf16)
+    g_out, mixed, d_gated = lax.optimization_barrier((g_out, mixed, d_gated))
+    mixed = lax.psum_scatter(mixed, "seq", scatter_dimension=0, tiled=True)
+    block_out = (inputs + mixed.astype(f32))[None]
     grad_out_weight = lax.dynamic_slice_in_dim(g_out, wsh_index * rows_out, rows_out, 0)
     for j in range(1, n_wsh):
         to = lax.rem(wsh_index + j, n_wsh)
@@ -733,11 +761,7 @@
         grad_out_weight = grad_out_weight + lax.ppermute(
             part, "wshard", [(i, (i + j) % n_wsh) for i in range(n_wsh)]
         )
-    mixed = lax.psum_scatter(
-        mm(gnormed, w_out, NN).astype(bf16), "seq", scatter_dimension=0, tiled=True
-    )
-    block_out = (inputs + mixed.astype(f32))[None]
-    dmain, dshared_t, dstep, dtaps, dhead = mixer_backward(
+    dmain, dshared_t, dstep_t, dtaps, dhead = mixer_backward(
         main, small, head, taps, y, states, d_gated, heads
     )
 
@@ -745,22 +769,39 @@
         (dshared_t.reshape(n_seq, share, -1),), ((0, "seq"),), n_seq, n_wsh, 2, "swap_shared"
     )
     shared_sum = jnp.sum(shared_parts.astype(f32), axis=0).astype(bf16)
-    d_ext = jnp.pad(
-        jnp.concatenate([shared_sum.T, dstep[:, :heads]], axis=1),
-        ((0, 0), (0, LANES - share - heads)),
-    )
-    d_normed = mm(dmain, w_main, NT) + mm(d_ext, w_ext, NT)
+    d_ext = jnp.concatenate([shared_sum, dstep_t], axis=0)
+    d_normed = mm(dmain, w_main, NT) + lax.dot_general(
+        d_ext, w_ext, (((0,), (1,)), ((), ())), preferred_element_type=f32
+    )
     d_normed = lax.psum_scatter(
         d_normed.astype(bf16), "seq", scatter_dimension=0, tiled=True
     ).astype(f32)
 
     g_main = mm(normed_all, dmain, TN).astype(bf16).reshape(n_seq, n_wsh, rows_in, 2 * width)
-    g_ext = mm(normed_all, d_ext, TN).astype(bf16).reshape(n_seq, n_wsh, rows_in, LANES)
-    g_main, g_ext = swap(
-        (g_main, g_ext), ((1, "wshard"), (1, "wshard")), n_seq, n_wsh, 3, "swap_grads"
+    g_ext = lax.dot_general(
+        normed_all, d_ext, (((0,), (1,)), ((), ())), preferred_element_type=f32
+    ).astype(bf16)
+    g_ext = jnp.pad(g_ext, ((0, 0), (0, -g_ext.shape[1] % LANES)))
+    g_ext = g_ext.reshape(n_seq, n_wsh, rows_in, LANES)
+
+    def pack(parts):
+        flat = jnp.concatenate([p.reshape(-1) for p in parts])
+        return jnp.pad(flat, (0, -flat.shape[0] % (8 * LANES))).reshape(-1, LANES)
+
+    d_skip = dtaps[5, 2 * N_STATE :].reshape(heads, P_SIZE).sum(-1)
+    d_head = jnp.concatenate([dhead[:2, :heads], d_skip[None]], axis=0)
+    pieces = (dtaps[:5, : 2 * N_STATE], d_out_gain, dtaps[:5, 2 * N_STATE :], d_head)
+    g_main, g_ext, flat = swap(
+        (g_main, g_ext, pack(pieces)),
+        ((1, "wshard"), (1, "wshard"), ("all", "wshard")),
+        n_seq,
+        n_wsh,
+        3,
+        "swap_grads",
     )
     g_main = jnp.sum(g_main.astype(f32), axis=0).astype(bf16)
     g_ext = jnp.sum(g_ext.astype(f32), axis=0).astype(bf16)
+    flat = jnp.sum(flat, axis=0)
 
     d_in_gain = jnp.sum(d_normed * inputs * rms_in, axis=0)
     scaled_in = d_normed * in_gain
@@ -770,20 +811,9 @@
         - inputs * rms_in**3 * jnp.mean(scaled_in * inputs, axis=-1, keepdims=True)
     )[None]
 
-    d_skip = dtaps[5, 2 * N_STATE :].reshape(heads, P_SIZE).sum(-1)
-    d_head = jnp.concatenate([dhead[:2, :heads], d_skip[None]], axis=0)
-    pieces = (
-        d_in_gain,
-        dtaps[:5, : 2 * N_STATE],
-        d_out_gain,
-        dtaps[:5, 2 * N_STATE :],
-        d_head,
-    )
-    flat = jnp.concatenate([p.reshape(-1) for p in pieces])
-    flat = jnp.pad(flat, (0, -flat.shape[0] % (8 * LANES))).reshape(-1, LANES)
-    g_main, g_ext, flat = swap(
-        (g_main, g_ext, flat),
-        ((0, "seq"), (0, "seq"), ("all", "both")),
+    g_main, g_ext, flat, in_gain_parts = swap(
+        (g_main, g_ext, flat, pack((d_in_gain,))),
+        ((0, "seq"), (0, "seq"), ("all", "seq"), ("all", "both")),
         n_seq,
         n_wsh,
         4,
@@ -799,16 +829,16 @@
         ],
         axis=1,
     ).astype(f32)
-    flat = jnp.sum(flat.reshape(n_seq, n_wsh, -1), axis=1)
+    grad_in_gain = jnp.sum(in_gain_parts, axis=0).reshape(-1)[:width_in]
+    flat = flat.reshape(n_seq, -1)
     sums, at = [], 0
     for p in pieces:
         sums.append(flat[:, at : at + p.size].reshape((n_seq,) + p.shape))
         at += p.size
-    grad_in_gain = jnp.sum(sums[0], axis=0)
-    grad_conv_shared = jnp.sum(sums[1], axis=0)
-    grad_out_gain = sums[2].reshape(-1)
-    grad_conv_inner = jnp.swapaxes(sums[3], 0, 1).reshape(conv_inner.shape)
-    grad_head_params = jnp.swapaxes(sums[4], 0, 1).reshape(head_params.shape)
+    grad_conv_shared = jnp.sum(sums[0], axis=0)
+    grad_out_gain = sums[1].reshape(-1)
+    grad_conv_inner = jnp.swapaxes(sums[2], 0, 1).reshape(conv_inner.shape)
+    grad_head_params = jnp.swapaxes(sums[3], 0, 1).reshape(head_params.shape)
     new_in_weight, new_first_in_weight, new_second_in_weight = adamw(
         in_weight,
         grad_in_weight,

time: 448 us -> 438 us (0.978)
  Pallas kernels: 294 us -> 260 us
  waiting for transfers between devices: 0.78 us -> 19.7 us
  matrix products: 62.6 us -> 73.2 us
  local copies, waits for them, and re-layouts: 28.1 us -> 19.3 us
    pallas_call x1, Pallas kernels: 86.8 us -> 58 us  [spread_weights(): pl.pallas_call(functools.partial(weights_kernel, n_seq, n_wsh), in_specs=...]
    ppermute x0 -> x3, waiting for transfers between devices: none -> 18.4 us  [local(): lax.ppermute(out_w16, 'wshard', [(i, (i + j) % n_wsh) for i in range(n_ws...]
    dot_general x0 -> x2, matrix products: none -> 11.9 us  [the longest x1 7.95 us: local(): lax.dot_general(d_ext, w_ext, (((0,), (1,)), ((), ())), preferred_element...]
    dot_general x9 -> x7, matrix products: 62.6 us -> 61.3 us  [mm(): return lax.dot_general(a, b, dims, preferred_element_type=f32)]
  transfers between devices with their start and end apart: 7 -> 10, of which waited for: 0 -> 2; matrix products, arithmetic and copies ran while one was open for 20% -> 17% of each run, Pallas kernels for 50% -> 44%
where the time goes in v2:
time: 438 us; the launch traced here: 437 us
  Pallas kernels  260 us (59%)
  matrix products  73.2 us (17%)
  other arithmetic  39.3 us (9%)
  waiting for transfers between devices  19.7 us (4%)
  local copies, waits for them, and re-layouts  19.3 us (4%)
  between operations  14.3 us (3%)
  starting transfers between devices  10.5 us (2%)
    pallas_call x3, Pallas kernels, swap(): pl.pallas_call(functools.partial(swap_kernel, plan, n_seq, n_wsh), in_spe...  128 us
    dot_general x7, matrix products, mm(): return lax.dot_general(a, b, dims, preferred_element_type=f32)  61.3 us
    pallas_call x1, Pallas kernels, spread_weights(): pl.pallas_call(functools.partial(weights_kernel, n_seq, n_wsh), in_specs=...  58 us
    pallas_call x1, Pallas kernels, mixer_backward(): pl.pallas_call(functools.partial(bwd_kernel, heads, count), grid=(count,)...  46.6 us
    pallas_call x1, Pallas kernels, mixer_forward(): pl.pallas_call(functools.partial(fwd_kernel, heads), grid=(count,), in_sp...  20.3 us
    ppermute x3, waiting for transfers between devices, local(): lax.ppermute(out_w16, 'wshard', [(i, (i + j) % n_wsh) for i in range(n_ws...  18.4 us
    sub x7, other arithmetic, adamw(): return (param - rate * (corrected + decay * param), first_new, second_new)  14.2 us
  transfers between devices with their start and end apart: 10, of which 2 were waited for; matrix products, arithmetic and copies ran while one was open for 17% of the time, Pallas kernels for 44%

profile of v2, /device:TPU:0, one launch (start us, length us, event | category | flops | bytes accessed | tf_op | source)
XLA Modules:
  0.0 436.7 jit_solution(13869689515522761527)
XLA Ops:
  7.2 1.4 fusion.17
  8.6 0.6 multiply_multiply_fusion.8
  9.2 2.4 fusion.19
  11.7 0.7 all-gather.6.cloned.1.call-update
  12.6 0.9 copy-done.3
  13.5 0.9 copy.90
  14.3 0.6 pad.24.small
  14.9 58.0 %spread_weights.1 = (bf16[8,4,48,768]{3,2,1,0:T(8,128)(2,1)}, bf16[8,4,48,384]{3,2,1,0:T(8,128)(2,1)}) custom-call(bf16[8,48,768]{2,1,0:T(8,128)(2,1)} %bitcast.99, bf16[48,384]{1,0:T(8,128)(2,1)} %pad.24.small), custom_call_target="tpu_custom_call" | custom-call | bytes 200000000 | tf_op jit(solution)/shard_map/spread_weights/pallas_call | solution.py:487
  72.9 3.3 collective-permute-start.2
  76.3 0.6 collective-permute-start
  77.2 0.8 dynamic_slice.23
  78.7 0.7 constant_dynamic-slice_fusion.3
  79.4 0.6 select_maximum_fusion.taps_ref
  80.1 1.1 broadcast_in_dim.61
  81.2 0.7 bitcast_dynamic-update-slice_fusion.3
  82.0 14.7 %collective-permute-done = bf16[96,1536]{1,0:T(8,128)(2,1)S(1)} collective-permute-done((bf16[96,1536]{1,0:T(8,128)(2,1)S(1)}, bf16[96,1536]{1,0:T(8,128)(2,1)S(1)}, u32[]{:S(2)}, u32[]{:S(2)}) %collective-permute-start) | collective-permute-done | bytes 294944 | tf_op jit(solution)/shard_map/ppermute | solution.py:711
  96.7 0.7 bitcast_dynamic-update-slice_fusion.2
  97.4 3.7 collective-permute-done.1
  101.1 0.7 bitcast_dynamic-update-slice_fusion.1
  101.8 0.7 bitcast_dynamic-update-slice_fusion
  102.6 8.4 %convolution_convert_fusion.3.small_ref.small_prev = bf16[2048,384]{1,0:T(8,128)(2,1)} fusion(bf16[2048,1536]{1,0:T(8,128)(2,1)} %all-gather.4.cloned.1.call-done, bf16[1536,384]{1,0:T(8,128)(2,1)} %bitcast.102, bf16[384,128]{1,0:T(8,128)(2,1)S(1)} %copy.74, bf16[384,256]{1,0:T(8,128)(2,1)S(1)} %select_convert_fusion), kind=kOutput, calls=%fused_computation.29 | convolution fusion | flops 2870870016 | bytes 9338880 | tf_op jit(solution)/shard_map/dot_general | solution.py:33
  111.0 9.0 %convolution_convert_fusion.2.main_ref.main_prev = bf16[2048,768]{1,0:T(8,128)(2,1)} fusion(bf16[2048,1536]{1,0:T(8,128)(2,1)} %all-gather.4.cloned.1.call-done, bf16[1536,768]{1,0:T(8,128)(2,1)} %bitcast.120), kind=kOutput, calls=%fused_computation.18 | convolution fusion | flops 4833411072 | bytes 11796480 | tf_op jit(solution)/shard_map/dot_general | solution.py:33
  120.0 20.3 %mixer_forward.1 = (bf16[2048,384]{1,0:T(8,128)(2,1)}, f32[2048,384]{1,0:T(8,128)}, f32[16,128,384]{2,1,0:T(8,128)}) custom-call(bf16[2048,768]{1,0:T(8,128)(2,1)} %convolution_convert_fusion.2.main_ref.main_prev, bf16[2048,384]{1,0:T(8,128)(2,1)} %convolution_convert_fusion.3.small_ref.small_prev, f32[8,128]{1,0:T(8,128)} %pad.25.head_ref, ...), custom_call_target="tpu_custom_call" | custom-call | tf_op jit(solution)/shard_map/mixer_forward/pallas_call | solution.py:190
  140.3 8.7 %fusion.4 = (f32[2048]{0:T(1024)S(1)}, f32[2048]{0:T(1024)S(1)}, f32[384,2048]{0,1:T(8,128)}) fusion(bf16[2048,384]{1,0:T(8,128)(2,1)} %get-tuple-element.56, f32[384]{0:T(512)S(1)} %dynamic_slice.23, bf16[384,1536]{1,0:T(8,128)(2,1)} %bitcast.10, bf16[1,2048,1536]{2,1,0:T(8,128)(2,1)} %all-gather.6.cloned.1.call-done), kind=kOutput, calls=%fused_computation.19 | convolution fusion | flops 2420633600 | bytes 12207616 | tf_op jit(solution)/shard_map/dot_general | solution.py:33
  149.0 0.6 reshape.189.x_ref
  149.6 7.3 %sum_over_seq.1 = f32[32,128]{1,0:T(8,128)} custom-call(f32[32,128]{1,0:T(8,128)} %reshape.189.x_ref), custom_call_target="tpu_custom_call" | custom-call | tf_op jit(solution)/shard_map/sum_over_seq/pallas_call | solution.py:630
  157.0 0.7 multiply_multiply_fusion.6
  157.7 0.7 multiply_bitcast_fusion
  158.4 7.9 %convolution_convert_fusion = bf16[2048,1536]{1,0:T(8,128)(2,1)} fusion(bf16[384,1536]{1,0:T(8,128)(2,1)} %bitcast.10, bf16[2048,384]{1,0:T(8,128)(2,1)} %get-tuple-element.56, f32[2048]{0:T(1024)S(1)} %get-tuple-element.111, f32[384]{0:T(512)S(1)} %dynamic_slice.23), kind=kOutput, calls=%fused_computation.1 | convolution fusion | flops 2422210560 | bytes 9053696 | tf_op jit(solution)/shard_map/dot_general | solution.py:33
  166.3 4.0 fusion.12
  170.3 6.9 %fusion = f32[384,1536]{1,0:T(8,128)} fusion(bf16[1,2048,1536]{2,1,0:T(8,128)(2,1)} %all-gather.6.cloned.1.call-done, bf16[2048,384]{1,0:T(8,128)(2,1)S(1)} %copy-done.4, f32[2048]{0:T(1024)S(1)} %get-tuple-element.111, f32[384]{0:T(512)S(1)} %dynamic_slice.23), kind=kOutput, calls=%fused_computation.2 | convolution fusion | flops 2419064832 | bytes 10233344 | tf_op jit(solution)/shard_map/dot_general | solution.py:33
  177.2 46.6 %mixer_backward.1 = (bf16[2048,768]{1,0:T(8,128)(2,1)}, bf16[256,2048]{1,0:T(8,128)(2,1)}, bf16[16,2048]{1,0:T(8,128)(2,1)}, f32[8,640]{1,0:T(8,128)}, f32[8,128]{1,0:T(8,128)}) custom-call(bf16[2048,768]{1,0:T(8,128)(2,1)} %convolution_convert_fusion.2.main_ref.main_prev, bf16[2048,384]{1,0:T(8,128)(2,1)} %convolution_convert_fusion.3.small_ref.small_prev, ...), custom_call_target="tpu_custom_call" | custom-call | tf_op jit(solution)/shard_map/mixer_backward/pallas_call | solution.py:360
  223.9 13.9 %swap_shared.1 = bf16[8,32,2048]{2,1,0:T(8,128)(2,1)} custom-call(bf16[8,32,2048]{2,1,0:T(8,128)(2,1)} %bitcast.104), custom_call_target="tpu_custom_call" | custom-call | tf_op jit(solution)/shard_map/swap_shared/pallas_call | solution.py:594
  237.8 1.4 reduce_sum.131
  239.2 10.2 %fusion.62 = f32[2048,1536]{1,0:T(8,128)} fusion(bf16[2048,768]{1,0:T(8,128)(2,1)} %get-tuple-element.62, bf16[1536,768]{1,0:T(8,128)(2,1)} %bitcast.121), kind=kOutput, calls=%fused_computation.131 | convolution fusion | flops 4831838208 | bytes 18087936 | tf_op jit(solution)/shard_map/dot_general | solution.py:33
  249.4 7.9 %add_convert_fusion = bf16[2048,1536]{1,0:T(8,128)(2,1)} fusion(f32[2048,1536]{1,0:T(8,128)} %fusion.62, bf16[1536,384]{1,0:T(8,128)(2,1)} %bitcast.103, bf16[16,2048]{1,0:T(8,128)(2,1)S(1)} %copy-done.10, bf16[32,2048]{1,0:T(8,128)(2,1)S(1)} %reduce_sum.131, bf16[384,16]{0,1:T(8,128)(2,1)S(1)} %slice-done, bf16[384,32]{0,1:T(8,128)(2,1)S(1)} %select_convert_fusion.2), kind=kOutput, calls=%fused_computation | convolution fusion | flops 365445120 | bytes 20287488 | tf_op jit(solution)/shard_map/dot_general | solution.py:773
  257.9 0.7 slice.67
  258.9 2.8 constant_dynamic-slice_fusion.2
  261.7 2.3 collective-permute-start.3
  264.0 1.5 collective-permute-start.5
  265.5 2.6 collective-permute-start.4
  268.1 10.2 %convolution_convert_fusion.1 = bf16[1536,768]{1,0:T(8,128)(2,1)} fusion(bf16[2048,1536]{1,0:T(8,128)(2,1)} %all-gather.4.cloned.1.call-done, bf16[2048,768]{1,0:T(8,128)(2,1)S(1)} %copy-done.27), kind=kOutput, calls=%fused_computation.17 | convolution fusion | flops 4833017856 | bytes 11796480 | tf_op jit(solution)/shard_map/dot_general | solution.py:33
  278.4 3.9 convolution_convert_fusion.5
  282.5 0.8 pad.27.clone
  283.4 0.6 fusion.45.refs_2_
  284.0 94.2 %swap_grads.1 = (bf16[4,8,48,768]{3,2,1,0:T(8,128)(2,1)}, bf16[4,8,48,128]{3,2,1,0:T(8,128)(2,1)}, f32[4,32,128]{2,1,0:T(8,128)}) custom-call(bf16[8,4,48,768]{3,2,1,0:T(8,128)(2,1)} %bitcast.98, bf16[8,4,48,128]{3,2,1,0:T(8,128)(2,1)} %bitcast.101, f32[32,128]{1,0:T(8,128)} %fusion.45.refs_2_), custom_call_target="tpu_custom_call" | custom-call | tf_op jit(solution)/shard_map/swap_grads/pallas_call | solution.py:594
  378.2 3.1 reduce_sum.135.refs_0_
  381.3 0.7 reduce_sum.136.refs_1_
  382.0 0.6 reduce_sum.137.refs_2_
  382.7 3.6 multiply_subtract_fusion.1
  386.3 2.2 fusion.24
  389.1 20.1 %swap_last.1 = (bf16[8,48,768]{2,1,0:T(8,128)(2,1)}, bf16[8,48,128]{2,1,0:T(8,128)(2,1)}, f32[8,32,128]{2,1,0:T(8,128)}, f32[32,16,128]{2,1,0:T(8,128)}) custom-call(bf16[8,48,768]{2,1,0:T(8,128)(2,1)} %reduce_sum.135.refs_0_, bf16[8,48,128]{2,1,0:T(8,128)(2,1)} %reduce_sum.136.refs_1_, f32[32,128]{1,0:T(8,128)} %reduce_sum.137.refs_2_, ...), custom_call_target="tpu_custom_call" | custom-call | tf_op jit(solution)/shard_map/swap_last/pallas_call | solution.py:594
  409.2 1.0 copy.91
  410.3 1.1 copy.85
  411.4 0.6 reduce_sum.139
  412.4 0.7 copy.80
  413.4 0.6 multiply_subtract_fusion.6
  414.6 1.3 broadcast_multiply_fusion
  416.4 1.3 multiply_subtract_fusion.4
  417.7 1.4 multiply_subtract_fusion.5
  419.1 1.4 multiply_subtract_fusion.3
  420.5 1.6 multiply_subtract_fusion.2
  422.1 4.3 multiply_subtract_fusion
  426.5 3.7 fusion.16
  (117 shorter events, 4.9 us)
Async XLA Ops:
  7.2 95.4 %all-gather.4.cloned.1.call-start = ((), (), s32[]{:S(2)}) async-start(), calls=%async_computation.2 | async-start | bytes 7077888 | tf_op jit(solution)/shard_map/all_gather | solution.py:696
  9.2 377.0 %copy-start.20 = (f32[256]{0:T(256)}, f32[256]{0:T(256)S(1)}, u32[]{:S(2)}) copy-start(f32[256]{0:T(256)S(1)} %get-tuple-element.113) | copy-start | bytes 3076
  9.2 3.2 copy-start.1
  11.6 128.7 %all-gather.6.cloned.1.call-start = ((), (), s32[]{:S(2)}) async-start(), calls=%async_computation.5 | async-start | bytes 7077888 | tf_op jit(solution)/shard_map/all_gather | solution.py:698
  12.4 1.1 copy-start.3
  12.4 373.9 %reduce-scatter.5.cloned.1.call-start = ((), (), s32[]{:S(2)}) async-start(), calls=%async_computation.4 | async-start | bytes 7077888 | tf_op jit(solution)/shard_map/reduce_scatter | solution.py:776
  13.4 64.6 %copy-start.23 = (f32[3,48]{1,0:T(4,128)S(1)}, f32[3,48]{1,0:T(4,128)}, u32[]{:S(2)}) copy-start(f32[3,48]{1,0:T(4,128)} %param.31) | copy-start | bytes 1732
  13.4 65.9 %copy-start.17 = (f32[5,256]{1,0:T(8,128)S(1)}, f32[5,256]{1,0:T(8,128)}, u32[]{:S(2)}) copy-start(f32[5,256]{1,0:T(8,128)} %param.30) | copy-start | bytes 15364
  72.9 28.9 %collective-permute-start.2 = (bf16[96,1536]{1,0:T(8,128)(2,1)S(1)}, bf16[96,1536]{1,0:T(8,128)(2,1)S(1)}, u32[]{:S(2)}, u32[]{:S(2)}) collective-permute-start(bf16[96,1536]{1,0:T(8,128)(2,1)S(1)} %convert_element_type.83), channel_id=1, source_target_pairs={{0,3},{1,0},{2,1},{3,2},{4,7},{5,4},{6,5},{7,6},{8,11},{9,8},{10,9... | collective-permute-start | bytes 884744 | tf_op jit(solution)/shard_map/ppermute | solution.py:711
  76.3 24.8 %collective-permute-start.1 = (bf16[96,1536]{1,0:T(8,128)(2,1)S(1)}, bf16[96,1536]{1,0:T(8,128)(2,1)S(1)}, u32[]{:S(2)}, u32[]{:S(2)}) collective-permute-start(bf16[96,1536]{1,0:T(8,128)(2,1)S(1)} %convert_element_type.83), channel_id=1, source_target_pairs={{0,2},{1,3},{2,0},{3,1},{4,6},{5,7},{6,4},{7,5},{8,10},{9,11},{10,... | collective-permute-start | bytes 884744 | tf_op jit(solution)/shard_map/ppermute | solution.py:711
  76.3 20.4 %collective-permute-start = (bf16[96,1536]{1,0:T(8,128)(2,1)S(1)}, bf16[96,1536]{1,0:T(8,128)(2,1)S(1)}, u32[]{:S(2)}, u32[]{:S(2)}) collective-permute-start(bf16[96,1536]{1,0:T(8,128)(2,1)S(1)} %convert_element_type.83), channel_id=1, source_target_pairs={{0,1},{1,2},{2,3},{3,0},{4,5},{5,6},{6,7},{7,4},{8,9},{9,10},{10,1... | collective-permute-start | bytes 884744 | tf_op jit(solution)/shard_map/ppermute | solution.py:711
  77.0 24.8 %copy-start.6 = (bf16[384,128]{0,1:T(8,128)(2,1)}, bf16[384,128]{0,1:T(8,128)(2,1)S(1)}, u32[]{:S(2)}) copy-start(bf16[384,128]{0,1:T(8,128)(2,1)S(1)} %select_convert_fusion.1) | copy-start | bytes 294916
  166.3 4.0 copy-start.4
  239.1 10.2 %slice-start = ((bf16[384,128]{0,1:T(8,128)(2,1)}), bf16[384,16]{0,1:T(8,128)(2,1)S(1)}, s32[]{:S(2)}) async-start(bf16[384,128]{0,1:T(8,128)(2,1)} %copy-done.6), calls=%async_computation.6 | async-start | bytes 24576 | tf_op jit(solution)/shard_map/slice | solution.py:726
  239.2 10.2 %copy-start.10 = (bf16[16,2048]{1,0:T(8,128)(2,1)S(1)}, bf16[16,2048]{1,0:T(8,128)(2,1)}, u32[]{:S(2)}) copy-start(bf16[16,2048]{1,0:T(8,128)(2,1)} %get-tuple-element.64) | copy-start | bytes 196612
  257.3 1.3 copy-start.19
  257.3 169.1 %reduce-scatter.3.cloned.1.call-start = ((), (), s32[]{:S(2)}) async-start(), calls=%async_computation.3 | async-start | bytes 7077888 | tf_op jit(solution)/shard_map/reduce_scatter | solution.py:755
  258.9 9.2 %copy-start.27 = (bf16[2048,768]{1,0:T(8,128)(2,1)S(1)}, bf16[2048,768]{1,0:T(8,128)(2,1)}, u32[]{:S(2)}) copy-start(bf16[2048,768]{1,0:T(8,128)(2,1)} %get-tuple-element.62) | copy-start | bytes 9437188
  261.7 121.0 %collective-permute-start.3 = (f32[96,1536]{1,0:T(8,128)}, f32[96,1536]{1,0:T(8,128)}, u32[]{:S(2)}, u32[]{:S(2)}) collective-permute-start(f32[96,1536]{1,0:T(8,128)} %get-tuple-element.105), channel_id=1, source_target_pairs={{0,1},{1,2},{2,3},{3,0},{4,5},{5,6},{6,7},{7,4},{8,9},{9,10},{10,1... | collective-permute-start | bytes 1769480 | tf_op jit(solution)/shard_map/ppermute | solution.py:761
  264.0 118.6 %collective-permute-start.5 = (f32[96,1536]{1,0:T(8,128)}, f32[96,1536]{1,0:T(8,128)}, u32[]{:S(2)}, u32[]{:S(2)}) collective-permute-start(f32[96,1536]{1,0:T(8,128)} %get-tuple-element.106), channel_id=1, source_target_pairs={{0,3},{1,0},{2,1},{3,2},{4,7},{5,4},{6,5},{7,6},{8,11},{9,8},{10,9... | collective-permute-start | bytes 1769480 | tf_op jit(solution)/shard_map/ppermute | solution.py:761
  265.5 117.1 %collective-permute-start.4 = (f32[96,1536]{1,0:T(8,128)}, f32[96,1536]{1,0:T(8,128)}, u32[]{:S(2)}, u32[]{:S(2)}) collective-permute-start(f32[96,1536]{1,0:T(8,128)} %get-tuple-element.107), channel_id=1, source_target_pairs={{0,2},{1,3},{2,0},{3,1},{4,6},{5,7},{6,4},{7,5},{8,10},{9,11},{10,... | collective-permute-start | bytes 1769480 | tf_op jit(solution)/shard_map/ppermute | solution.py:761
  378.2 3.1 copy-start.7
  378.2 3.8 copy-start.15
  378.2 4.4 %copy-start.5 = (f32[96,1536]{1,0:T(8,128)S(1)}, f32[96,1536]{1,0:T(8,128)}, u32[]{:S(2)}) copy-start(f32[96,1536]{1,0:T(8,128)} %param.33) | copy-start | bytes 1769476
  382.6 3.6 copy-start
  382.6 3.6 copy-start.12
  389.0 24.3 %copy-start.25 = (f32[3,48]{1,0:T(4,128)S(1)}, f32[3,48]{1,0:T(4,128)}, u32[]{:S(2)}) copy-start(f32[3,48]{1,0:T(4,128)} %param.38) | copy-start | bytes 1732
  389.0 24.3 %copy-start.26 = (f32[3,48]{1,0:T(4,128)S(1)}, f32[3,48]{1,0:T(4,128)}, u32[]{:S(2)}) copy-start(f32[3,48]{1,0:T(4,128)} %param.45) | copy-start | bytes 1732
  409.2 2.2 copy-start.11
  409.2 2.9 copy-start.8
  409.2 11.3 %copy-start.13 = (f32[5,3072]{1,0:T(8,128)S(1)}, f32[5,3072]{1,0:T(8,128)}, u32[]{:S(2)}) copy-start(f32[5,3072]{1,0:T(8,128)} %param.29) | copy-start | bytes 184324
  409.2 11.3 %copy-start.14 = (f32[5,3072]{1,0:T(8,128)S(1)}, f32[5,3072]{1,0:T(8,128)}, u32[]{:S(2)}) copy-start(f32[5,3072]{1,0:T(8,128)} %param.36) | copy-start | bytes 184324
  413.2 8.9 %copy-start.18 = (f32[5,256]{1,0:T(8,128)}, f32[5,256]{1,0:T(8,128)S(1)}, u32[]{:S(2)}) copy-start(f32[5,256]{1,0:T(8,128)S(1)} %reduce_sum.141) | copy-start | bytes 15364
  413.4 0.6 copy-start.22
  414.5 7.6 %copy-start.16 = (f32[3072]{0:T(1024)}, f32[3072]{0:T(1024)S(1)}, u32[]{:S(2)}) copy-start(f32[3072]{0:T(1024)S(1)} %reshape.202) | copy-start | bytes 36868
  414.6 11.9 %copy-start.9 = (f32[1,5,8,384]{3,1,2,0:T(8,128)}, f32[1,5,8,384]{3,1,2,0:T(8,128)S(1)}, u32[]{:S(2)}) copy-start(f32[1,5,8,384]{3,1,2,0:T(8,128)S(1)} %copy.87) | copy-start | bytes 184324
  422.1 4.3 copy-start.2
  422.1 4.3 copy-start.21
  422.1 4.3 copy-start.24
Sparse Core Ops, SparseCore 0:
  11.7 61.2 all-gather.3
  74.9 45.3 all-gather.5
  257.4 64.1 reduce-scatter.4
  324.9 61.7 reduce-scatter.2

commit v3 on v2

--- a/solution.py
+++ b/solution.py
@@ -6,6 +6,7 @@
 from jax.experimental import pallas as pl
 from jax.experimental.pallas import tpu as pltpu
 from jax.sharding import PartitionSpec as P
+
 
 P_SIZE = 64
 N_STATE = 128
@@ -21,6 +22,7 @@
 weight_learning_rate = 0.01
 matrix_decay = 0.1
 small_rate = 0.1
+
 
 f32 = jnp.float32
 bf16 = jnp.bfloat16
@@ -210,6 +212,9 @@
             pltpu.VMEM((N_STATE, width), f32),
             pltpu.VMEM((CHUNK + 8, all_w), f32),
         ],
+        cost_estimate=pl.CostEstimate(
+            flops=0, bytes_accessed=70_000_000, transcendentals=0
+        ),
         name="mixer_forward",
     )(main, small, head, taps)
 
@@ -390,6 +395,9 @@
             pltpu.VMEM((CHUNK + 8, all_w), f32),
             pltpu.VMEM((CHUNK + 8, all_w), f32),
         ],
+        cost_estimate=pl.CostEstimate(
+            flops=0, bytes_accessed=160_000_000, transcendentals=0
+        ),
         name="mixer_backward",
     )(main, small, main, small, head, taps, y, states, dgated)
 
@@ -574,7 +582,7 @@
         lax.fori_loop(1, size[axis], finish, 0)
 
 
-def swap(arrays, plan, n_seq, n_wsh, collective_id, name):
+def swap(arrays, plan, n_seq, n_wsh, collective_id):
     anywhere = pl.BlockSpec(memory_space=pl.ANY)
     size = {"seq": n_seq, "wshard": n_wsh, "both": n_seq * n_wsh}
     shapes, sems = [], []
@@ -600,7 +608,6 @@
         compiler_params=pltpu.CompilerParams(
             collective_id=collective_id, has_side_effects=True
         ),
-        name=name,
     )(*arrays)
 
 
@@ -651,6 +658,40 @@
         / (jnp.sqrt(second_new / (1.0 - beta_two**adam_step)) + adam_eps)
     )
     return (param - rate * (corrected + decay * param), first_new, second_new)
+
+
+def shift(x, j, n_wsh):
+    return lax.ppermute(x, "wshard", [(i, (i + j) % n_wsh) for i in range(n_wsh)])
+
+
+def adam_kernel(count, g_ref, ext_ref, p_ref, m_ref, v_ref, grad_ref, *out_refs):
+    at_ext = pl.program_id(0) == count
+    grad = jnp.where(at_ext, ext_ref[...].astype(f32), g_ref[0].astype(f32))
+    grad_ref[...] = grad
+    news = adamw(
+        p_ref[...], grad, m_ref[...], v_ref[...], weight_learning_rate, matrix_decay
+    )
+    for ref, new in zip(out_refs, news):
+        ref[...] = new
+
+
+def adam_in(g_main, g_ext, param, first, second):
+    count, rows, cols = g_main.shape
+    wide = pl.BlockSpec((rows, cols), lambda i: (0, i))
+    return pl.pallas_call(
+        functools.partial(adam_kernel, count),
+        grid=(count + 1,),
+        in_specs=[
+            pl.BlockSpec((1, rows, cols), lambda i: (jnp.minimum(i, count - 1), 0, 0)),
+            pl.BlockSpec((rows, cols), lambda i: (0, 0)),
+            wide,
+            wide,
+            wide,
+        ],
+        out_specs=[wide] * 4,
+        out_shape=[jax.ShapeDtypeStruct(param.shape, f32)] * 4,
+        name="adam_in",
+    )(g_main, g_ext, param, first, second)
 
 
 def local(
@@ -682,9 +723,9 @@
     wsh_index = lax.axis_index("wshard")
     n_seq = lax.axis_size("seq")
     n_wsh = lax.axis_size("wshard")
-    rows_in, cols_in = in_weight.shape
+    rows_in, _ = in_weight.shape
     rows_out = out_weight.shape[0]
-    tokens, width_in = block_in.shape[1:]
+    _, width_in = block_in.shape[1:]
     heads = head_params.shape[1] // n_seq
     width = heads * P_SIZE
     inner_all = out_gain.shape[0]
@@ -708,7 +749,7 @@
     w_out = jnp.zeros((n_wsh,) + out_w16.shape, bf16)
     w_out = lax.dynamic_update_index_in_dim(w_out, out_w16, wsh_index, 0)
     for j in range(1, n_wsh):
-        got = lax.ppermute(out_w16, "wshard", [(i, (i + j) % n_wsh) for i in range(n_wsh)])
+        got = shift(out_w16, j, n_wsh)
         w_out = lax.dynamic_update_index_in_dim(
             w_out, got, lax.rem(wsh_index - j + n_wsh, n_wsh), 0
         )
@@ -753,57 +794,36 @@
     mixed = mm(gnormed, w_out, NN).astype(bf16)
     g_out, mixed, d_gated = lax.optimization_barrier((g_out, mixed, d_gated))
     mixed = lax.psum_scatter(mixed, "seq", scatter_dimension=0, tiled=True)
-    block_out = (inputs + mixed.astype(f32))[None]
     grad_out_weight = lax.dynamic_slice_in_dim(g_out, wsh_index * rows_out, rows_out, 0)
     for j in range(1, n_wsh):
         to = lax.rem(wsh_index + j, n_wsh)
         part = lax.dynamic_slice_in_dim(g_out, to * rows_out, rows_out, 0)
-        grad_out_weight = grad_out_weight + lax.ppermute(
-            part, "wshard", [(i, (i + j) % n_wsh) for i in range(n_wsh)]
-        )
+        grad_out_weight = grad_out_weight + shift(part, j, n_wsh)
     dmain, dshared_t, dstep_t, dtaps, dhead = mixer_backward(
         main, small, head, taps, y, states, d_gated, heads
     )
 
+    g_main = mm(normed_all, dmain, TN)
+    d_gain_part = jnp.sum(g_main * w_main.astype(f32), axis=1)
+    g_main = g_main.astype(bf16).reshape(n_seq, n_wsh, rows_in, 2 * width)
+    g_parts = [lax.dynamic_index_in_dim(g_main, wsh_index, 1, keepdims=False)]
+    for j in range(1, n_wsh):
+        to = lax.rem(wsh_index + j, n_wsh)
+        part = lax.dynamic_index_in_dim(g_main, to, 1, keepdims=False)
+        g_parts.append(shift(part, j, n_wsh))
+
     (shared_parts,) = swap(
-        (dshared_t.reshape(n_seq, share, -1),), ((0, "seq"),), n_seq, n_wsh, 2, "swap_shared"
+        (dshared_t.reshape(n_seq, share, -1),), ((0, "seq"),), n_seq, n_wsh, 2
     )
     shared_sum = jnp.sum(shared_parts.astype(f32), axis=0).astype(bf16)
     d_ext = jnp.concatenate([shared_sum, dstep_t], axis=0)
     d_normed = mm(dmain, w_main, NT) + lax.dot_general(
         d_ext, w_ext, (((0,), (1,)), ((), ())), preferred_element_type=f32
     )
-    d_normed = lax.psum_scatter(
-        d_normed.astype(bf16), "seq", scatter_dimension=0, tiled=True
-    ).astype(f32)
-
-    g_main = mm(normed_all, dmain, TN).astype(bf16).reshape(n_seq, n_wsh, rows_in, 2 * width)
-    g_ext = lax.dot_general(
-        normed_all, d_ext, (((0,), (1,)), ((), ())), preferred_element_type=f32
-    ).astype(bf16)
-    g_ext = jnp.pad(g_ext, ((0, 0), (0, -g_ext.shape[1] % LANES)))
-    g_ext = g_ext.reshape(n_seq, n_wsh, rows_in, LANES)
-
-    def pack(parts):
-        flat = jnp.concatenate([p.reshape(-1) for p in parts])
-        return jnp.pad(flat, (0, -flat.shape[0] % (8 * LANES))).reshape(-1, LANES)
-
-    d_skip = dtaps[5, 2 * N_STATE :].reshape(heads, P_SIZE).sum(-1)
-    d_head = jnp.concatenate([dhead[:2, :heads], d_skip[None]], axis=0)
-    pieces = (dtaps[:5, : 2 * N_STATE], d_out_gain, dtaps[:5, 2 * N_STATE :], d_head)
-    g_main, g_ext, flat = swap(
-        (g_main, g_ext, pack(pieces)),
-        ((1, "wshard"), (1, "wshard"), ("all", "wshard")),
-        n_seq,
-        n_wsh,
-        3,
-        "swap_grads",
-    )
-    g_main = jnp.sum(g_main.astype(f32), axis=0).astype(bf16)
-    g_ext = jnp.sum(g_ext.astype(f32), axis=0).astype(bf16)
-    flat = jnp.sum(flat, axis=0)
-
-    d_in_gain = jnp.sum(d_normed * inputs * rms_in, axis=0)
+    d_normed, mixed = lax.optimization_barrier((d_normed.astype(bf16), mixed))
+    block_out = (inputs + mixed.astype(f32))[None]
+    d_normed = lax.psum_scatter(d_normed, "seq", scatter_dimension=0, tiled=True)
+    d_normed = d_normed.astype(f32)
     scaled_in = d_normed * in_gain
     grad_in = (
         cot.astype(f32)
@@ -811,41 +831,61 @@
         - inputs * rms_in**3 * jnp.mean(scaled_in * inputs, axis=-1, keepdims=True)
     )[None]
 
-    g_main, g_ext, flat, in_gain_parts = swap(
-        (g_main, g_ext, flat, pack((d_in_gain,))),
-        ((0, "seq"), (0, "seq"), ("all", "seq"), ("all", "both")),
-        n_seq,
-        n_wsh,
-        4,
-        "swap_last",
-    )
-    g_main = jnp.swapaxes(g_main, 0, 1).reshape(rows_in, 2 * inner_all)
-    g_ext = jnp.swapaxes(g_ext, 0, 1)
-    grad_in_weight = jnp.concatenate(
-        [
-            g_main,
-            g_ext[:, :, :share].reshape(rows_in, 2 * N_STATE),
-            g_ext[:, :, share : share + heads].reshape(rows_in, heads * n_seq),
-        ],
-        axis=1,
-    ).astype(f32)
-    grad_in_gain = jnp.sum(in_gain_parts, axis=0).reshape(-1)[:width_in]
+    g_ext = lax.dot_general(
+        normed_all, d_ext, (((0,), (1,)), ((), ())), preferred_element_type=f32
+    )
+    d_gain_part = d_gain_part + jnp.sum(g_ext * w_ext.astype(f32), axis=1)
+    g_ext = jnp.pad(g_ext.astype(bf16), ((0, 0), (0, -g_ext.shape[1] % LANES)))
+    g_ext = g_ext.reshape(n_seq, n_wsh, rows_in, LANES)
+
+    d_skip = dtaps[5, 2 * N_STATE :].reshape(heads, P_SIZE).sum(-1)
+    d_head = jnp.concatenate([dhead[:2, :heads], d_skip[None]], axis=0)
+    pieces = (
+        d_gain_part,
+        dtaps[:5, : 2 * N_STATE],
+        d_out_gain,
+        dtaps[:5, 2 * N_STATE :],
+        d_head,
+    )
+    flat = jnp.concatenate([p.reshape(-1) for p in pieces])
+    flat = jnp.pad(flat, (0, -flat.shape[0] % (8 * LANES))).reshape(-1, LANES)
+    g_ext, flat = swap(
+        (g_ext, flat), ((1, "wshard"), ("all", "wshard")), n_seq, n_wsh, 3
+    )
+    g_ext = jnp.sum(g_ext.astype(f32), axis=0)
+    (flat,) = swap((jnp.sum(flat, axis=0),), (("all", "seq"),), n_seq, n_wsh, 4)
     flat = flat.reshape(n_seq, -1)
     sums, at = [], 0
     for p in pieces:
         sums.append(flat[:, at : at + p.size].reshape((n_seq,) + p.shape))
         at += p.size
-    grad_conv_shared = jnp.sum(sums[0], axis=0)
-    grad_out_gain = sums[1].reshape(-1)
-    grad_conv_inner = jnp.swapaxes(sums[2], 0, 1).reshape(conv_inner.shape)
-    grad_head_params = jnp.swapaxes(sums[3], 0, 1).reshape(head_params.shape)
-    new_in_weight, new_first_in_weight, new_second_in_weight = adamw(
-        in_weight,
-        grad_in_weight,
-        first_in_weight,
-        second_in_weight,
-        weight_learning_rate,
-        matrix_decay,
+    grad_in_gain = jnp.sum(sums[0], axis=0) / in_gain
+    grad_conv_shared = jnp.sum(sums[1], axis=0)
+    grad_out_gain = sums[2].reshape(-1)
+    grad_conv_inner = jnp.swapaxes(sums[3], 0, 1).reshape(conv_inner.shape)
+    grad_head_params = jnp.swapaxes(sums[4], 0, 1).reshape(head_params.shape)
+
+    g_main = g_parts[0].astype(f32)
+    for part in g_parts[1:]:
+        g_main = g_main + part.astype(f32)
+    g_main, g_ext = swap(
+        (g_main.astype(bf16), g_ext.astype(bf16)),
+        ((0, "seq"), (0, "seq")),
+        n_seq,
+        n_wsh,
+        5,
+    )
+    g_ext = jnp.swapaxes(g_ext, 0, 1)
+    g_ext = jnp.concatenate(
+        [
+            g_ext[:, :, :share].reshape(rows_in, 2 * N_STATE),
+            g_ext[:, :, share : share + heads].reshape(rows_in, heads * n_seq),
+        ],
+        axis=1,
+    )
+    g_ext = jnp.pad(g_ext, ((0, 0), (0, 2 * width - g_ext.shape[1])))
+    grad_in_weight, new_in_weight, new_first_in_weight, new_second_in_weight = adam_in(
+        g_main, g_ext, in_weight, first_in_weight, second_in_weight
     )
     new_out_weight, new_first_out_weight, new_second_out_weight = adamw(
         out_weight,

time: 438 us -> 428 us (0.977)
  Pallas kernels: 260 us -> 196 us
  waiting for transfers between devices: 19.7 us -> 76.8 us
  starting transfers between devices: 10.5 us -> 24.2 us
  other arithmetic: 39.3 us -> 29.5 us
  matrix products: 73.2 us -> 67.3 us
    pallas_call x3 -> x4, Pallas kernels: 128 us -> 56.9 us  [swap(): pl.pallas_call(functools.partial(swap_kernel, plan, n_seq, n_wsh), in_spe...]
    ppermute x6 -> x9, waiting for transfers between devices: 18.4 us -> 76 us  [shift(): lax.ppermute(x, 'wshard', [(i, (i + j) % n_wsh) for i in range(n_wsh)])]
    ppermute x6 -> x9, starting transfers between devices: 10.4 us -> 24.1 us  [shift(): lax.ppermute(x, 'wshard', [(i, (i + j) % n_wsh) for i in range(n_wsh)])]
    pallas_call x0 -> x1, Pallas kernels: none -> 8.13 us  [adam_in(): pl.pallas_call(functools.partial(adam_kernel, count), grid=(count + 1,),...]
    sub x7 -> x6, other arithmetic: 14.2 us -> 6.74 us  [adamw(): return (param - rate * (corrected + decay * param), first_new, second_new)]
    dot_general x7 -> x8, matrix products: 61.3 us -> 58.9 us  [mm(): return lax.dot_general(a, b, dims, preferred_element_type=f32)]
  transfers between devices with their start and end apart: 10 -> 13, of which waited for: 2 -> 5; matrix products, arithmetic and copies ran while one was open for 17% -> 18% of each run, Pallas kernels for 44% -> 44%
where the time goes in v3:
time: 428 us; the launch traced here: 426 us
  Pallas kernels  196 us (46%)
  waiting for transfers between devices  76.8 us (18%)
  matrix products  67.3 us (16%)
  other arithmetic  29.5 us (7%)
  starting transfers between devices  24.2 us (6%)
  local copies, waits for them, and re-layouts  17.6 us (4%)
  between operations  14.6 us (3%)
    ppermute x9, waiting for transfers between devices, shift(): lax.ppermute(x, 'wshard', [(i, (i + j) % n_wsh) for i in range(n_wsh)])  76 us
    dot_general x8, matrix products, mm(): return lax.dot_general(a, b, dims, preferred_element_type=f32)  58.9 us
    pallas_call x1, Pallas kernels, spread_weights(): pl.pallas_call(functools.partial(weights_kernel, n_seq, n_wsh), in_specs=...  57.2 us
    pallas_call x4, Pallas kernels, swap(): pl.pallas_call(functools.partial(swap_kernel, plan, n_seq, n_wsh), in_spe...  56.9 us
    pallas_call x1, Pallas kernels, mixer_backward(): pl.pallas_call(functools.partial(bwd_kernel, heads, count), grid=(count,)...  46.6 us
    ppermute x9, starting transfers between devices, shift(): lax.ppermute(x, 'wshard', [(i, (i + j) % n_wsh) for i in range(n_wsh)])  24.1 us
    pallas_call x1, Pallas kernels, mixer_forward(): pl.pallas_call(functools.partial(fwd_kernel, heads), grid=(count,), in_sp...  20.3 us
  transfers between devices with their start and end apart: 13, of which 5 were waited for; matrix products, arithmetic and copies ran while one was open for 18% of the time, Pallas kernels for 44%

profile of v3, /device:TPU:0, one launch (start us, length us, event | category | flops | bytes accessed | tf_op | source)
XLA Modules:
  0.0 426.4 jit_solution(16525501730439985989)
XLA Ops:
  7.3 1.5 fusion.13
  9.8 2.3 fusion.15
  12.2 0.7 all-gather.6.cloned.1.call-update
  13.2 0.9 copy.92
  14.1 0.6 pad.24.small
  14.7 57.2 %spread_weights.1 = (bf16[8,4,48,768]{3,2,1,0:T(8,128)(2,1)}, bf16[8,4,48,384]{3,2,1,0:T(8,128)(2,1)}) custom-call(bf16[8,48,768]{2,1,0:T(8,128)(2,1)} %bitcast.101, bf16[48,384]{1,0:T(8,128)(2,1)} %pad.24.small), custom_call_target="tpu_custom_call" | custom-call | bytes 200000000 | tf_op jit(solution)/shard_map/spread_weights/pallas_call | solution.py:495
  71.9 3.3 collective-permute-start.2
  75.2 0.6 collective-permute-start
  76.0 0.8 copy.76
  76.8 0.8 dynamic_slice.36
  78.2 0.7 constant_dynamic-slice_fusion.3
  79.7 16.2 %collective-permute-done = bf16[96,1536]{1,0:T(8,128)(2,1)} collective-permute-done((bf16[96,1536]{1,0:T(8,128)(2,1)S(1)}, bf16[96,1536]{1,0:T(8,128)(2,1)}, u32[]{:S(2)}, u32[]{:S(2)}) %collective-permute-start) | collective-permute-done | bytes 294944 | tf_op jit(solution)/shard_map/ppermute | solution.py:664
  95.9 1.0 bitcast_dynamic-update-slice_fusion.2
  96.8 3.2 collective-permute-done.1
  100.2 8.5 %convolution_convert_fusion.2.small_ref.small_prev = bf16[2048,384]{1,0:T(8,128)(2,1)} fusion(bf16[2048,1536]{1,0:T(8,128)(2,1)} %all-gather.4.cloned.1.call-done, bf16[1536,384]{1,0:T(8,128)(2,1)S(1)} %bitcast.109, bf16[384,128]{1,0:T(8,128)(2,1)} %copy.76, bf16[384,256]{1,0:T(8,128)(2,1)S(1)} %select_convert_fusion), kind=kOutput, calls=%fused_computation.28 | convolution fusion | flops 2870870016 | bytes 9338880 | tf_op jit(solution)/shard_map/dot_general | solution.py:35
  108.7 9.0 %convolution_convert_fusion.1.main_ref.main_prev = bf16[2048,768]{1,0:T(8,128)(2,1)} fusion(bf16[2048,1536]{1,0:T(8,128)(2,1)} %all-gather.4.cloned.1.call-done, bf16[1536,768]{1,0:T(8,128)(2,1)} %bitcast.126), kind=kOutput, calls=%fused_computation.12 | convolution fusion | flops 4833411072 | bytes 11796480 | tf_op jit(solution)/shard_map/dot_general | solution.py:35
  117.7 20.3 %mixer_forward.1 = (bf16[2048,384]{1,0:T(8,128)(2,1)}, f32[2048,384]{1,0:T(8,128)}, f32[16,128,384]{2,1,0:T(8,128)}) custom-call(bf16[2048,768]{1,0:T(8,128)(2,1)} %convolution_convert_fusion.1.main_ref.main_prev, bf16[2048,384]{1,0:T(8,128)(2,1)} %convolution_convert_fusion.2.small_ref.small_prev, f32[8,128]{1,0:T(8,128)} %pad.25.head_ref, ...), custom_call_target="tpu_custom_call" | custom-call | bytes 70000000 | tf_op jit(solution)/shard_map/mixer_forward/pallas_call | solution.py:192
  138.0 7.1 %fusion.4 = (f32[2048]{0:T(1024)S(1)}, f32[2048]{0:T(1024)S(1)}, f32[384,2048]{0,1:T(8,128)S(1)}) fusion(bf16[2048,384]{1,0:T(8,128)(2,1)} %get-tuple-element.61, f32[384]{0:T(512)S(1)} %dynamic_slice.36, bf16[384,1536]{1,0:T(8,128)(2,1)} %bitcast.106, bf16[1,2048,1536]{2,1,0:T(8,128)(2,1)} %all-gather.6.cloned.1.call-done), kind=kOutput, calls=%fused_computation.13 | convolution fusion | flops 2420633600 | bytes 12207616 | tf_op jit(solution)/shard_map/dot_general | solution.py:35
  145.2 0.6 reshape.183.x_ref
  145.8 7.2 %sum_over_seq.1 = f32[32,128]{1,0:T(8,128)} custom-call(f32[32,128]{1,0:T(8,128)} %reshape.183.x_ref), custom_call_target="tpu_custom_call" | custom-call | tf_op jit(solution)/shard_map/sum_over_seq/pallas_call | solution.py:637
  153.0 0.7 multiply_multiply_fusion.5
  153.7 0.7 multiply_bitcast_fusion
  154.5 7.9 %convolution_convert_fusion = bf16[2048,1536]{1,0:T(8,128)(2,1)} fusion(bf16[384,1536]{1,0:T(8,128)(2,1)} %bitcast.107, bf16[2048,384]{1,0:T(8,128)(2,1)} %get-tuple-element.61, f32[2048]{0:T(1024)S(1)} %get-tuple-element.118, f32[384]{0:T(512)S(1)} %dynamic_slice.36), kind=kOutput, calls=%fused_computation.1 | convolution fusion | flops 2422210560 | bytes 9053696 | tf_op jit(solution)/shard_map/dot_general | solution.py:35
  162.3 3.5 fusion.12
  165.9 5.1 %fusion = f32[384,1536]{1,0:T(8,128)S(1)} fusion(bf16[1,2048,1536]{2,1,0:T(8,128)(2,1)} %all-gather.6.cloned.1.call-done, bf16[2048,384]{1,0:T(8,128)(2,1)S(1)} %copy-done.6, f32[2048]{0:T(1024)S(1)} %get-tuple-element.118, f32[384]{0:T(512)S(1)} %dynamic_slice.36), kind=kOutput, calls=%fused_computation.2 | convolution fusion | flops 2419064832 | bytes 10233344 | tf_op jit(solution)/shard_map/dot_general | solution.py:35
  171.2 2.4 convolution_convert_fusion.4
  173.6 46.6 %mixer_backward.1 = (bf16[2048,768]{1,0:T(8,128)(2,1)}, bf16[256,2048]{1,0:T(8,128)(2,1)}, bf16[16,2048]{1,0:T(8,128)(2,1)}, f32[8,640]{1,0:T(8,128)}, f32[8,128]{1,0:T(8,128)}) custom-call(bf16[2048,768]{1,0:T(8,128)(2,1)} %convolution_convert_fusion.1.main_ref.main_prev, bf16[2048,384]{1,0:T(8,128)(2,1)} %convolution_convert_fusion.2.small_ref.small_prev, ...), custom_call_target="tpu_custom_call" | custom-call | bytes 160000000 | tf_op jit(solution)/shard_map/mixer_backward/pallas_call | solution.py:365
  220.2 22.1 %shard_map.462 = bf16[8,32,2048]{2,1,0:T(8,128)(2,1)} custom-call(bf16[8,32,2048]{2,1,0:T(8,128)(2,1)} %bitcast.110), custom_call_target="tpu_custom_call" | custom-call | tf_op jit(solution)/shard_map/pallas_call | solution.py:602
  242.3 1.4 reduce_sum.128
  243.7 7.9 %fusion.59 = f32[2048,1536]{1,0:T(8,128)S(1)} fusion(bf16[2048,768]{1,0:T(8,128)(2,1)} %get-tuple-element.64, bf16[1536,768]{1,0:T(8,128)(2,1)} %bitcast.127), kind=kOutput, calls=%fused_computation.135 | convolution fusion | flops 4831838208 | bytes 18087936 | tf_op jit(solution)/shard_map/dot_general | solution.py:35
  251.7 4.4 %add_convert_fusion = bf16[2048,1536]{1,0:T(8,128)(2,1)} fusion(f32[2048,1536]{1,0:T(8,128)S(1)} %fusion.59, bf16[1536,48]{0,1:T(8,128)(2,1)S(1)} %convolution_convert_fusion.4, bf16[16,2048]{1,0:T(8,128)(2,1)S(1)} %copy-done.12, bf16[32,2048]{1,0:T(8,128)(2,1)S(1)} %reduce_sum.128), kind=kOutput, calls=%fused_computation | convolution fusion | flops 308674560 | bytes 19218432 | tf_op jit(solution)/shard_map/dot_general | solution.py:820
  256.2 0.6 copy-done.20
  256.9 0.7 slice.64
  257.9 3.9 multiply_reduce_fusion.1
  262.1 0.8 pad.27.clone
  262.9 11.0 %multiply_reduce_fusion = (f32[1536]{0:T(1024)S(1)}, bf16[1536,768]{1,0:T(8,128)(2,1)}) fusion(bf16[8,4,48,768]{3,2,1,0:T(8,128)(2,1)} %get-tuple-element.57, bf16[2048,1536]{1,0:T(8,128)(2,1)} %all-gather.4.cloned.1.call-done, bf16[2048,768]{1,0:T(8,128)(2,1)} %get-tuple-element.64), kind=kOutput, calls=%fused_computation.11 | convolution fusion | flops 4836555264 | bytes 14161920 | tf_op jit(solution)/shard_map/dot_general | solution.py:35
  274.5 14.1 %shard_map.463 = (bf16[4,8,48,128]{3,2,1,0:T(8,128)(2,1)}, f32[4,48,128]{2,1,0:T(8,128)}) custom-call(bf16[8,4,48,128]{3,2,1,0:T(8,128)(2,1)} %bitcast.105, f32[48,128]{1,0:T(8,128)} %pad_bitcast_fusion.refs_1_), custom_call_target="tpu_custom_call" | custom-call | tf_op jit(solution)/shard_map/pallas_call | solution.py:602
  288.7 1.5 reduce_sum.135.refs_0_
  290.2 9.0 %shard_map.465 = f32[8,48,128]{2,1,0:T(8,128)} custom-call(f32[48,128]{1,0:T(8,128)} %reduce_sum.135.refs_0_), custom_call_target="tpu_custom_call" | custom-call | tf_op jit(solution)/shard_map/pallas_call | solution.py:602
  299.2 1.0 copy.93
  300.2 1.7 reduce_sum.134.refs_1_
  303.3 1.6 dynamic-slice_bitcast_fusion.2
  305.1 1.2 collective-permute-start.3
  306.3 2.7 collective-permute-start.5
  309.0 1.2 constant_dynamic-slice_fusion.2
  310.2 1.7 collective-permute-start.6
  311.9 2.1 collective-permute-start.8
  314.1 0.8 multiply_subtract_fusion.1
  314.9 0.6 multiply_subtract_fusion.4
  315.5 0.6 multiply_subtract_fusion.3
  316.1 0.6 multiply_subtract_fusion.2
  316.8 6.4 %collective-permute-done.3 = bf16[8,48,768]{2,1,0:T(8,128)(2,1)S(1)} collective-permute-done((bf16[8,48,768]{2,1,0:T(8,128)(2,1)S(1)}, bf16[8,48,768]{2,1,0:T(8,128)(2,1)S(1)}, u32[]{:S(2)}, u32[]{:S(2)}) %collective-permute-start.3) | collective-permute-done | bytes 589856 | tf_op jit(solution)/shard_map/ppermute | solution.py:664
  323.2 12.4 %collective-permute-start.7 = (f32[96,1536]{1,0:T(8,128)}, f32[96,1536]{1,0:T(8,128)}, u32[]{:S(2)}, u32[]{:S(2)}) collective-permute-start(f32[96,1536]{1,0:T(8,128)} %get-tuple-element.109), channel_id=1, source_target_pairs={{0,2},{1,3},{2,0},{3,1},{4,6},{5,7},{6,4},{7,5},{8,10},{9,11},{10,... | collective-permute-start | bytes 1769480 | tf_op jit(solution)/shard_map/ppermute | solution.py:664
  336.1 37.5 %collective-permute-done.4 = bf16[8,48,768]{2,1,0:T(8,128)(2,1)S(1)} collective-permute-done((bf16[8,48,768]{2,1,0:T(8,128)(2,1)S(1)}, bf16[8,48,768]{2,1,0:T(8,128)(2,1)S(1)}, u32[]{:S(2)}, u32[]{:S(2)}) %collective-permute-start.4) | collective-permute-done | bytes 589856 | tf_op jit(solution)/shard_map/ppermute | solution.py:664
  373.5 2.2 fusion.23.refs_0_
  375.7 11.8 %shard_map.464 = (bf16[8,48,768]{2,1,0:T(8,128)(2,1)}, bf16[8,48,128]{2,1,0:T(8,128)(2,1)}) custom-call(bf16[8,48,768]{2,1,0:T(8,128)(2,1)} %fusion.23.refs_0_, bf16[8,48,128]{2,1,0:T(8,128)(2,1)} %reduce_sum.134.refs_1_), custom_call_target="tpu_custom_call" | custom-call | tf_op jit(solution)/shard_map/pallas_call | solution.py:602
  387.5 1.0 slice.79
  388.5 0.9 copy.80
  389.8 0.7 fusion.39.ext_ref
  390.4 8.1 %adam_in.1 = (f32[48,6448]{1,0:T(8,128)}, f32[48,6448]{1,0:T(8,128)}, f32[48,6448]{1,0:T(8,128)}, f32[48,6448]{1,0:T(8,128)}) custom-call(bf16[8,48,768]{2,1,0:T(8,128)(2,1)} %get-tuple-element.73.g_ref, bf16[48,768]{1,0:T(8,128)(2,1)} %fusion.39.ext_ref, f32[48,6448]{1,0:T(8,128)} %p_ref.1, f32[48,6448]{1,0:T(8,128)} %m_ref.1, f32[48,6448]{1,0:T(8,128)} %v_ref.1), custom_call_target="tpu_custom_call" | custom-call | tf_op jit(solution)/shard_map/adam_in/pallas_call | solution.py:681
  398.6 12.7 %collective-permute-done.7 = f32[96,1536]{1,0:T(8,128)} collective-permute-done((f32[96,1536]{1,0:T(8,128)}, f32[96,1536]{1,0:T(8,128)}, u32[]{:S(2)}, u32[]{:S(2)}) %collective-permute-start.7) | collective-permute-done | bytes 589856 | tf_op jit(solution)/shard_map/ppermute | solution.py:664
  411.4 3.5 multiply_subtract_fusion
  414.9 1.5 fusion.20
  416.4 3.4 fusion.19
  (144 shorter events, 7.0 us)
Async XLA Ops:
  7.2 5.7 %copy-start.1 = (f32[48,6448]{1,0:T(8,128)S(1)}, f32[48,6448]{1,0:T(8,128)}, u32[]{:S(2)}) copy-start(f32[48,6448]{1,0:T(8,128)} %p_ref.1) | copy-start | bytes 3714052
  7.2 92.9 %all-gather.4.cloned.1.call-start = ((), (), s32[]{:S(2)}) async-start(), calls=%async_computation.2 | async-start | bytes 7077888 | tf_op jit(solution)/shard_map/all_gather | solution.py:737
  9.3 0.5 copy-start.24
  12.1 1.1 copy-start.3
  12.1 125.9 %all-gather.6.cloned.1.call-start = ((), (), s32[]{:S(2)}) async-start(), calls=%async_computation.5 | async-start | bytes 7077888 | tf_op jit(solution)/shard_map/all_gather | solution.py:739
  12.9 243.2 %reduce-scatter.3.cloned.1.call-start = ((), (), s32[]{:S(2)}) async-start(), calls=%async_computation.3 | async-start | bytes 7077888 | tf_op jit(solution)/shard_map/reduce_scatter | solution.py:796
  13.0 64.5 %copy-start.29 = (f32[3,48]{1,0:T(4,128)S(1)}, f32[3,48]{1,0:T(4,128)}, u32[]{:S(2)}) copy-start(f32[3,48]{1,0:T(4,128)} %param.31) | copy-start | bytes 1732
  13.0 65.9 %copy-start.18 = (f32[5,256]{1,0:T(8,128)S(1)}, f32[5,256]{1,0:T(8,128)}, u32[]{:S(2)}) copy-start(f32[5,256]{1,0:T(8,128)} %param.30) | copy-start | bytes 15364
  71.9 28.3 %copy-start.8 = (bf16[8,4,48,384]{3,2,1,0:T(8,128)(2,1)S(1)}, bf16[8,4,48,384]{3,2,1,0:T(8,128)(2,1)}, u32[]{:S(2)}) copy-start(bf16[8,4,48,384]{3,2,1,0:T(8,128)(2,1)} %get-tuple-element.58) | copy-start | bytes 3538948
  71.9 28.2 %collective-permute-start.2 = (bf16[96,1536]{1,0:T(8,128)(2,1)S(1)}, bf16[96,1536]{1,0:T(8,128)(2,1)S(1)}, u32[]{:S(2)}, u32[]{:S(2)}) collective-permute-start(bf16[96,1536]{1,0:T(8,128)(2,1)S(1)} %convert_element_type.102), channel_id=1, source_target_pairs={{0,3},{1,0},{2,1},{3,2},{4,7},{5,4},{6,5},{7,6},{8,11},{9,8},{10,9... | collective-permute-start | bytes 884744 | tf_op jit(solution)/shard_map/ppermute | solution.py:664
  75.2 24.8 %collective-permute-start.1 = (bf16[96,1536]{1,0:T(8,128)(2,1)S(1)}, bf16[96,1536]{1,0:T(8,128)(2,1)S(1)}, u32[]{:S(2)}, u32[]{:S(2)}) collective-permute-start(bf16[96,1536]{1,0:T(8,128)(2,1)S(1)} %convert_element_type.102), channel_id=1, source_target_pairs={{0,2},{1,3},{2,0},{3,1},{4,6},{5,7},{6,4},{7,5},{8,10},{9,11},{10,... | collective-permute-start | bytes 884744 | tf_op jit(solution)/shard_map/ppermute | solution.py:664
  75.2 20.6 %collective-permute-start = (bf16[96,1536]{1,0:T(8,128)(2,1)S(1)}, bf16[96,1536]{1,0:T(8,128)(2,1)}, u32[]{:S(2)}, u32[]{:S(2)}) collective-permute-start(bf16[96,1536]{1,0:T(8,128)(2,1)S(1)} %convert_element_type.102), channel_id=1, source_target_pairs={{0,1},{1,2},{2,3},{3,0},{4,5},{5,6},{6,7},{7,4},{8,9},{9,10},{10,1... | collective-permute-start | bytes 884744 | tf_op jit(solution)/shard_map/ppermute | solution.py:664
  100.1 8.6 %copy-start.7 = (bf16[4,96,1536]{2,1,0:T(8,128)(2,1)}, bf16[4,96,1536]{2,1,0:T(8,128)(2,1)S(1)}, u32[]{:S(2)}) copy-start(bf16[4,96,1536]{2,1,0:T(8,128)(2,1)S(1)} %bitcast_dynamic-update-slice_fusion) | copy-start | bytes 3538948
  162.3 3.5 copy-start.6
  171.0 138.0 %copy-start.5 = (f32[384,1536]{1,0:T(8,128)}, f32[384,1536]{1,0:T(8,128)S(1)}, u32[]{:S(2)}) copy-start(f32[384,1536]{1,0:T(8,128)S(1)} %fusion) | copy-start | bytes 7077892
  171.0 243.9 %reduce-scatter.5.cloned.1.call-start = ((), (), s32[]{:S(2)}) async-start(), calls=%async_computation.4 | async-start | bytes 7077888 | tf_op jit(solution)/shard_map/reduce_scatter | solution.py:825
  243.7 8.0 %copy-start.12 = (bf16[16,2048]{1,0:T(8,128)(2,1)S(1)}, bf16[16,2048]{1,0:T(8,128)(2,1)}, u32[]{:S(2)}) copy-start(bf16[16,2048]{1,0:T(8,128)(2,1)} %get-tuple-element.66) | copy-start | bytes 196612
  256.1 0.7 copy-start.20
  262.9 39.2 %copy-start.33 = (f32[3,48]{1,0:T(4,128)S(1)}, f32[3,48]{1,0:T(4,128)}, u32[]{:S(2)}) copy-start(f32[3,48]{1,0:T(4,128)} %param.38) | copy-start | bytes 1732
  262.9 39.2 %copy-start.34 = (f32[3,48]{1,0:T(4,128)S(1)}, f32[3,48]{1,0:T(4,128)}, u32[]{:S(2)}) copy-start(f32[3,48]{1,0:T(4,128)} %param.45) | copy-start | bytes 1732
  301.9 13.6 %copy-start.19 = (f32[5,256]{1,0:T(8,128)}, f32[5,256]{1,0:T(8,128)S(1)}, u32[]{:S(2)}) copy-start(f32[5,256]{1,0:T(8,128)S(1)} %reduce_sum.138) | copy-start | bytes 15364
  302.1 0.6 copy-start.28
  303.3 12.8 %copy-start.17 = (f32[3072]{0:T(1024)}, f32[3072]{0:T(1024)S(1)}, u32[]{:S(2)}) copy-start(f32[3072]{0:T(1024)S(1)} %reshape.194) | copy-start | bytes 36868
  303.3 10.7 %copy-start.11 = (f32[1,5,8,384]{3,1,2,0:T(8,128)}, f32[1,5,8,384]{3,1,2,0:T(8,128)S(1)}, u32[]{:S(2)}) copy-start(f32[1,5,8,384]{3,1,2,0:T(8,128)S(1)} %copy.89) | copy-start | bytes 184324
  304.9 9.1 %copy-start.14 = (f32[5,3072]{1,0:T(8,128)S(1)}, f32[5,3072]{1,0:T(8,128)}, u32[]{:S(2)}) copy-start(f32[5,3072]{1,0:T(8,128)} %param.29) | copy-start | bytes 184324
  305.0 9.1 %copy-start.15 = (f32[5,3072]{1,0:T(8,128)S(1)}, f32[5,3072]{1,0:T(8,128)}, u32[]{:S(2)}) copy-start(f32[5,3072]{1,0:T(8,128)} %param.36) | copy-start | bytes 184324
  305.0 9.1 %copy-start.16 = (f32[5,3072]{1,0:T(8,128)S(1)}, f32[5,3072]{1,0:T(8,128)}, u32[]{:S(2)}) copy-start(f32[5,3072]{1,0:T(8,128)} %param.43) | copy-start | bytes 184324
  305.0 9.9 %copy-start.13 = (f32[1536]{0:T(1024)S(1)}, f32[1536]{0:T(1024)}, u32[]{:S(2)}) copy-start(f32[1536]{0:T(1024)} %param.27) | copy-start | bytes 18436
  305.0 9.9 %copy-start.30 = (f32[1536]{0:T(1024)S(1)}, f32[1536]{0:T(1024)}, u32[]{:S(2)}) copy-start(f32[1536]{0:T(1024)} %param.34) | copy-start | bytes 18436
  305.0 9.8 %copy-start.31 = (f32[1536]{0:T(1024)S(1)}, f32[1536]{0:T(1024)}, u32[]{:S(2)}) copy-start(f32[1536]{0:T(1024)} %param.41) | copy-start | bytes 18436
  305.0 10.5 %copy-start.26 = (f32[5,256]{1,0:T(8,128)S(1)}, f32[5,256]{1,0:T(8,128)}, u32[]{:S(2)}) copy-start(f32[5,256]{1,0:T(8,128)} %param.37) | copy-start | bytes 15364
  305.0 10.5 %copy-start.27 = (f32[5,256]{1,0:T(8,128)S(1)}, f32[5,256]{1,0:T(8,128)}, u32[]{:S(2)}) copy-start(f32[5,256]{1,0:T(8,128)} %param.44) | copy-start | bytes 15364
  305.0 11.1 %copy-start.21 = (f32[3072]{0:T(1024)S(1)}, f32[3072]{0:T(1024)}, u32[]{:S(2)}) copy-start(f32[3072]{0:T(1024)} %param.28) | copy-start | bytes 36868
  305.1 11.1 %copy-start.22 = (f32[3072]{0:T(1024)S(1)}, f32[3072]{0:T(1024)}, u32[]{:S(2)}) copy-start(f32[3072]{0:T(1024)} %param.35) | copy-start | bytes 36868
  305.1 11.1 %copy-start.23 = (f32[3072]{0:T(1024)S(1)}, f32[3072]{0:T(1024)}, u32[]{:S(2)}) copy-start(f32[3072]{0:T(1024)} %param.42) | copy-start | bytes 36868
  305.1 18.1 %collective-permute-start.3 = (bf16[8,48,768]{2,1,0:T(8,128)(2,1)S(1)}, bf16[8,48,768]{2,1,0:T(8,128)(2,1)S(1)}, u32[]{:S(2)}, u32[]{:S(2)}) collective-permute-start(bf16[8,48,768]{2,1,0:T(8,128)(2,1)S(1)} %get-tuple-element.110), channel_id=1, source_target_pairs={{0,1},{1,2},{2,3},{3,0},{4,5},{5,6},{6,7},{7,4},{8,9},{9,10},{10,1... | collective-permute-start | bytes 1769480 | tf_op jit(solution)/shard_map/ppermute | solution.py:664
  306.3 29.8 %collective-permute-start.5 = (bf16[8,48,768]{2,1,0:T(8,128)(2,1)S(1)}, bf16[8,48,768]{2,1,0:T(8,128)(2,1)S(1)}, u32[]{:S(2)}, u32[]{:S(2)}) collective-permute-start(bf16[8,48,768]{2,1,0:T(8,128)(2,1)S(1)} %get-tuple-element.111), channel_id=1, source_target_pairs={{0,3},{1,0},{2,1},{3,2},{4,7},{5,4},{6,5},{7,6},{8,11},{9,8},{10,9... | collective-permute-start | bytes 1769480 | tf_op jit(solution)/shard_map/ppermute | solution.py:664
  309.0 64.6 %collective-permute-start.4 = (bf16[8,48,768]{2,1,0:T(8,128)(2,1)S(1)}, bf16[8,48,768]{2,1,0:T(8,128)(2,1)S(1)}, u32[]{:S(2)}, u32[]{:S(2)}) collective-permute-start(bf16[8,48,768]{2,1,0:T(8,128)(2,1)S(1)} %get-tuple-element.112), channel_id=1, source_target_pairs={{0,2},{1,3},{2,0},{3,1},{4,6},{5,7},{6,4},{7,5},{8,10},{9,11},{10,... | collective-permute-start | bytes 1769480 | tf_op jit(solution)/shard_map/ppermute | solution.py:664
  310.2 88.4 %collective-permute-start.6 = (f32[96,1536]{1,0:T(8,128)}, f32[96,1536]{1,0:T(8,128)}, u32[]{:S(2)}, u32[]{:S(2)}) collective-permute-start(f32[96,1536]{1,0:T(8,128)} %get-tuple-element.107), channel_id=1, source_target_pairs={{0,1},{1,2},{2,3},{3,0},{4,5},{5,6},{6,7},{7,4},{8,9},{9,10},{10,1... | collective-permute-start | bytes 1769480 | tf_op jit(solution)/shard_map/ppermute | solution.py:664
  311.9 86.7 %collective-permute-start.8 = (f32[96,1536]{1,0:T(8,128)}, f32[96,1536]{1,0:T(8,128)}, u32[]{:S(2)}, u32[]{:S(2)}) collective-permute-start(f32[96,1536]{1,0:T(8,128)} %get-tuple-element.108), channel_id=1, source_target_pairs={{0,3},{1,0},{2,1},{3,2},{4,7},{5,4},{6,5},{7,6},{8,11},{9,8},{10,9... | collective-permute-start | bytes 1769480 | tf_op jit(solution)/shard_map/ppermute | solution.py:664
  323.2 88.2 %collective-permute-start.7 = (f32[96,1536]{1,0:T(8,128)}, f32[96,1536]{1,0:T(8,128)}, u32[]{:S(2)}, u32[]{:S(2)}) collective-permute-start(f32[96,1536]{1,0:T(8,128)} %get-tuple-element.109), channel_id=1, source_target_pairs={{0,2},{1,3},{2,0},{3,1},{4,6},{5,7},{6,4},{7,5},{8,10},{9,11},{10,... | collective-permute-start | bytes 1769480 | tf_op jit(solution)/shard_map/ppermute | solution.py:664
  389.5 21.9 %copy-start.4 = (f32[96,1536]{1,0:T(8,128)S(1)}, f32[96,1536]{1,0:T(8,128)}, u32[]{:S(2)}) copy-start(f32[96,1536]{1,0:T(8,128)} %param.26) | copy-start | bytes 1769476
  389.5 21.9 %copy-start.10 = (f32[96,1536]{1,0:T(8,128)S(1)}, f32[96,1536]{1,0:T(8,128)}, u32[]{:S(2)}) copy-start(f32[96,1536]{1,0:T(8,128)} %param.33) | copy-start | bytes 1769476
  398.6 16.3 %copy-start = (bf16[1,256,1536]{2,1,0:T(8,128)(2,1)S(1)}, bf16[1,256,1536]{2,1,0:T(8,128)(2,1)}, u32[]{:S(2)}) copy-start(bf16[1,256,1536]{2,1,0:T(8,128)(2,1)} %param.23) | copy-start | bytes 2359300
  398.6 17.8 %copy-start.2 = (bf16[1,256,1536]{2,1,0:T(8,128)(2,1)S(1)}, bf16[1,256,1536]{2,1,0:T(8,128)(2,1)}, u32[]{:S(2)}) copy-start(bf16[1,256,1536]{2,1,0:T(8,128)(2,1)} %param.24) | copy-start | bytes 2359300
  398.6 17.8 %copy-start.9 = (bf16[256,1536]{1,0:T(8,128)(2,1)S(1)}, bf16[256,1536]{1,0:T(8,128)(2,1)}, u32[]{:S(2)}) copy-start(bf16[256,1536]{1,0:T(8,128)(2,1)} %reduce-scatter.3.cloned.1.call-done) | copy-start | bytes 2359300
  398.6 17.8 %copy-start.25 = (f32[256]{0:T(256)S(1)}, f32[256]{0:T(256)}, u32[]{:S(2)}) copy-start(f32[256]{0:T(256)} %copy-done.24) | copy-start | bytes 3076
  398.6 17.8 %copy-start.32 = (f32[256]{0:T(256)S(1)}, f32[256]{0:T(256)}, u32[]{:S(2)}) copy-start(f32[256]{0:T(256)} %get-tuple-element.119) | copy-start | bytes 3076
Sparse Core Ops, SparseCore 0:
  12.3 61.3 all-gather.3
  75.5 45.3 all-gather.5
  171.1 74.2 reduce-scatter.2
  256.3 64.4 reduce-scatter.4

commit v4 on v3

--- a/solution.py
+++ b/solution.py
@@ -89,8 +89,9 @@
     return jnp.concatenate(out, axis=1)
 
 
-def expand(cols, heads):
+def expand(cols, heads, offset=0):
     rows = cols.shape[0]
+    cols = cols[:, offset : offset + heads]
     low = low_half(rows)
     out = []
     for h in range(0, heads, 2):
@@ -219,28 +220,26 @@
     )(main, small, head, taps)
 
 
-def bwd_kernel(
-    heads,
-    count,
-    main_ref,
-    small_ref,
-    main_prev,
-    small_prev,
-    head_ref,
-    taps_ref,
-    y_ref,
-    states_ref,
-    dgated_ref,
-    dmain_ref,
-    dshared_ref,
-    dstep_ref,
-    dtaps_ref,
-    dhead_ref,
-    dstate,
-    cat,
-    dcat,
-):
+def bwd_kernel(heads, offset, count, has_before, is_last, *refs):
+    refs = list(refs)
+    main_ref, small_ref, main_prev, small_prev, head_ref, taps_ref = refs[:6]
+    y_ref, states_ref, dgated_ref = refs[6:9]
+    refs = refs[9:]
+    if has_before:
+        dmain_before, dbc_before = refs[:2]
+        refs = refs[2:]
+    dmain_ref, dstep_ref, dtaps_ref, dhead_ref = refs[:4]
+    refs = refs[4:]
+    if is_last:
+        dshared_ref = refs.pop(0)
+        if has_before:
+            dall_ref = refs.pop(0)
+    else:
+        dbc_ref = refs.pop(0)
+    dstate, cat, dcat = refs
     rows, width = y_ref.shape
+    base = 2 * N_STATE if is_last else 0
+    skip_cols = 2 * N_STATE - base
     step = pl.program_id(0)
 
     @pl.when(step == 0)
@@ -265,14 +264,16 @@
     )
     sig = jax.nn.sigmoid(conv)
     act = conv * sig
-    dsilu = sig * (1.0 + conv * (1.0 - sig))
+    conv_s = conv[:, skip_cols:]
+    sig_s = sig[:, skip_cols:]
+    dsilu = sig_s * (1.0 + conv_s * (1.0 - sig_s))
     b2 = two_parts(act[:, :N_STATE])
     c2 = two_parts(act[:, N_STATE : 2 * N_STATE])
     inner = act[:, 2 * N_STATE :]
-    dt_x = expand(dt, heads)
+    dt_x = expand(dt, heads, offset)
     scaled = inner * dt_x
     scaled2 = two_parts(scaled)
-    skip = expand(head_ref[2:3], heads)
+    skip = expand(head_ref[2:3], heads, offset)
     y = y_ref[...]
     sgate = jax.nn.sigmoid(gate)
     dgated = dgated_ref[...].astype(f32)
@@ -287,7 +288,8 @@
     parts = []
     dscores_t = None
     for h in range(heads):
-        spread = cumul_t[h : h + 1, :] - cumul[:, h : h + 1]
+        at = offset + h
+        spread = cumul_t[at : at + 1, :] - cumul[:, at : at + 1]
         decay = jnp.exp(jnp.where(upper, spread, -1e30))
         weights = two_parts(scores_t * decay)
         dy_pair = tuple(pair_of(part, h, heads) for part in dy2)
@@ -302,9 +304,9 @@
     ds = dstate[...]
     ds2 = two_parts(ds)
     last = cumul[rows - 1 : rows]
-    tail = expand(jnp.exp(last - cumul), heads)
-    ecum = expand(jnp.exp(cumul), heads)
-    elast = expand(jnp.exp(last), heads)
+    tail = expand(jnp.exp(last - cumul), heads, offset)
+    ecum = expand(jnp.exp(cumul), heads, offset)
+    elast = expand(jnp.exp(last), heads, offset)
     tail_b = tail * mm3(b2, ds2, NN)
     z = merge_pairs(parts, heads) + tail_b
     extra = jnp.sum(tail_b * scaled, axis=0, keepdims=True) + elast * jnp.sum(
@@ -313,7 +315,7 @@
     at_end = lax.broadcasted_iota(jnp.int32, (rows, width), 0) == rows - 1
     u = dy * y - scaled * z + jnp.where(at_end, extra, 0.0)
     pick = (
-        lax.broadcasted_iota(jnp.int32, (width, LANES), 0) // P_SIZE
+        lax.broadcasted_iota(jnp.int32, (width, LANES), 0) // P_SIZE + offset
         == lax.broadcasted_iota(jnp.int32, (width, LANES), 1)
     ).astype(f32)
     dcumul = mm_high(u, pick)
@@ -324,82 +326,124 @@
     dhead_ref[0:1] += jnp.sum(dstep, axis=0, keepdims=True)
     dhead_ref[1:2] += jnp.sum(decay_log * ddecay, axis=0, keepdims=True)
 
-    dinner = dt_x * z + skip * dy
+    dact = dt_x * z + skip * dy
     dscores2 = two_parts(dscores_t)
     edy2 = two_parts(ecum * dy)
     db = mm3(dscores2, c2, NN) + mm3(two_parts(tail * scaled), ds2, NT)
     dc = mm3(dscores2, b2, TN) + mm3(edy2, s2, NT)
     dstate[...] = elast * ds + mm3(c2, edy2, TN)
-
-    dconv = jnp.concatenate([db, dc, dinner], axis=1) * dsilu
+    dbc = jnp.concatenate([db, dc], axis=1)
+    if has_before:
+        dbc = dbc + dbc_before[...]
+    if is_last:
+        dact = jnp.concatenate([dbc, dact], axis=1)
+    else:
+        dbc_ref[...] = dbc
+
+    dconv = dact * dsilu
     dcat[0:rows] = dconv
-    draw = taps_ref[3:4] * dconv
+    draw = taps_ref[3:4, skip_cols:] * dconv
     for k in range(3):
-        draw = draw + taps_ref[k : k + 1] * dcat[3 - k : 3 - k + rows]
+        draw = draw + taps_ref[k : k + 1, skip_cols:] * dcat[3 - k : 3 - k + rows]
     for k in range(4):
         dtaps_ref[k : k + 1] += jnp.sum(
-            dconv * cat[5 + k : 5 + k + rows], axis=0, keepdims=True
+            dconv * cat[5 + k : 5 + k + rows, skip_cols:], axis=0, keepdims=True
         )
     dtaps_ref[4:5] += jnp.sum(dconv, axis=0, keepdims=True)
-    dtaps_ref[5:6, 2 * N_STATE :] += jnp.sum(dy * inner, axis=0, keepdims=True)
+    dtaps_ref[5:6, base:] += jnp.sum(dy * inner, axis=0, keepdims=True)
     dcat[rows : rows + 8] = dconv[0:8]
-    dshared_ref[...] = draw[:, : 2 * N_STATE].T.astype(bf16)
-    dmain_ref[...] = join_pairs(dgate, draw[:, 2 * N_STATE :], heads).astype(bf16)
-
-
-def mixer_backward(main, small, head, taps, y, states, dgated, heads):
-    length, width = y.shape
+    dmain = join_pairs(dgate, draw[:, base:], heads).astype(bf16)
+    dmain_ref[...] = dmain
+    if is_last:
+        dshared_ref[...] = draw[:, : 2 * N_STATE].T.astype(bf16)
+        if has_before:
+            dall_ref[...] = jnp.concatenate([dmain_before[...], dmain], axis=1)
+
+
+def mixer_backward(main, small, head, taps, y, states, dgated, heads, offset, before):
+    length, all_width = y.shape
+    all_heads = all_width // P_SIZE
+    width = heads * P_SIZE
+    is_last = offset + heads == all_heads
+    has_before = before is not None
+    place = offset * P_SIZE // width
     count = length // CHUNK
-    all_w = width + 2 * N_STATE
+    cat_w = width + 2 * N_STATE
+    dcat_w = cat_w if is_last else width
     per = CHUNK // 16
 
     def at(i):
         return (count - 1 - i, 0)
 
-    def before(i):
-        return (jnp.maximum((count - 1 - i) * per - 1, 0), 0)
+    def own(i):
+        return (count - 1 - i, place)
+
+    def turned(i):
+        return (0, count - 1 - i)
+
+    def ahead(col):
+        return lambda i: (jnp.maximum((count - 1 - i) * per - 1, 0), col)
 
     def fixed(i):
         return (0, 0)
 
+    taps = jnp.concatenate(
+        [
+            taps[:, : 2 * N_STATE],
+            taps[:, 2 * N_STATE + offset * P_SIZE : 2 * N_STATE + offset * P_SIZE + width],
+        ],
+        axis=1,
+    )
+    args = [main, small, main, small, head, taps, y, states, dgated]
+    in_specs = [
+        pl.BlockSpec((CHUNK, 2 * width), own),
+        pl.BlockSpec((CHUNK, 3 * LANES), at),
+        pl.BlockSpec((16, 2 * width), ahead(place)),
+        pl.BlockSpec((16, 3 * LANES), ahead(0)),
+        pl.BlockSpec((8, LANES), fixed),
+        pl.BlockSpec((8, cat_w), fixed),
+        pl.BlockSpec((CHUNK, width), own),
+        pl.BlockSpec((1, N_STATE, width), lambda i: (count - 1 - i, 0, place)),
+        pl.BlockSpec((CHUNK, width), own),
+    ]
+    if has_before:
+        args += list(before)
+        in_specs += [
+            pl.BlockSpec((CHUNK, before[0].shape[1]), at),
+            pl.BlockSpec((CHUNK, 2 * N_STATE), at),
+        ]
+    outs = [
+        (pl.BlockSpec((CHUNK, 2 * width), at), (length, 2 * width), bf16),
+        (pl.BlockSpec((STEP_ROWS, CHUNK), turned), (STEP_ROWS, length), bf16),
+        (pl.BlockSpec((8, dcat_w), fixed), (8, dcat_w), f32),
+        (pl.BlockSpec((8, LANES), fixed), (8, LANES), f32),
+    ]
+    if is_last:
+        outs.append(
+            (pl.BlockSpec((2 * N_STATE, CHUNK), turned), (2 * N_STATE, length), bf16)
+        )
+        if has_before:
+            outs.append(
+                (pl.BlockSpec((CHUNK, 2 * all_width), at), (length, 2 * all_width), bf16)
+            )
+    else:
+        outs.append((pl.BlockSpec((CHUNK, 2 * N_STATE), at), (length, 2 * N_STATE), f32))
     return pl.pallas_call(
-        functools.partial(bwd_kernel, heads, count),
+        functools.partial(bwd_kernel, heads, offset, count, has_before, is_last),
         grid=(count,),
-        in_specs=[
-            pl.BlockSpec((CHUNK, 2 * width), at),
-            pl.BlockSpec((CHUNK, 3 * LANES), at),
-            pl.BlockSpec((16, 2 * width), before),
-            pl.BlockSpec((16, 3 * LANES), before),
-            pl.BlockSpec((8, LANES), fixed),
-            pl.BlockSpec((8, all_w), fixed),
-            pl.BlockSpec((CHUNK, width), at),
-            pl.BlockSpec((1, N_STATE, width), lambda i: (count - 1 - i, 0, 0)),
-            pl.BlockSpec((CHUNK, width), at),
-        ],
-        out_specs=[
-            pl.BlockSpec((CHUNK, 2 * width), at),
-            pl.BlockSpec((2 * N_STATE, CHUNK), lambda i: (0, count - 1 - i)),
-            pl.BlockSpec((STEP_ROWS, CHUNK), lambda i: (0, count - 1 - i)),
-            pl.BlockSpec((8, all_w), fixed),
-            pl.BlockSpec((8, LANES), fixed),
-        ],
-        out_shape=[
-            jax.ShapeDtypeStruct((length, 2 * width), bf16),
-            jax.ShapeDtypeStruct((2 * N_STATE, length), bf16),
-            jax.ShapeDtypeStruct((STEP_ROWS, length), bf16),
-            jax.ShapeDtypeStruct((8, all_w), f32),
-            jax.ShapeDtypeStruct((8, LANES), f32),
-        ],
+        in_specs=in_specs,
+        out_specs=[spec for spec, _, _ in outs],
+        out_shape=[jax.ShapeDtypeStruct(shape, dtype) for _, shape, dtype in outs],
         scratch_shapes=[
             pltpu.VMEM((N_STATE, width), f32),
-            pltpu.VMEM((CHUNK + 8, all_w), f32),
-            pltpu.VMEM((CHUNK + 8, all_w), f32),
+            pltpu.VMEM((CHUNK + 8, cat_w), f32),
+            pltpu.VMEM((CHUNK + 8, dcat_w), f32),
         ],
         cost_estimate=pl.CostEstimate(
-            flops=0, bytes_accessed=160_000_000, transcendentals=0
+            flops=0, bytes_accessed=30_000_000 * (heads + 1), transcendentals=0
         ),
-        name="mixer_backward",
-    )(main, small, main, small, head, taps, y, states, dgated)
+        name="mixer_backward_last" if is_last else "mixer_backward_first",
+    )(*args)
 
 
 MESH = pl.DeviceIdType.MESH
@@ -664,9 +708,15 @@
     return lax.ppermute(x, "wshard", [(i, (i + j) % n_wsh) for i in range(n_wsh)])
 
 
-def adam_kernel(count, g_ref, ext_ref, p_ref, m_ref, v_ref, grad_ref, *out_refs):
+def two_groups(heads):
+    return heads % 2 == 0 and heads >= 4 and (heads - 2) % 2 == 0
+
+
+def adam_kernel(count, groups, *refs):
+    g_refs, (ext_ref, p_ref, m_ref, v_ref, grad_ref, *out_refs) = refs[:groups], refs[groups:]
     at_ext = pl.program_id(0) == count
-    grad = jnp.where(at_ext, ext_ref[...].astype(f32), g_ref[0].astype(f32))
+    own = jnp.concatenate([ref[0] for ref in g_refs], axis=1)
+    grad = jnp.where(at_ext, ext_ref[...].astype(f32), own.astype(f32))
     grad_ref[...] = grad
     news = adamw(
         p_ref[...], grad, m_ref[...], v_ref[...], weight_learning_rate, matrix_decay
@@ -676,13 +726,17 @@
 
 
 def adam_in(g_main, g_ext, param, first, second):
-    count, rows, cols = g_main.shape
+    count, rows = g_main[0].shape[:2]
+    cols = g_ext.shape[1]
     wide = pl.BlockSpec((rows, cols), lambda i: (0, i))
     return pl.pallas_call(
-        functools.partial(adam_kernel, count),
+        functools.partial(adam_kernel, count, len(g_main)),
         grid=(count + 1,),
         in_specs=[
-            pl.BlockSpec((1, rows, cols), lambda i: (jnp.minimum(i, count - 1), 0, 0)),
+            *(
+                pl.BlockSpec((1,) + g.shape[1:], lambda i: (jnp.minimum(i, count - 1), 0, 0))
+                for g in g_main
+            ),
             pl.BlockSpec((rows, cols), lambda i: (0, 0)),
             wide,
             wide,
@@ -691,7 +745,7 @@
         out_specs=[wide] * 4,
         out_shape=[jax.ShapeDtypeStruct(param.shape, f32)] * 4,
         name="adam_in",
-    )(g_main, g_ext, param, first, second)
+    )(*g_main, g_ext, param, first, second)
 
 
 def local(
@@ -794,23 +848,40 @@
     mixed = mm(gnormed, w_out, NN).astype(bf16)
     g_out, mixed, d_gated = lax.optimization_barrier((g_out, mixed, d_gated))
     mixed = lax.psum_scatter(mixed, "seq", scatter_dimension=0, tiled=True)
-    grad_out_weight = lax.dynamic_slice_in_dim(g_out, wsh_index * rows_out, rows_out, 0)
+    out_parts = [lax.dynamic_slice_in_dim(g_out, wsh_index * rows_out, rows_out, 0)]
     for j in range(1, n_wsh):
         to = lax.rem(wsh_index + j, n_wsh)
         part = lax.dynamic_slice_in_dim(g_out, to * rows_out, rows_out, 0)
-        grad_out_weight = grad_out_weight + shift(part, j, n_wsh)
-    dmain, dshared_t, dstep_t, dtaps, dhead = mixer_backward(
-        main, small, head, taps, y, states, d_gated, heads
-    )
-
-    g_main = mm(normed_all, dmain, TN)
-    d_gain_part = jnp.sum(g_main * w_main.astype(f32), axis=1)
-    g_main = g_main.astype(bf16).reshape(n_seq, n_wsh, rows_in, 2 * width)
-    g_parts = [lax.dynamic_index_in_dim(g_main, wsh_index, 1, keepdims=False)]
-    for j in range(1, n_wsh):
-        to = lax.rem(wsh_index + j, n_wsh)
-        part = lax.dynamic_index_in_dim(g_main, to, 1, keepdims=False)
-        g_parts.append(shift(part, j, n_wsh))
+        out_parts.append(shift(part, j, n_wsh))
+
+    def send_grad(d_part):
+        grad = mm(normed_all, d_part, TN)
+        blocks = grad.astype(bf16).reshape(n_seq, n_wsh, rows_in, grad.shape[1])
+        got = [lax.dynamic_index_in_dim(blocks, wsh_index, 1, keepdims=False)]
+        for j in range(1, n_wsh):
+            to = lax.rem(wsh_index + j, n_wsh)
+            part = lax.dynamic_index_in_dim(blocks, to, 1, keepdims=False)
+            got.append(shift(part, j, n_wsh))
+        return grad, got
+
+    back_args = (main, small, head, taps, y, states, d_gated)
+    if two_groups(heads):
+        early = heads - 2
+        d_first, step_a, taps_a, head_a, dbc = mixer_backward(*back_args, early, 0, None)
+        grad_a, got_a = send_grad(d_first)
+        d_last, step_b, taps_b, head_b, dshared_t, dmain = mixer_backward(
+            *back_args, 2, early, (d_first, dbc)
+        )
+        dstep_t = step_a + step_b
+        dhead = head_a + head_b
+        dtaps = jnp.concatenate(
+            [taps_b[:, : 2 * N_STATE], taps_a, taps_b[:, 2 * N_STATE :]], axis=1
+        )
+    else:
+        d_last, dstep_t, dtaps, dhead, dshared_t = mixer_backward(
+            *back_args, heads, 0, None
+        )
+        dmain = d_last
 
     (shared_parts,) = swap(
         (dshared_t.reshape(n_seq, share, -1),), ((0, "seq"),), n_seq, n_wsh, 2
@@ -820,7 +891,9 @@
     d_normed = mm(dmain, w_main, NT) + lax.dot_general(
         d_ext, w_ext, (((0,), (1,)), ((), ())), preferred_element_type=f32
     )
-    d_normed, mixed = lax.optimization_barrier((d_normed.astype(bf16), mixed))
+    d_normed, mixed, d_last = lax.optimization_barrier(
+        (d_normed.astype(bf16), mixed, d_last)
+    )
     block_out = (inputs + mixed.astype(f32))[None]
     d_normed = lax.psum_scatter(d_normed, "seq", scatter_dimension=0, tiled=True)
     d_normed = d_normed.astype(f32)
@@ -831,10 +904,25 @@
         - inputs * rms_in**3 * jnp.mean(scaled_in * inputs, axis=-1, keepdims=True)
     )[None]
 
+    grad_b, got_b = send_grad(d_last)
+    if two_groups(heads):
+        grad_b, d_ext, out_parts, got_a = lax.optimization_barrier(
+            (grad_b, d_ext, out_parts, got_a)
+        )
+    grad_out_weight = sum(out_parts)
     g_ext = lax.dot_general(
         normed_all, d_ext, (((0,), (1,)), ((), ())), preferred_element_type=f32
     )
-    d_gain_part = d_gain_part + jnp.sum(g_ext * w_ext.astype(f32), axis=1)
+    d_gain_part = jnp.sum(g_ext * w_ext.astype(f32), axis=1)
+    if two_groups(heads):
+        grads, got = [grad_a, grad_b], [got_a, got_b]
+    else:
+        grads, got = [grad_b], [got_b]
+    first = 0
+    for grad in grads:
+        part = w_main[:, first : first + grad.shape[1]].astype(f32)
+        d_gain_part = d_gain_part + jnp.sum(grad * part, axis=1)
+        first += grad.shape[1]
     g_ext = jnp.pad(g_ext.astype(bf16), ((0, 0), (0, -g_ext.shape[1] % LANES)))
     g_ext = g_ext.reshape(n_seq, n_wsh, rows_in, LANES)
 
@@ -865,15 +953,9 @@
     grad_conv_inner = jnp.swapaxes(sums[3], 0, 1).reshape(conv_inner.shape)
     grad_head_params = jnp.swapaxes(sums[4], 0, 1).reshape(head_params.shape)
 
-    g_main = g_parts[0].astype(f32)
-    for part in g_parts[1:]:
-        g_main = g_main + part.astype(f32)
-    g_main, g_ext = swap(
-        (g_main.astype(bf16), g_ext.astype(bf16)),
-        ((0, "seq"), (0, "seq")),
-        n_seq,
-        n_wsh,
-        5,
+    sums = [sum(part.astype(f32) for part in parts).astype(bf16) for parts in got]
+    *g_main, g_ext = swap(
+        (*sums, g_ext.astype(bf16)), ((0, "seq"),) * (len(sums) + 1), n_seq, n_wsh, 5
     )
     g_ext = jnp.swapaxes(g_ext, 0, 1)
     g_ext = jnp.concatenate(

time: 428 us -> 465 us (1.086)
  waiting for transfers between devices: 76.8 us -> 94.1 us
  Pallas kernels: 196 us -> 209 us
  starting transfers between devices: 24.2 us -> 18.3 us
    pallas_call x2 -> x3, Pallas kernels: 54.8 us -> 77.3 us  [the longest x2 68.9 us: mixer_backward(): pl.pallas_call(functools.partial(bwd_kernel, heads, offset, count, has_be...]
    ppermute x9 -> x12, waiting for transfers between devices: 76 us -> 93.4 us  [shift(): lax.ppermute(x, 'wshard', [(i, (i + j) % n_wsh) for i in range(n_wsh)])]
    pallas_call x4, Pallas kernels: 56.9 us -> 46.8 us  [swap(): pl.pallas_call(functools.partial(swap_kernel, plan, n_seq, n_wsh), in_spe...]
    ppermute x9 -> x12, starting transfers between devices: 24.1 us -> 18.2 us  [shift(): lax.ppermute(x, 'wshard', [(i, (i + j) % n_wsh) for i in range(n_wsh)])]
    dot_general x8 -> x9, matrix products: 58.9 us -> 62.7 us  [mm(): return lax.dot_general(a, b, dims, preferred_element_type=f32)]
  transfers between devices with their start and end apart: 13 -> 16, of which waited for: 5 -> 4; matrix products, arithmetic and copies ran while one was open for 18% -> 19% of each run, Pallas kernels for 44% -> 44%
where the time goes in v4:
time: 465 us; the launch traced here: 460 us
  Pallas kernels  209 us (45%)
  waiting for transfers between devices  94.1 us (20%)
  matrix products  68.9 us (15%)
  other arithmetic  33.8 us (7%)
  local copies, waits for them, and re-layouts  20.5 us (4%)
  starting transfers between devices  18.3 us (4%)
  between operations  15.1 us (3%)
    ppermute x12, waiting for transfers between devices, shift(): lax.ppermute(x, 'wshard', [(i, (i + j) % n_wsh) for i in range(n_wsh)])  93.4 us
    pallas_call x2, Pallas kernels, mixer_backward(): pl.pallas_call(functools.partial(bwd_kernel, heads, offset, count, has_be...  68.9 us
    dot_general x9, matrix products, mm(): return lax.dot_general(a, b, dims, preferred_element_type=f32)  62.7 us
    pallas_call x1, Pallas kernels, spread_weights(): pl.pallas_call(functools.partial(weights_kernel, n_seq, n_wsh), in_specs=...  57.2 us
    pallas_call x4, Pallas kernels, swap(): pl.pallas_call(functools.partial(swap_kernel, plan, n_seq, n_wsh), in_spe...  46.8 us
    pallas_call x1, Pallas kernels, mixer_forward(): pl.pallas_call(functools.partial(fwd_kernel, heads), grid=(count,), in_sp...  20.3 us
    ppermute x12, starting transfers between devices, shift(): lax.ppermute(x, 'wshard', [(i, (i + j) % n_wsh) for i in range(n_wsh)])  18.2 us
  transfers between devices with their start and end apart: 16, of which 4 were waited for; matrix products, arithmetic and copies ran while one was open for 19% of the time, Pallas kernels for 44%

profile of v4, /device:TPU:0, one launch (start us, length us, event | category | flops | bytes accessed | tf_op | source)
XLA Modules:
  0.0 459.7 jit_solution(12661523815148830609)
XLA Ops:
  7.3 1.5 fusion.13
  9.9 2.3 fusion.15
  12.2 0.7 all-gather.6.cloned.1.call-update
  13.3 0.9 copy.112
  14.8 57.2 %spread_weights.1 = (bf16[8,4,48,768]{3,2,1,0:T(8,128)(2,1)}, bf16[8,4,48,384]{3,2,1,0:T(8,128)(2,1)}) custom-call(bf16[8,48,768]{2,1,0:T(8,128)(2,1)} %bitcast.122, bf16[48,384]{1,0:T(8,128)(2,1)} %pad.24.small), custom_call_target="tpu_custom_call" | custom-call | bytes 200000000 | tf_op jit(solution)/shard_map/spread_weights/pallas_call | solution.py:539
  72.0 3.3 collective-permute-start.2
  76.1 0.8 copy.88
  76.9 0.8 dynamic_slice.49
  78.3 0.7 constant_dynamic-slice_fusion.4
  79.8 16.2 %collective-permute-done = bf16[96,1536]{1,0:T(8,128)(2,1)} collective-permute-done((bf16[96,1536]{1,0:T(8,128)(2,1)S(1)}, bf16[96,1536]{1,0:T(8,128)(2,1)}, u32[]{:S(2)}, u32[]{:S(2)}) %collective-permute-start) | collective-permute-done | bytes 294944 | tf_op jit(solution)/shard_map/ppermute | solution.py:708
  96.0 1.0 bitcast_dynamic-update-slice_fusion.2
  97.0 3.1 collective-permute-done.1
  100.3 8.5 %convolution_convert_fusion.2.small_ref.refs_1_.refs_3_ = bf16[2048,384]{1,0:T(8,128)(2,1)} fusion(bf16[2048,1536]{1,0:T(8,128)(2,1)} %all-gather.4.cloned.1.call-done, bf16[1536,384]{1,0:T(8,128)(2,1)S(1)} %bitcast.129, bf16[384,128]{1,0:T(8,128)(2,1)} %copy.88, bf16[384,256]{1,0:T(8,128)(2,1)S(1)} %select_convert_fusion), kind=kOutput, calls=%fused_computation.28 | convolution fusion | flops 2870870016 | bytes 9338880 | tf_op jit(solution)/shard_map/dot_general | solution.py:35
  108.8 9.5 %convolution_convert_fusion.1.main_ref.refs_0_.refs_2_ = bf16[2048,768]{1,0:T(8,128)(2,1)} fusion(bf16[2048,1536]{1,0:T(8,128)(2,1)} %all-gather.4.cloned.1.call-done, bf16[1536,768]{1,0:T(8,128)(2,1)} %bitcast.143), kind=kOutput, calls=%fused_computation.11 | convolution fusion | flops 4833411072 | bytes 11796480 | tf_op jit(solution)/shard_map/dot_general | solution.py:35
  118.3 20.3 %mixer_forward.1 = (bf16[2048,384]{1,0:T(8,128)(2,1)}, f32[2048,384]{1,0:T(8,128)}, f32[16,128,384]{2,1,0:T(8,128)}) custom-call(bf16[2048,768]{1,0:T(8,128)(2,1)} %convolution_convert_fusion.1.main_ref.refs_0_.refs_2_, bf16[2048,384]{1,0:T(8,128)(2,1)} %convolution_convert_fusion.2.small_ref.refs_1_.refs_3_, f32[8,128]{1,0:T(8,128)} %pad.25.head_ref.refs_4_, ...), custom_call_target="tpu_custom_call" | custom-call | bytes 70000000 | tf_op jit(solution)/shard_map/mixer_forward/pallas_call | solution.py:193
  138.5 7.1 %fusion.4 = (f32[2048]{0:T(1024)S(1)}, f32[2048]{0:T(1024)S(1)}, f32[384,2048]{0,1:T(8,128)S(1)}) fusion(bf16[2048,384]{1,0:T(8,128)(2,1)} %get-tuple-element.79, f32[384]{0:T(512)S(1)} %dynamic_slice.49, bf16[384,1536]{1,0:T(8,128)(2,1)} %bitcast.126, bf16[1,2048,1536]{2,1,0:T(8,128)(2,1)} %all-gather.6.cloned.1.call-done), kind=kOutput, calls=%fused_computation.12 | convolution fusion | flops 2420633600 | bytes 12207616 | tf_op jit(solution)/shard_map/dot_general | solution.py:35
  146.3 7.3 %sum_over_seq.1 = f32[32,128]{1,0:T(8,128)} custom-call(f32[32,128]{1,0:T(8,128)} %reshape.186.x_ref), custom_call_target="tpu_custom_call" | custom-call | tf_op jit(solution)/shard_map/sum_over_seq/pallas_call | solution.py:681
  153.6 0.7 multiply_multiply_fusion.5
  154.3 0.7 multiply_bitcast_fusion
  155.1 7.9 %convolution_convert_fusion = bf16[2048,1536]{1,0:T(8,128)(2,1)} fusion(bf16[384,1536]{1,0:T(8,128)(2,1)} %bitcast.127, bf16[2048,384]{1,0:T(8,128)(2,1)} %get-tuple-element.79, f32[2048]{0:T(1024)S(1)} %get-tuple-element.159, f32[384]{0:T(512)S(1)} %dynamic_slice.49), kind=kOutput, calls=%fused_computation.1 | convolution fusion | flops 2422210560 | bytes 9053696 | tf_op jit(solution)/shard_map/dot_general | solution.py:35
  163.0 4.0 fusion.12
  167.0 5.1 %fusion = f32[384,1536]{1,0:T(8,128)S(1)} fusion(bf16[1,2048,1536]{2,1,0:T(8,128)(2,1)} %all-gather.6.cloned.1.call-done, bf16[2048,384]{1,0:T(8,128)(2,1)S(1)} %copy-done.6, f32[2048]{0:T(1024)S(1)} %get-tuple-element.159, f32[384]{0:T(512)S(1)} %dynamic_slice.49), kind=kOutput, calls=%fused_computation.2 | convolution fusion | flops 2419064832 | bytes 10233344 | tf_op jit(solution)/shard_map/dot_general | solution.py:35
  174.1 1.7 convolution_convert_fusion.4
  175.9 41.8 %mixer_backward_first.1 = (bf16[2048,512]{1,0:T(8,128)(2,1)}, bf16[16,2048]{1,0:T(8,128)(2,1)}, f32[8,256]{1,0:T(8,128)}, f32[8,128]{1,0:T(8,128)}, f32[2048,256]{1,0:T(8,128)}) custom-call(bf16[2048,768]{1,0:T(8,128)(2,1)} %convolution_convert_fusion.1.main_ref.refs_0_.refs_2_, bf16[2048,384]{1,0:T(8,128)(2,1)} %convolution_convert_fusion.2.small_ref.refs_1_.refs_3_, ...), custom_call_target="tpu_custom_call" | custom-call | bytes 150000000 | tf_op jit(solution)/shard_map/mixer_backward_first/pallas_call | solution.py:431
  217.7 27.1 %mixer_backward_last.1 = (bf16[2048,256]{1,0:T(8,128)(2,1)}, bf16[16,2048]{1,0:T(8,128)(2,1)}, f32[8,384]{1,0:T(8,128)}, f32[8,128]{1,0:T(8,128)}, bf16[256,2048]{1,0:T(8,128)(2,1)}, /*index=5*/bf16[2048,768]{1,0:T(8,128)(2,1)}) custom-call(bf16[2048,768]{1,0:T(8,128)(2,1)} %convolution_convert_fusion.1.main_ref.refs_0_.refs_2_, ...), custom_call_target="tpu_custom_call" | custom-call | bytes 90000000 | tf_op jit(solution)/shard_map/mixer_backward_last/pallas_call | solution.py:431
  244.8 14.3 %shard_map.462 = bf16[8,32,2048]{2,1,0:T(8,128)(2,1)} custom-call(bf16[8,32,2048]{2,1,0:T(8,128)(2,1)} %bitcast.130), custom_call_target="tpu_custom_call" | custom-call | tf_op jit(solution)/shard_map/pallas_call | solution.py:646
  259.2 1.4 reduce_sum.137
  260.6 7.8 %fusion.58 = f32[2048,1536]{1,0:T(8,128)S(1)} fusion(bf16[2048,768]{1,0:T(8,128)(2,1)} %get-tuple-element.84, bf16[1536,768]{1,0:T(8,128)(2,1)} %bitcast.144), kind=kOutput, calls=%fused_computation.143 | convolution fusion | flops 4831838208 | bytes 18087936 | tf_op jit(solution)/shard_map/dot_general | solution.py:35
  268.5 4.5 add_convert_fusion
  273.0 0.7 slice.89
  273.7 8.0 %multiply_reduce_fusion = (f32[1536]{0:T(1024)}, bf16[1536,512]{1,0:T(8,128)(2,1)S(1)}) fusion(bf16[1536,768]{1,0:T(8,128)(2,1)} %bitcast.145, bf16[2048,1536]{1,0:T(8,128)(2,1)} %all-gather.4.cloned.1.call-done, bf16[2048,512]{1,0:T(8,128)(2,1)} %get-tuple-element.82.refs_9_), kind=kOutput, calls=%fused_computation.27 | convolution fusion | flops 3224369664 | bytes 11540480 | tf_op jit(solution)/shard_map/dot_general | solution.py:35
  281.8 1.0 dynamic-slice_bitcast_fusion
  282.9 1.3 constant_dynamic-slice_fusion
  284.2 5.6 %collective-permute-start.5 = (f32[96,1536]{1,0:T(8,128)}, f32[96,1536]{1,0:T(8,128)S(1)}, u32[]{:S(2)}, u32[]{:S(2)}) collective-permute-start(f32[96,1536]{1,0:T(8,128)} %get-tuple-element.143), channel_id=1, source_target_pairs={{0,3},{1,0},{2,1},{3,2},{4,7},{5,4},{6,5},{7,6},{8,11},{9,8},{10,9... | collective-permute-start | bytes 1769480 | tf_op jit(solution)/shard_map/ppermute | solution.py:708
  291.7 0.7 fusion.47
  293.2 2.3 collective-permute-start.7
  295.5 0.9 pad_maximum_fusion
  296.5 1.7 collective-permute-start.6
  298.1 7.0 %fusion.57 = (bf16[1536,256]{1,0:T(8,128)(2,1)}, f32[1536,256]{1,0:T(8,128)S(1)}) fusion(bf16[2048,1536]{1,0:T(8,128)(2,1)} %all-gather.4.cloned.1.call-done, bf16[2048,256]{1,0:T(8,128)(2,1)} %get-tuple-element.92), kind=kOutput, calls=%fused_computation.142 | convolution fusion | flops 1611005952 | bytes 9699328 | tf_op jit(solution)/shard_map/dot_general | solution.py:35
  305.1 67.2 %collective-permute-done.7 = bf16[8,48,512]{2,1,0:T(8,128)(2,1)S(1)} collective-permute-done((bf16[8,48,512]{2,1,0:T(8,128)(2,1)}, bf16[8,48,512]{2,1,0:T(8,128)(2,1)S(1)}, u32[]{:S(2)}, u32[]{:S(2)}) %collective-permute-start.7) | collective-permute-done | bytes 393248 | tf_op jit(solution)/shard_map/ppermute | solution.py:708
  372.3 1.8 multiply_reduce_fusion.2
  374.2 1.2 copy.106
  375.4 0.8 pad.27.clone
  376.2 1.5 multiply_reduce_fusion.1
  378.6 14.9 %shard_map.463 = (bf16[4,8,48,128]{3,2,1,0:T(8,128)(2,1)}, f32[4,48,128]{2,1,0:T(8,128)}) custom-call(bf16[8,4,48,128]{3,2,1,0:T(8,128)(2,1)} %bitcast.124, f32[48,128]{1,0:T(8,128)} %pad_bitcast_fusion.refs_1_), custom_call_target="tpu_custom_call" | custom-call | tf_op jit(solution)/shard_map/pallas_call | solution.py:646
  393.4 1.5 reduce_sum.145.refs_0_
  394.9 5.9 %shard_map.465 = f32[8,48,128]{2,1,0:T(8,128)} custom-call(f32[48,128]{1,0:T(8,128)} %reduce_sum.145.refs_0_), custom_call_target="tpu_custom_call" | custom-call | tf_op jit(solution)/shard_map/pallas_call | solution.py:646
  400.9 1.0 copy.113
  401.9 1.8 reduce_sum.144.refs_2_
  405.3 0.9 collective-permute-start.9
  406.1 3.0 collective-permute-start.11
  409.8 1.3 multiply_subtract_fusion.4
  411.8 2.2 add_convert_fusion.1.refs_0_
  414.1 3.0 multiply_subtract_fusion
  417.1 0.8 multiply_subtract_fusion.1
  418.4 6.8 %collective-permute-done.10 = bf16[8,48,256]{2,1,0:T(8,128)(2,1)S(1)} collective-permute-done((bf16[8,48,256]{2,1,0:T(8,128)(2,1)S(1)}, bf16[8,48,256]{2,1,0:T(8,128)(2,1)S(1)}, u32[]{:S(2)}, u32[]{:S(2)}) %collective-permute-start.10) | collective-permute-done | bytes 196640 | tf_op jit(solution)/shard_map/ppermute | solution.py:708
  425.2 0.8 fusion.26.refs_1_
  426.0 11.7 %shard_map.464 = (bf16[8,48,512]{2,1,0:T(8,128)(2,1)}, bf16[8,48,256]{2,1,0:T(8,128)(2,1)}, bf16[8,48,128]{2,1,0:T(8,128)(2,1)}) custom-call(bf16[8,48,512]{2,1,0:T(8,128)(2,1)} %add_convert_fusion.1.refs_0_, bf16[8,48,256]{2,1,0:T(8,128)(2,1)} %fusion.26.refs_1_, bf16[8,48,128]{2,1,0:T(8,128)(2,1)} %reduce_sum.144.refs_2_), custom_call_target="tpu_custom_call" | custom-call | tf_op jit(solution)/shard_map/pallas_call | solution.py:646
  437.7 1.0 slice.112
  438.7 0.9 copy.96
  440.0 0.7 fusion.38.refs_2_
  440.6 8.3 %adam_in.1 = (f32[48,6448]{1,0:T(8,128)}, f32[48,6448]{1,0:T(8,128)}, f32[48,6448]{1,0:T(8,128)}, f32[48,6448]{1,0:T(8,128)}) custom-call(bf16[8,48,512]{2,1,0:T(8,128)(2,1)} %get-tuple-element.105.refs_0_, bf16[8,48,256]{2,1,0:T(8,128)(2,1)} %get-tuple-element.106.refs_1_, bf16[48,768]{1,0:T(8,128)(2,1)} %fusion.38.refs_2_, f32[48,6448]{1,0:T(8,128)} %refs_3_.1, ...), custom_call_target="tpu_custom_call" | custom-call | tf_op jit(solution)/shard_map/adam_in/pallas_call | solution.py:732
  449.0 1.5 fusion.20
  450.6 2.3 fusion.19
  (208 shorter events, 14.4 us)
Async XLA Ops:
  7.2 5.8 %copy-start.1 = (f32[48,6448]{1,0:T(8,128)S(1)}, f32[48,6448]{1,0:T(8,128)}, u32[]{:S(2)}) copy-start(f32[48,6448]{1,0:T(8,128)} %refs_3_.1) | copy-start | bytes 3714052
  7.2 93.1 %all-gather.4.cloned.1.call-start = ((), (), s32[]{:S(2)}) async-start(), calls=%async_computation.2 | async-start | bytes 7077888 | tf_op jit(solution)/shard_map/all_gather | solution.py:791
  12.2 126.3 %all-gather.6.cloned.1.call-start = ((), (), s32[]{:S(2)}) async-start(), calls=%async_computation.5 | async-start | bytes 7077888 | tf_op jit(solution)/shard_map/all_gather | solution.py:793
  13.0 260.0 %reduce-scatter.3.cloned.1.call-start = ((), (), s32[]{:S(2)}) async-start(), calls=%async_computation.3 | async-start | bytes 7077888 | tf_op jit(solution)/shard_map/reduce_scatter | solution.py:850
  13.1 64.5 %copy-start.45 = (f32[3,48]{1,0:T(4,128)S(1)}, f32[3,48]{1,0:T(4,128)}, u32[]{:S(2)}) copy-start(f32[3,48]{1,0:T(4,128)} %param.31) | copy-start | bytes 1732
  13.1 65.9 %copy-start.28 = (f32[5,256]{1,0:T(8,128)S(1)}, f32[5,256]{1,0:T(8,128)}, u32[]{:S(2)}) copy-start(f32[5,256]{1,0:T(8,128)} %param.30) | copy-start | bytes 15364
  72.0 28.2 %collective-permute-start.2 = (bf16[96,1536]{1,0:T(8,128)(2,1)S(1)}, bf16[96,1536]{1,0:T(8,128)(2,1)S(1)}, u32[]{:S(2)}, u32[]{:S(2)}) collective-permute-start(bf16[96,1536]{1,0:T(8,128)(2,1)S(1)} %convert_element_type.123), channel_id=1, source_target_pairs={{0,3},{1,0},{2,1},{3,2},{4,7},{5,4},{6,5},{7,6},{8,11},{9,8},{10,9... | collective-permute-start | bytes 884744 | tf_op jit(solution)/shard_map/ppermute | solution.py:708
  75.3 24.8 %collective-permute-start.1 = (bf16[96,1536]{1,0:T(8,128)(2,1)S(1)}, bf16[96,1536]{1,0:T(8,128)(2,1)S(1)}, u32[]{:S(2)}, u32[]{:S(2)}) collective-permute-start(bf16[96,1536]{1,0:T(8,128)(2,1)S(1)} %convert_element_type.123), channel_id=1, source_target_pairs={{0,2},{1,3},{2,0},{3,1},{4,6},{5,7},{6,4},{7,5},{8,10},{9,11},{10,... | collective-permute-start | bytes 884744 | tf_op jit(solution)/shard_map/ppermute | solution.py:708
  75.3 20.7 %collective-permute-start = (bf16[96,1536]{1,0:T(8,128)(2,1)S(1)}, bf16[96,1536]{1,0:T(8,128)(2,1)}, u32[]{:S(2)}, u32[]{:S(2)}) collective-permute-start(bf16[96,1536]{1,0:T(8,128)(2,1)S(1)} %convert_element_type.123), channel_id=1, source_target_pairs={{0,1},{1,2},{2,3},{3,0},{4,5},{5,6},{6,7},{7,4},{8,9},{9,10},{10,1... | collective-permute-start | bytes 884744 | tf_op jit(solution)/shard_map/ppermute | solution.py:708
  76.0 24.3 %copy-start.9 = (bf16[8,4,48,384]{3,2,1,0:T(8,128)(2,1)S(1)}, bf16[8,4,48,384]{3,2,1,0:T(8,128)(2,1)}, u32[]{:S(2)}) copy-start(bf16[8,4,48,384]{3,2,1,0:T(8,128)(2,1)} %get-tuple-element.76) | copy-start | bytes 3538948
  100.2 8.6 %copy-start.8 = (bf16[4,96,1536]{2,1,0:T(8,128)(2,1)}, bf16[4,96,1536]{2,1,0:T(8,128)(2,1)S(1)}, u32[]{:S(2)}) copy-start(bf16[4,96,1536]{2,1,0:T(8,128)(2,1)S(1)} %bitcast_dynamic-update-slice_fusion) | copy-start | bytes 3538948
  163.0 4.0 copy-start.6
  172.1 276.9 %reduce-scatter.5.cloned.1.call-start = ((), (), s32[]{:S(2)}) async-start(), calls=%async_computation.4 | async-start | bytes 7077888 | tf_op jit(solution)/shard_map/reduce_scatter | solution.py:898
  244.8 15.8 %copy-start.24 = (bf16[16,2048]{1,0:T(8,128)(2,1)S(1)}, bf16[16,2048]{1,0:T(8,128)(2,1)}, u32[]{:S(2)}) copy-start(bf16[16,2048]{1,0:T(8,128)(2,1)} %get-tuple-element.86) | copy-start | bytes 196612
  244.8 15.8 %copy-start.25 = (bf16[16,2048]{1,0:T(8,128)(2,1)S(1)}, bf16[16,2048]{1,0:T(8,128)(2,1)}, u32[]{:S(2)}) copy-start(bf16[16,2048]{1,0:T(8,128)(2,1)} %get-tuple-element.87) | copy-start | bytes 196612
  260.6 7.9 %copy-start.7 = (bf16[32,2048]{1,0:T(8,128)(2,1)}, bf16[32,2048]{1,0:T(8,128)(2,1)S(1)}, u32[]{:S(2)}) copy-start(bf16[32,2048]{1,0:T(8,128)(2,1)S(1)} %reduce_sum.137) | copy-start | bytes 393220
  273.7 10.4 %copy-start.27 = (f32[8,128]{1,0:T(8,128)}, f32[8,128]{1,0:T(8,128)S(1)}, u32[]{:S(2)}) copy-start(f32[8,128]{1,0:T(8,128)S(1)} %slice.89) | copy-start | bytes 12292
  282.8 7.6 %copy-start.49 = (f32[8,128]{1,0:T(8,128)S(1)}, f32[8,128]{1,0:T(8,128)}, u32[]{:S(2)}) copy-start(f32[8,128]{1,0:T(8,128)} %get-tuple-element.102) | copy-start | bytes 12292
  282.8 7.6 %copy-start.50 = (f32[8,128]{1,0:T(8,128)S(1)}, f32[8,128]{1,0:T(8,128)}, u32[]{:S(2)}) copy-start(f32[8,128]{1,0:T(8,128)} %get-tuple-element.103) | copy-start | bytes 12292
  282.8 13.6 %collective-permute-start.8 = (bf16[8,48,512]{2,1,0:T(8,128)(2,1)}, bf16[8,48,512]{2,1,0:T(8,128)(2,1)}, u32[]{:S(2)}, u32[]{:S(2)}) collective-permute-start(bf16[8,48,512]{2,1,0:T(8,128)(2,1)} %get-tuple-element.147), channel_id=1, source_target_pairs={{0,3},{1,0},{2,1},{3,2},{4,7},{5,4},{6,5},{7,6},{8,11},{9,8},{10,9... | collective-permute-start | bytes 1179656 | tf_op jit(solution)/shard_map/ppermute | solution.py:708
  284.2 88.1 %collective-permute-start.5 = (f32[96,1536]{1,0:T(8,128)}, f32[96,1536]{1,0:T(8,128)S(1)}, u32[]{:S(2)}, u32[]{:S(2)}) collective-permute-start(f32[96,1536]{1,0:T(8,128)} %get-tuple-element.143), channel_id=1, source_target_pairs={{0,3},{1,0},{2,1},{3,2},{4,7},{5,4},{6,5},{7,6},{8,11},{9,8},{10,9... | collective-permute-start | bytes 1769480 | tf_op jit(solution)/shard_map/ppermute | solution.py:708
  289.8 82.5 %collective-permute-start.4 = (f32[96,1536]{1,0:T(8,128)}, f32[96,1536]{1,0:T(8,128)}, u32[]{:S(2)}, u32[]{:S(2)}) collective-permute-start(f32[96,1536]{1,0:T(8,128)} %get-tuple-element.144), channel_id=1, source_target_pairs={{0,2},{1,3},{2,0},{3,1},{4,6},{5,7},{6,4},{7,5},{8,10},{9,11},{10,... | collective-permute-start | bytes 1769480 | tf_op jit(solution)/shard_map/ppermute | solution.py:708
  289.8 82.5 %collective-permute-start.3 = (f32[96,1536]{1,0:T(8,128)}, f32[96,1536]{1,0:T(8,128)}, u32[]{:S(2)}, u32[]{:S(2)}) collective-permute-start(f32[96,1536]{1,0:T(8,128)} %get-tuple-element.145), channel_id=1, source_target_pairs={{0,1},{1,2},{2,3},{3,0},{4,5},{5,6},{6,7},{7,4},{8,9},{9,10},{10,1... | collective-permute-start | bytes 1769480 | tf_op jit(solution)/shard_map/ppermute | solution.py:708
  293.2 79.1 %collective-permute-start.7 = (bf16[8,48,512]{2,1,0:T(8,128)(2,1)}, bf16[8,48,512]{2,1,0:T(8,128)(2,1)S(1)}, u32[]{:S(2)}, u32[]{:S(2)}) collective-permute-start(bf16[8,48,512]{2,1,0:T(8,128)(2,1)} %get-tuple-element.148), channel_id=1, source_target_pairs={{0,2},{1,3},{2,0},{3,1},{4,6},{5,7},{6,4},{7,5},{8,10},{9,11},{10,... | collective-permute-start | bytes 1179656 | tf_op jit(solution)/shard_map/ppermute | solution.py:708
  296.4 75.9 %slice-start = ((s8[6291456]{0:T(1024)(128)(4,1)}), s8[4194304]{0:T(1024)(128)(4,1)S(1)}, s32[]{:S(2)}) async-start(s8[6291456]{0:T(1024)(128)(4,1)} %bitcast.120), calls=%async_computation.6 | async-start | bytes 8388608
  296.4 75.9 %slice-start.1 = ((s8[6291456]{0:T(1024)(128)(4,1)}), s8[2097152]{0:T(1024)(128)(4,1)S(1)}, s32[]{:S(2)}) async-start(s8[6291456]{0:T(1024)(128)(4,1)} %bitcast.120), calls=%async_computation.7 | async-start | bytes 4194304
  296.5 75.8 %collective-permute-start.6 = (bf16[8,48,512]{2,1,0:T(8,128)(2,1)}, bf16[8,48,512]{2,1,0:T(8,128)(2,1)S(1)}, u32[]{:S(2)}, u32[]{:S(2)}) collective-permute-start(bf16[8,48,512]{2,1,0:T(8,128)(2,1)} %get-tuple-element.149), channel_id=1, source_target_pairs={{0,1},{1,2},{2,3},{3,0},{4,5},{5,6},{6,7},{7,4},{8,9},{9,10},{10,1... | collective-permute-start | bytes 1179656 | tf_op jit(solution)/shard_map/ppermute | solution.py:708
  372.3 1.9 copy-start.17
  374.2 3.7 copy-start.34
  374.2 3.7 copy-start.47
  374.2 3.7 copy-start.33
  374.2 3.7 copy-start.41
  374.2 3.7 copy-start.32
  374.2 3.7 copy-start.53
  376.2 27.7 %copy-start.46 = (f32[3,48]{1,0:T(4,128)S(1)}, f32[3,48]{1,0:T(4,128)}, u32[]{:S(2)}) copy-start(f32[3,48]{1,0:T(4,128)} %param.31) | copy-start | bytes 1732
  376.2 27.7 %copy-start.51 = (f32[3,48]{1,0:T(4,128)S(1)}, f32[3,48]{1,0:T(4,128)}, u32[]{:S(2)}) copy-start(f32[3,48]{1,0:T(4,128)} %param.38) | copy-start | bytes 1732
  376.2 27.7 %copy-start.52 = (f32[3,48]{1,0:T(4,128)S(1)}, f32[3,48]{1,0:T(4,128)}, u32[]{:S(2)}) copy-start(f32[3,48]{1,0:T(4,128)} %param.45) | copy-start | bytes 1732
  376.2 29.0 %copy-start.11 = (bf16[1536,256]{1,0:T(8,128)(2,1)S(1)}, bf16[1536,256]{1,0:T(8,128)(2,1)}, u32[]{:S(2)}) copy-start(bf16[1536,256]{1,0:T(8,128)(2,1)} %get-tuple-element.164) | copy-start | bytes 2359300
  377.7 31.4 %copy-start.29 = (f32[5,256]{1,0:T(8,128)S(1)}, f32[5,256]{1,0:T(8,128)}, u32[]{:S(2)}) copy-start(f32[5,256]{1,0:T(8,128)} %param.30) | copy-start | bytes 15364
  377.7 31.4 %copy-start.42 = (f32[5,256]{1,0:T(8,128)S(1)}, f32[5,256]{1,0:T(8,128)}, u32[]{:S(2)}) copy-start(f32[5,256]{1,0:T(8,128)} %param.37) | copy-start | bytes 15364
  377.8 31.4 %copy-start.43 = (f32[5,256]{1,0:T(8,128)S(1)}, f32[5,256]{1,0:T(8,128)}, u32[]{:S(2)}) copy-start(f32[5,256]{1,0:T(8,128)} %param.44) | copy-start | bytes 15364
  377.8 32.1 %copy-start.20 = (f32[1536]{0:T(1024)S(1)}, f32[1536]{0:T(1024)}, u32[]{:S(2)}) copy-start(f32[1536]{0:T(1024)} %param.27) | copy-start | bytes 18436
  377.8 33.4 %copy-start.35 = (f32[3072]{0:T(1024)S(1)}, f32[3072]{0:T(1024)}, u32[]{:S(2)}) copy-start(f32[3072]{0:T(1024)} %param.28) | copy-start | bytes 36868
  377.8 33.4 %copy-start.37 = (f32[3072]{0:T(1024)S(1)}, f32[3072]{0:T(1024)}, u32[]{:S(2)}) copy-start(f32[3072]{0:T(1024)} %param.35) | copy-start | bytes 36868
  377.8 33.4 %copy-start.38 = (f32[3072]{0:T(1024)S(1)}, f32[3072]{0:T(1024)}, u32[]{:S(2)}) copy-start(f32[3072]{0:T(1024)} %param.42) | copy-start | bytes 36868
  401.9 12.1 %copy-start.5 = (f32[96,1536]{1,0:T(8,128)S(1)}, f32[96,1536]{1,0:T(8,128)}, u32[]{:S(2)}) copy-start(f32[96,1536]{1,0:T(8,128)} %param.26) | copy-start | bytes 1769476
  401.9 12.1 %copy-start.12 = (f32[96,1536]{1,0:T(8,128)S(1)}, f32[96,1536]{1,0:T(8,128)}, u32[]{:S(2)}) copy-start(f32[96,1536]{1,0:T(8,128)} %param.33) | copy-start | bytes 1769476
  403.8 13.3 %copy-start.31 = (f32[5,256]{1,0:T(8,128)}, f32[5,256]{1,0:T(8,128)S(1)}, u32[]{:S(2)}) copy-start(f32[5,256]{1,0:T(8,128)S(1)} %reduce_sum.148) | copy-start | bytes 15364
  404.0 13.1 %copy-start.44 = (f32[3,48]{1,0:T(4,128)}, f32[3,48]{1,0:T(4,128)S(1)}, u32[]{:S(2)}) copy-start(f32[3,48]{1,0:T(4,128)S(1)} %reshape.202) | copy-start | bytes 1732
  405.1 11.9 %copy-start.26 = (f32[3072]{0:T(1024)}, f32[3072]{0:T(1024)S(1)}, u32[]{:S(2)}) copy-start(f32[3072]{0:T(1024)S(1)} %reshape.198) | copy-start | bytes 36868
  405.1 8.9 %copy-start.13 = (f32[96,1536]{1,0:T(8,128)S(1)}, f32[96,1536]{1,0:T(8,128)}, u32[]{:S(2)}) copy-start(f32[96,1536]{1,0:T(8,128)} %param.40) | copy-start | bytes 1769476
  405.1 8.9 %copy-start.15 = (f32[96,1536]{1,0:T(8,128)S(1)}, f32[96,1536]{1,0:T(8,128)}, u32[]{:S(2)}) copy-start(f32[96,1536]{1,0:T(8,128)} %copy-done.14) | copy-start | bytes 1769476
  405.2 11.9 %copy-start.16 = (f32[1,5,8,384]{3,1,2,0:T(8,128)}, f32[1,5,8,384]{3,1,2,0:T(8,128)S(1)}, u32[]{:S(2)}) copy-start(f32[1,5,8,384]{3,1,2,0:T(8,128)S(1)} %copy.109) | copy-start | bytes 184324
  405.3 13.1 %collective-permute-start.9 = (bf16[8,48,256]{2,1,0:T(8,128)(2,1)S(1)}, bf16[8,48,256]{2,1,0:T(8,128)(2,1)S(1)}, u32[]{:S(2)}, u32[]{:S(2)}) collective-permute-start(bf16[8,48,256]{2,1,0:T(8,128)(2,1)S(1)} %get-tuple-element.151), channel_id=1, source_target_pairs={{0,1},{1,2},{2,3},{3,0},{4,5},{5,6},{6,7},{7,4},{8,9},{9,10},{10,1... | collective-permute-start | bytes 589832 | tf_op jit(solution)/shard_map/ppermute | solution.py:708
  406.1 12.3 %collective-permute-start.11 = (bf16[8,48,256]{2,1,0:T(8,128)(2,1)S(1)}, bf16[8,48,256]{2,1,0:T(8,128)(2,1)S(1)}, u32[]{:S(2)}, u32[]{:S(2)}) collective-permute-start(bf16[8,48,256]{2,1,0:T(8,128)(2,1)S(1)} %get-tuple-element.152), channel_id=1, source_target_pairs={{0,3},{1,0},{2,1},{3,2},{4,7},{5,4},{6,5},{7,6},{8,11},{9,8},{10,9... | collective-permute-start | bytes 589832 | tf_op jit(solution)/shard_map/ppermute | solution.py:708
  409.1 16.1 %collective-permute-start.10 = (bf16[8,48,256]{2,1,0:T(8,128)(2,1)S(1)}, bf16[8,48,256]{2,1,0:T(8,128)(2,1)S(1)}, u32[]{:S(2)}, u32[]{:S(2)}) collective-permute-start(bf16[8,48,256]{2,1,0:T(8,128)(2,1)S(1)} %get-tuple-element.153), channel_id=1, source_target_pairs={{0,2},{1,3},{2,0},{3,1},{4,6},{5,7},{6,4},{7,5},{8,10},{9,11},{10,... | collective-permute-start | bytes 589832 | tf_op jit(solution)/shard_map/ppermute | solution.py:708
  414.0 3.1 copy-start.21
  414.0 3.1 copy-start.22
  414.0 3.1 copy-start.23
  440.6 8.4 %copy-start = (bf16[1,256,1536]{2,1,0:T(8,128)(2,1)S(1)}, bf16[1,256,1536]{2,1,0:T(8,128)(2,1)}, u32[]{:S(2)}) copy-start(bf16[1,256,1536]{2,1,0:T(8,128)(2,1)} %param.23) | copy-start | bytes 2359300
  440.6 9.9 %copy-start.2 = (bf16[1,256,1536]{2,1,0:T(8,128)(2,1)S(1)}, bf16[1,256,1536]{2,1,0:T(8,128)(2,1)}, u32[]{:S(2)}) copy-start(bf16[1,256,1536]{2,1,0:T(8,128)(2,1)} %param.24) | copy-start | bytes 2359300
  440.6 10.0 %copy-start.10 = (bf16[256,1536]{1,0:T(8,128)(2,1)S(1)}, bf16[256,1536]{1,0:T(8,128)(2,1)}, u32[]{:S(2)}) copy-start(bf16[256,1536]{1,0:T(8,128)(2,1)} %reduce-scatter.3.cloned.1.call-done) | copy-start | bytes 2359300
  440.6 10.0 %copy-start.40 = (f32[256]{0:T(256)S(1)}, f32[256]{0:T(256)}, u32[]{:S(2)}) copy-start(f32[256]{0:T(256)} %copy-done.39) | copy-start | bytes 3076
  440.6 10.0 %copy-start.48 = (f32[256]{0:T(256)S(1)}, f32[256]{0:T(256)}, u32[]{:S(2)}) copy-start(f32[256]{0:T(256)} %get-tuple-element.160) | copy-start | bytes 3076
  (10 other events, 13.1 us)
Sparse Core Ops, SparseCore 0:
  12.3 61.3 all-gather.3
  75.6 45.3 all-gather.5
  172.2 63.1 reduce-scatter.2
  273.1 63.9 reduce-scatter.4

commit v5 on v3

--- a/solution.py
+++ b/solution.py
@@ -119,15 +119,15 @@
     return jnp.concatenate(out, axis=1)
 
 
-def chunk_common(heads, main, small, cat, head_ref, taps_ref):
+def chunk_common(heads, main, small16, sel_ref, cat, head_ref, taps_ref):
     rows = main.shape[0]
     gate, inner = split_pairs(main, heads)
-    raw = jnp.concatenate([small[:, : 2 * N_STATE], inner], axis=1)
+    raw = jnp.concatenate([small16[:, : 2 * N_STATE].astype(f32), inner], axis=1)
     cat[8 : 8 + rows] = raw
     conv = taps_ref[4:5] + taps_ref[0:1] * cat[5 : 5 + rows]
     for k in range(1, 4):
         conv = conv + taps_ref[k : k + 1] * cat[5 + k : 5 + k + rows]
-    step_in = small[:, 2 * N_STATE :] + head_ref[0:1]
+    step_in = mm(small16[:, 2 * N_STATE :], sel_ref[...], NN) + head_ref[0:1]
     dt = jnp.maximum(step_in, 0.0) + jnp.log1p(jnp.exp(-jnp.abs(step_in)))
     neg_rate = -jnp.exp(head_ref[1:2])
     decay_log = neg_rate * dt
@@ -139,7 +139,7 @@
 
 
 def fwd_kernel(
-    heads, main_ref, small_ref, head_ref, taps_ref, gated_ref, y_ref, states_ref, state, cat
+    heads, main_ref, small_ref, sel_ref, head_ref, taps_ref, gated_ref, y_ref, states_ref, state, cat
 ):
     rows = main_ref.shape[0]
 
@@ -151,7 +151,8 @@
     gate, conv, _, dt, _, _, cumul, r, c = chunk_common(
         heads,
         main_ref[...].astype(f32),
-        small_ref[...].astype(f32),
+        small_ref[...],
+        sel_ref,
         cat,
         head_ref,
         taps_ref,
@@ -184,8 +185,8 @@
     gated_ref[...] = (full * (gate * jax.nn.sigmoid(gate))).astype(bf16)
 
 
-def mixer_forward(main, small, head, taps, heads):
-    length = main.shape[0]
+def mixer_forward(proj, sel, head, taps, heads):
+    length = proj.shape[0]
     width = heads * P_SIZE
     count = length // CHUNK
     all_w = width + 2 * N_STATE
@@ -194,7 +195,8 @@
         grid=(count,),
         in_specs=[
             pl.BlockSpec((CHUNK, 2 * width), lambda i: (i, 0)),
-            pl.BlockSpec((CHUNK, 3 * LANES), lambda i: (i, 0)),
+            pl.BlockSpec((CHUNK, 3 * LANES), lambda i: (i, 2 * width // (3 * LANES))),
+            pl.BlockSpec((LANES, LANES), lambda i: (0, 0)),
             pl.BlockSpec((8, LANES), lambda i: (0, 0)),
             pl.BlockSpec((8, all_w), lambda i: (0, 0)),
         ],
@@ -216,7 +218,7 @@
             flops=0, bytes_accessed=70_000_000, transcendentals=0
         ),
         name="mixer_forward",
-    )(main, small, head, taps)
+    )(proj, proj, sel, head, taps)
 
 
 def bwd_kernel(
@@ -226,6 +228,7 @@
     small_ref,
     main_prev,
     small_prev,
+    sel_ref,
     head_ref,
     taps_ref,
     y_ref,
@@ -258,7 +261,8 @@
     gate, conv, step_in, dt, neg_rate, decay_log, cumul, r, c = chunk_common(
         heads,
         main_ref[...].astype(f32),
-        small_ref[...].astype(f32),
+        small_ref[...],
+        sel_ref,
         cat,
         head_ref,
         taps_ref,
@@ -347,7 +351,7 @@
     dmain_ref[...] = join_pairs(dgate, draw[:, 2 * N_STATE :], heads).astype(bf16)
 
 
-def mixer_backward(main, small, head, taps, y, states, dgated, heads):
+def mixer_backward(proj, sel, head, taps, y, states, dgated, heads):
     length, width = y.shape
     count = length // CHUNK
     all_w = width + 2 * N_STATE
@@ -356,8 +360,16 @@
     def at(i):
         return (count - 1 - i, 0)
 
+    small_at = 2 * width // (3 * LANES)
+
+    def at_small(i):
+        return (count - 1 - i, small_at)
+
     def before(i):
         return (jnp.maximum((count - 1 - i) * per - 1, 0), 0)
+
+    def before_small(i):
+        return (jnp.maximum((count - 1 - i) * per - 1, 0), small_at)
 
     def fixed(i):
         return (0, 0)
@@ -367,9 +379,10 @@
         grid=(count,),
         in_specs=[
             pl.BlockSpec((CHUNK, 2 * width), at),
-            pl.BlockSpec((CHUNK, 3 * LANES), at),
+            pl.BlockSpec((CHUNK, 3 * LANES), at_small),
             pl.BlockSpec((16, 2 * width), before),
-            pl.BlockSpec((16, 3 * LANES), before),
+            pl.BlockSpec((16, 3 * LANES), before_small),
+            pl.BlockSpec((LANES, LANES), fixed),
             pl.BlockSpec((8, LANES), fixed),
             pl.BlockSpec((8, all_w), fixed),
             pl.BlockSpec((CHUNK, width), at),
@@ -399,7 +412,7 @@
             flops=0, bytes_accessed=160_000_000, transcendentals=0
         ),
         name="mixer_backward",
-    )(main, small, main, small, head, taps, y, states, dgated)
+    )(proj, proj, proj, proj, sel, head, taps, y, states, dgated)
 
 
 MESH = pl.DeviceIdType.MESH
@@ -423,37 +436,46 @@
     )
 
 
-def weights_kernel(n_seq, n_wsh, main, small, w_main, w_small, *sems):
+def weights_kernel(n_seq, n_wsh, main, small, w_all, *sems):
     send_a, recv_a, send_b, recv_b, send_e, recv_e, send_r, recv_r, send_l, recv_l, own = sems
+    cols = main.shape[2]
+
+    def main_at(i, j):
+        return w_all.at[i, j, :, :cols]
+
+    def small_at(i, j):
+        return w_all.at[i, j, :, cols:]
+
     s = lax.axis_index("seq")
     w = lax.axis_index("wshard")
     row = [(lax.rem(s + k, n_seq), w) for k in range(1, n_seq)]
     col = [(s, lax.rem(w + j, n_wsh)) for j in range(1, n_wsh)]
     greet(row + col, n_seq + n_wsh - 2)
     first = [
-        wire(main.at[peer[0]], w_main.at[s, w], send_a.at[k], recv_a.at[k], peer)
+        wire(main.at[peer[0]], main_at(s, w), send_a.at[k], recv_a.at[k], peer)
         for k, peer in enumerate(row)
     ]
     spread = [
-        wire(small, w_small.at[s, w], send_b.at[j], recv_b.at[j], peer)
+        wire(small, small_at(s, w), send_b.at[j], recv_b.at[j], peer)
         for j, peer in enumerate(col)
     ]
+    plane = w_all.at[s, :, :, cols:]
     third = [
-        wire(w_small.at[s], w_small.at[s], send_e.at[k], recv_e.at[k], peer)
+        wire(plane, plane, send_e.at[k], recv_e.at[k], peer)
         for k, peer in enumerate(row)
     ]
     mine = [
-        pltpu.make_async_copy(main.at[s], w_main.at[s, w], own.at[0]),
-        pltpu.make_async_copy(small, w_small.at[s, w], own.at[1]),
+        pltpu.make_async_copy(main.at[s], main_at(s, w), own.at[0]),
+        pltpu.make_async_copy(small, small_at(s, w), own.at[1]),
     ]
 
     def right(t):
-        block = w_main.at[:, jnp.maximum(w - t, 0)]
+        block = w_all.at[:, jnp.maximum(w - t, 0), :, :cols]
         peer = (s, jnp.minimum(w + 1, n_wsh - 1))
         return wire(block, block, send_r.at[t], recv_r.at[t], peer)
 
     def left(t):
-        block = w_main.at[:, jnp.minimum(w + t, n_wsh - 1)]
+        block = w_all.at[:, jnp.minimum(w + t, n_wsh - 1), :, :cols]
         peer = (s, jnp.maximum(w - 1, 0))
         return wire(block, block, send_l.at[t], recv_l.at[t], peer)
 
@@ -495,11 +517,10 @@
     return pl.pallas_call(
         functools.partial(weights_kernel, n_seq, n_wsh),
         in_specs=[anywhere] * 2,
-        out_specs=[anywhere] * 2,
-        out_shape=[
-            jax.ShapeDtypeStruct((n_seq, n_wsh, rows_in, cols), bf16),
-            jax.ShapeDtypeStruct((n_seq, n_wsh) + small.shape, bf16),
-        ],
+        out_specs=anywhere,
+        out_shape=jax.ShapeDtypeStruct(
+            (n_seq, n_wsh, rows_in, cols + small.shape[1]), bf16
+        ),
         scratch_shapes=[dma((n,)) for n in (a, a, c, c, a, a, c, c, c, c, 2)],
         compiler_params=pltpu.CompilerParams(collective_id=0, has_side_effects=True),
         cost_estimate=pl.CostEstimate(
@@ -742,10 +763,12 @@
     main_send = jnp.swapaxes(main_send, 0, 1)
     small_send = in_w16[:, 2 * inner_all :]
     small_send = jnp.pad(small_send, ((0, 0), (0, -small_send.shape[1] % LANES)))
-    w_main, w_small = spread_weights(main_send, small_send, n_seq, n_wsh)
-    out_w16, w_main = lax.optimization_barrier((out_weight.astype(bf16), w_main))
-    w_main = w_main.reshape(width_in, 2 * width)
-    w_small = w_small.reshape(width_in, small_send.shape[1])
+    w_all = spread_weights(main_send, small_send, n_seq, n_wsh)
+    out_w16, w_all = lax.optimization_barrier((out_weight.astype(bf16), w_all))
+    w_all = w_all.reshape(width_in, 2 * width + small_send.shape[1])
+    proj = mm(normed_all, w_all, NN).astype(bf16)
+    w_main = w_all[:, : 2 * width]
+    w_small = w_all[:, 2 * width :]
     w_out = jnp.zeros((n_wsh,) + out_w16.shape, bf16)
     w_out = lax.dynamic_update_index_in_dim(w_out, out_w16, wsh_index, 0)
     for j in range(1, n_wsh):
@@ -760,23 +783,19 @@
         lane = lax.broadcasted_iota(jnp.int32, (w_small.shape[1], width_to), 1)
         return jnp.where((col == lane + first) & (lane < count), 1.0, 0.0)
 
-    first_step = 2 * N_STATE + seq_index * heads
-    to_step = pick(first_step, heads, LANES)
-    to_fwd = jnp.concatenate([pick(0, 2 * N_STATE, 2 * N_STATE), to_step], axis=1)
+    to_step = pick(2 * N_STATE + seq_index * heads, heads, LANES)
     to_ext = jnp.concatenate(
         [pick(seq_index * share, share, share), to_step[:, :STEP_ROWS]], axis=1
     )
-    w_fwd = mm(w_small, to_fwd.astype(bf16), NN).astype(bf16)
     w_ext = mm(w_small, to_ext.astype(bf16), NN).astype(bf16)
-
-    main = mm(normed_all, w_main, NN).astype(bf16)
-    small = mm(normed_all, w_fwd, NN).astype(bf16)
+    sel = to_step[2 * N_STATE :].astype(bf16)
+
     head_local = lax.dynamic_slice_in_dim(head_params, seq_index * heads, heads, 1)
     head = jnp.pad(head_local, ((0, 5), (0, LANES - heads)))
     conv_local = lax.dynamic_slice_in_dim(conv_inner, seq_index * width, width, 1)
     taps = jnp.pad(jnp.concatenate([conv_shared, conv_local], axis=1), ((0, 3), (0, 0)))
     gain_local = lax.dynamic_slice_in_dim(out_gain, seq_index * width, width, 0)
-    gated, y, states = mixer_forward(main, small, head, taps, heads)
+    gated, y, states = mixer_forward(proj, sel, head, taps, heads)
     d_gnormed = mm(cot_all, w_out, NT)
     gated32 = gated.astype(f32)
     scaled = d_gnormed * gain_local
@@ -794,17 +813,17 @@
     mixed = mm(gnormed, w_out, NN).astype(bf16)
     g_out, mixed, d_gated = lax.optimization_barrier((g_out, mixed, d_gated))
     mixed = lax.psum_scatter(mixed, "seq", scatter_dimension=0, tiled=True)
-    grad_out_weight = lax.dynamic_slice_in_dim(g_out, wsh_index * rows_out, rows_out, 0)
+    out_parts = [lax.dynamic_slice_in_dim(g_out, wsh_index * rows_out, rows_out, 0)]
     for j in range(1, n_wsh):
         to = lax.rem(wsh_index + j, n_wsh)
         part = lax.dynamic_slice_in_dim(g_out, to * rows_out, rows_out, 0)
-        grad_out_weight = grad_out_weight + shift(part, j, n_wsh)
+        out_parts.append(shift(part, j, n_wsh))
     dmain, dshared_t, dstep_t, dtaps, dhead = mixer_backward(
-        main, small, head, taps, y, states, d_gated, heads
+        proj, sel, head, taps, y, states, d_gated, heads
     )
 
     g_main = mm(normed_all, dmain, TN)
-    d_gain_part = jnp.sum(g_main * w_main.astype(f32), axis=1)
+    g_full = g_main
     g_main = g_main.astype(bf16).reshape(n_seq, n_wsh, rows_in, 2 * width)
     g_parts = [lax.dynamic_index_in_dim(g_main, wsh_index, 1, keepdims=False)]
     for j in range(1, n_wsh):
@@ -820,7 +839,9 @@
     d_normed = mm(dmain, w_main, NT) + lax.dot_general(
         d_ext, w_ext, (((0,), (1,)), ((), ())), preferred_element_type=f32
     )
-    d_normed, mixed = lax.optimization_barrier((d_normed.astype(bf16), mixed))
+    d_normed, mixed, g_full, d_ext = lax.optimization_barrier(
+        (d_normed.astype(bf16), mixed, g_full, d_ext)
+    )
     block_out = (inputs + mixed.astype(f32))[None]
     d_normed = lax.psum_scatter(d_normed, "seq", scatter_dimension=0, tiled=True)
     d_normed = d_normed.astype(f32)
@@ -834,7 +855,9 @@
     g_ext = lax.dot_general(
         normed_all, d_ext, (((0,), (1,)), ((), ())), preferred_element_type=f32
     )
-    d_gain_part = d_gain_part + jnp.sum(g_ext * w_ext.astype(f32), axis=1)
+    d_gain_part = jnp.sum(g_full * w_main.astype(f32), axis=1) + jnp.sum(
+        g_ext * w_ext.astype(f32), axis=1
+    )
     g_ext = jnp.pad(g_ext.astype(bf16), ((0, 0), (0, -g_ext.shape[1] % LANES)))
     g_ext = g_ext.reshape(n_seq, n_wsh, rows_in, LANES)
 
@@ -865,6 +888,19 @@
     grad_conv_inner = jnp.swapaxes(sums[3], 0, 1).reshape(conv_inner.shape)
     grad_head_params = jnp.swapaxes(sums[4], 0, 1).reshape(head_params.shape)
 
+    flat, out_parts = lax.optimization_barrier((flat, out_parts))
+    grad_out_weight = sum(out_parts)
+    new_out_weight, new_first_out_weight, new_second_out_weight = adamw(
+        out_weight,
+        grad_out_weight,
+        first_out_weight,
+        second_out_weight,
+        weight_learning_rate,
+        matrix_decay,
+    )
+    ready = (new_out_weight, new_first_out_weight, new_second_out_weight, grad_out_weight)
+    ready, g_parts = lax.optimization_barrier((ready, g_parts))
+    new_out_weight, new_first_out_weight, new_second_out_weight, grad_out_weight = ready
     g_main = g_parts[0].astype(f32)
     for part in g_parts[1:]:
         g_main = g_main + part.astype(f32)
@@ -886,14 +922,6 @@
     g_ext = jnp.pad(g_ext, ((0, 0), (0, 2 * width - g_ext.shape[1])))
     grad_in_weight, new_in_weight, new_first_in_weight, new_second_in_weight = adam_in(
         g_main, g_ext, in_weight, first_in_weight, second_in_weight
-    )
-    new_out_weight, new_first_out_weight, new_second_out_weight = adamw(
-        out_weight,
-        grad_out_weight,
-        first_out_weight,
-        second_out_weight,
-        weight_learning_rate,
-        matrix_decay,
     )
     updated_input_gain, new_first_in_gain, new_second_in_gain = adamw(
         in_gain, grad_in_gain, first_in_gain, second_in_gain, small_rate, 0.0

time: 428 us -> 462 us (1.079)
  Pallas kernels: 196 us -> 273 us
  waiting for transfers between devices: 76.8 us -> 29.9 us
  local copies, waits for them, and re-layouts: 17.6 us -> 35.3 us
  starting transfers between devices: 24.2 us -> 12.1 us
  matrix products: 67.3 us -> 59.2 us
  other arithmetic: 29.5 us -> 36.1 us
    pallas_call x4, Pallas kernels: 56.9 us -> 129 us  [swap(): pl.pallas_call(functools.partial(swap_kernel, plan, n_seq, n_wsh), in_spe...]
    ppermute x9, waiting for transfers between devices: 76 us -> 29.2 us  [shift(): lax.ppermute(x, 'wshard', [(i, (i + j) % n_wsh) for i in range(n_wsh)])]
    ppermute x9, starting transfers between devices: 24.1 us -> 12 us  [shift(): lax.ppermute(x, 'wshard', [(i, (i + j) % n_wsh) for i in range(n_wsh)])]
    dot_general x8 -> x7, matrix products: 58.9 us -> 53.6 us  [mm(): return lax.dot_general(a, b, dims, preferred_element_type=f32)]
  transfers between devices with their start and end apart: 13 -> 13, of which waited for: 5 -> 3; matrix products, arithmetic and copies ran while one was open for 18% -> 19% of each run, Pallas kernels for 44% -> 58%
where the time goes in v5:
time: 462 us; the launch traced here: 460 us
  Pallas kernels  273 us (59%)
  matrix products  59.2 us (13%)
  other arithmetic  36.1 us (8%)
  local copies, waits for them, and re-layouts  35.3 us (8%)
  waiting for transfers between devices  29.9 us (6%)
  between operations  14.6 us (3%)
  starting transfers between devices  12.1 us (3%)
    pallas_call x4, Pallas kernels, swap(): pl.pallas_call(functools.partial(swap_kernel, plan, n_seq, n_wsh), in_spe...  129 us
    pallas_call x1, Pallas kernels, spread_weights(): pl.pallas_call(functools.partial(weights_kernel, n_seq, n_wsh), in_specs=...  57.9 us
    dot_general x7, matrix products, mm(): return lax.dot_general(a, b, dims, preferred_element_type=f32)  53.6 us
    pallas_call x1, Pallas kernels, mixer_backward(): pl.pallas_call(functools.partial(bwd_kernel, heads, count), grid=(count,)...  47.8 us
    ppermute x9, waiting for transfers between devices, shift(): lax.ppermute(x, 'wshard', [(i, (i + j) % n_wsh) for i in range(n_wsh)])  29.2 us
    pallas_call x1, Pallas kernels, mixer_forward(): pl.pallas_call(functools.partial(fwd_kernel, heads), grid=(count,), in_sp...  22.3 us
    ppermute x9, starting transfers between devices, shift(): lax.ppermute(x, 'wshard', [(i, (i + j) % n_wsh) for i in range(n_wsh)])  12 us
  transfers between devices with their start and end apart: 13, of which 3 were waited for; matrix products, arithmetic and copies ran while one was open for 19% of the time, Pallas kernels for 58%

profile of v5, /device:TPU:0, one launch (start us, length us, event | category | flops | bytes accessed | tf_op | source)
XLA Modules:
  0.0 460.1 jit_solution(159537522723692479)
XLA Ops:
  7.3 1.5 fusion.15
  9.3 2.3 fusion.17
  11.6 0.7 all-gather.6.cloned.1.call-update
  12.6 0.7 convert_element_type.93
  13.3 0.9 copy.108
  14.8 57.9 %spread_weights.1 = bf16[8,4,48,1152]{3,2,1,0:T(8,128)(2,1)} custom-call(bf16[8,48,768]{2,1,0:T(8,128)(2,1)} %bitcast.108, bf16[48,384]{1,0:T(8,128)(2,1)} %pad.24.small), custom_call_target="tpu_custom_call" | custom-call | bytes 200000000 | tf_op jit(solution)/shard_map/spread_weights/pallas_call | solution.py:517
  72.8 3.3 collective-permute-start.2
  78.1 0.8 dynamic_slice.36
  79.5 0.7 constant_dynamic-slice_fusion.4
  80.8 1.1 broadcast_in_dim.51
  81.9 1.7 bitcast_dynamic-update-slice_fusion.3
  83.7 13.1 %collective-permute-done = bf16[96,1536]{1,0:T(8,128)(2,1)} collective-permute-done((bf16[96,1536]{1,0:T(8,128)(2,1)}, bf16[96,1536]{1,0:T(8,128)(2,1)}, u32[]{:S(2)}, u32[]{:S(2)}) %collective-permute-start) | collective-permute-done | bytes 294944 | tf_op jit(solution)/shard_map/ppermute | solution.py:685
  96.8 1.7 bitcast_dynamic-update-slice_fusion.2
  98.5 2.7 collective-permute-done.1
  101.2 1.7 bitcast_dynamic-update-slice_fusion.1
  102.9 1.7 bitcast_dynamic-update-slice_fusion
  104.6 11.8 %convolution_convert_fusion.1.main_ref.small_ref.main_prev.small_prev = bf16[2048,1152]{1,0:T(8,128)(2,1)} fusion(bf16[2048,1536]{1,0:T(8,128)(2,1)} %all-gather.4.cloned.1.call-done, bf16[1536,1152]{1,0:T(8,128)(2,1)S(1)} %bitcast.102), kind=kOutput, calls=%fused_computation.2 | convolution fusion | flops 7250116608 | bytes 14548992 | tf_op jit(solution)/shard_map/dot_general | solution.py:35
  116.4 22.3 %mixer_forward.1 = (bf16[2048,384]{1,0:T(8,128)(2,1)}, f32[2048,384]{1,0:T(8,128)}, f32[16,128,384]{2,1,0:T(8,128)}) custom-call(bf16[2048,1152]{1,0:T(8,128)(2,1)} %convolution_convert_fusion.1.main_ref.small_ref.main_prev.small_prev, bf16[2048,1152]{1,0:T(8,128)(2,1)} %convolution_convert_fusion.1.main_ref.small_ref.main_prev.small_prev, ...), custom_call_target="tpu_custom_call" | custom-call | bytes 70000000 | tf_op jit(solution)/shard_map/mixer_forward/pallas_call | solution.py:193
  138.7 8.7 %fusion.4 = (f32[2048]{0:T(1024)S(1)}, f32[2048]{0:T(1024)S(1)}, f32[384,2048]{0,1:T(8,128)}) fusion(bf16[2048,384]{1,0:T(8,128)(2,1)} %get-tuple-element.71, f32[384]{0:T(512)S(1)} %dynamic_slice.36, bf16[384,1536]{1,0:T(8,128)(2,1)} %bitcast.9, bf16[1,2048,1536]{2,1,0:T(8,128)(2,1)} %all-gather.6.cloned.1.call-done), kind=kOutput, calls=%fused_computation.13 | convolution fusion | flops 2420633600 | bytes 12207616 | tf_op jit(solution)/shard_map/dot_general | solution.py:35
  148.0 7.3 %sum_over_seq.1 = f32[32,128]{1,0:T(8,128)} custom-call(f32[32,128]{1,0:T(8,128)} %reshape.177.x_ref), custom_call_target="tpu_custom_call" | custom-call | tf_op jit(solution)/shard_map/sum_over_seq/pallas_call | solution.py:658
  155.4 0.7 multiply_multiply_fusion.5
  156.1 1.3 multiply_bitcast_fusion
  157.4 7.9 %convolution_convert_fusion = bf16[2048,1536]{1,0:T(8,128)(2,1)} fusion(bf16[384,1536]{1,0:T(8,128)(2,1)} %bitcast.9, bf16[2048,384]{1,0:T(8,128)(2,1)} %get-tuple-element.71, f32[2048]{0:T(1024)S(1)} %get-tuple-element.142, f32[384]{0:T(512)} %copy-done.36), kind=kOutput, calls=%fused_computation.1 | convolution fusion | flops 2422210560 | bytes 9053696 | tf_op jit(solution)/shard_map/dot_general | solution.py:35
  165.3 4.8 %fusion.12 = (f32[384]{0:T(512)}, bf16[2048,384]{1,0:T(8,128)(2,1)}) fusion(bf16[2048,384]{1,0:T(8,128)(2,1)} %get-tuple-element.71, f32[384,2048]{0,1:T(8,128)} %get-tuple-element.145, f32[2048]{0:T(1024)S(1)} %get-tuple-element.142, f32[2048]{0:T(1024)} %get-tuple-element.141, f32[2048]{0:T(1024)S(1)} %multiply_multiply_fusion.5, f32[384]{0:T(512)} %copy-done.36), kind=kLoop, calls=%fused_computation.21 | loop fusion | flops 7863936 | bytes 6319104 | tf_op jit(solution)/shard_map/reduce_sum | solution.py:810
  170.0 6.9 %fusion = f32[384,1536]{1,0:T(8,128)} fusion(bf16[1,2048,1536]{2,1,0:T(8,128)(2,1)} %all-gather.6.cloned.1.call-done, bf16[2048,384]{1,0:T(8,128)(2,1)S(1)} %copy-done.9, f32[2048]{0:T(1024)S(1)} %get-tuple-element.142, f32[384]{0:T(512)S(1)} %copy-done.37), kind=kOutput, calls=%fused_computation.3 | convolution fusion | flops 2419064832 | bytes 10233344 | tf_op jit(solution)/shard_map/dot_general | solution.py:35
  177.0 1.0 copy.87
  178.1 1.1 convolution_convert_fusion.2
  179.2 47.8 %mixer_backward.1 = (bf16[2048,768]{1,0:T(8,128)(2,1)}, bf16[256,2048]{1,0:T(8,128)(2,1)}, bf16[16,2048]{1,0:T(8,128)(2,1)}, f32[8,640]{1,0:T(8,128)}, f32[8,128]{1,0:T(8,128)}) custom-call(bf16[2048,1152]{1,0:T(8,128)(2,1)} %convolution_convert_fusion.1.main_ref.small_ref.main_prev.small_prev, ...), custom_call_target="tpu_custom_call" | custom-call | bytes 160000000 | tf_op jit(solution)/shard_map/mixer_backward/pallas_call | solution.py:377
  227.1 21.9 %shard_map.462 = bf16[8,32,2048]{2,1,0:T(8,128)(2,1)} custom-call(bf16[8,32,2048]{2,1,0:T(8,128)(2,1)} %bitcast.112), custom_call_target="tpu_custom_call" | custom-call | tf_op jit(solution)/shard_map/pallas_call | solution.py:623
  248.9 2.1 reduce_sum.128
  251.0 1.6 pad_maximum_fusion
  252.6 7.2 %fusion.13 = f32[2048,1536]{1,0:T(8,128)S(1)} fusion(bf16[2048,768]{1,0:T(8,128)(2,1)} %get-tuple-element.74, bf16[1536,1152]{1,0:T(8,128)(2,1)S(1)} %bitcast.104), kind=kOutput, calls=%fused_computation.29 | convolution fusion | flops 4831838208 | bytes 18087936 | tf_op jit(solution)/shard_map/dot_general | solution.py:35
  259.9 4.5 add_convert_fusion
  264.4 10.0 %fusion.47 = (bf16[1536,768]{1,0:T(8,128)(2,1)}, f32[1536,768]{1,0:T(8,128)}) fusion(bf16[2048,1536]{1,0:T(8,128)(2,1)} %all-gather.4.cloned.1.call-done, bf16[2048,768]{1,0:T(8,128)(2,1)} %get-tuple-element.74), kind=kOutput, calls=%fused_computation.124 | convolution fusion | flops 4833017856 | bytes 16515072 | tf_op jit(solution)/shard_map/dot_general | solution.py:35
  274.5 1.3 slice.75
  275.8 0.7 slice.76
  276.5 1.2 slice.77
  277.7 1.3 slice_reduce_fusion.2
  279.0 0.8 reshape_squeeze.3
  280.4 0.7 pad_maximum_fusion.2
  282.3 0.7 reshape.180
  283.0 3.5 constant_dynamic-slice_fusion
  286.6 3.2 collective-permute-start.4
  289.8 1.5 collective-permute-start.3
  291.3 3.2 dynamic-slice_bitcast_fusion
  294.4 2.4 collective-permute-start.8
  297.9 1.2 multiply_reduce_fusion.1
  299.4 0.8 pad.27.clone
  300.9 88.4 %shard_map.463 = (bf16[4,8,48,128]{3,2,1,0:T(8,128)(2,1)}, f32[4,48,128]{2,1,0:T(8,128)}) custom-call(bf16[8,4,48,128]{3,2,1,0:T(8,128)(2,1)} %bitcast.111, f32[48,128]{1,0:T(8,128)} %pad_bitcast_fusion.refs_1_), custom_call_target="tpu_custom_call" | custom-call | tf_op jit(solution)/shard_map/pallas_call | solution.py:623
  389.3 1.5 reduce_sum.134.refs_0_
  390.8 7.2 %shard_map.464 = f32[8,48,128]{2,1,0:T(8,128)} custom-call(f32[48,128]{1,0:T(8,128)} %reduce_sum.134.refs_0_), custom_call_target="tpu_custom_call" | custom-call | tf_op jit(solution)/shard_map/pallas_call | solution.py:623
  398.0 1.0 copy.109
  399.1 1.7 reduce_sum.135.refs_1_
  400.8 0.9 collective-permute-start.6
  401.8 3.2 multiply_subtract_fusion
  405.0 13.3 %collective-permute-done.6 = bf16[8,48,768]{2,1,0:T(8,128)(2,1)} collective-permute-done((bf16[8,48,768]{2,1,0:T(8,128)(2,1)}, bf16[8,48,768]{2,1,0:T(8,128)(2,1)}, u32[]{:S(2)}, u32[]{:S(2)}) %collective-permute-start.6) | collective-permute-done | bytes 589856 | tf_op jit(solution)/shard_map/ppermute | solution.py:685
  419.7 2.6 add_convert_fusion.1.refs_0_
  422.3 11.8 %shard_map.465 = (bf16[8,48,768]{2,1,0:T(8,128)(2,1)}, bf16[8,48,128]{2,1,0:T(8,128)(2,1)}) custom-call(bf16[8,48,768]{2,1,0:T(8,128)(2,1)} %add_convert_fusion.1.refs_0_, bf16[8,48,128]{2,1,0:T(8,128)(2,1)} %reduce_sum.135.refs_1_), custom_call_target="tpu_custom_call" | custom-call | tf_op jit(solution)/shard_map/pallas_call | solution.py:623
  434.1 1.0 slice.95
  435.1 0.9 copy.93
  437.1 8.2 %adam_in.1 = (f32[48,6448]{1,0:T(8,128)}, f32[48,6448]{1,0:T(8,128)}, f32[48,6448]{1,0:T(8,128)}, f32[48,6448]{1,0:T(8,128)}) custom-call(bf16[8,48,768]{2,1,0:T(8,128)(2,1)} %get-tuple-element.95.g_ref, bf16[48,768]{1,0:T(8,128)(2,1)} %fusion.31.ext_ref, f32[48,6448]{1,0:T(8,128)} %p_ref.1, f32[48,6448]{1,0:T(8,128)} %m_ref.1, f32[48,6448]{1,0:T(8,128)} %v_ref.1), custom_call_target="tpu_custom_call" | custom-call | tf_op jit(solution)/shard_map/adam_in/pallas_call | solution.py:702
  447.9 0.8 multiply_subtract_fusion.1
  448.6 1.5 fusion.22
  450.1 3.4 fusion.21
  (176 shorter events, 14.3 us)
Async XLA Ops:
  7.2 5.2 %copy-start.2 = (f32[48,6448]{1,0:T(8,128)S(1)}, f32[48,6448]{1,0:T(8,128)}, u32[]{:S(2)}) copy-start(f32[48,6448]{1,0:T(8,128)} %p_ref.1) | copy-start | bytes 3714052
  7.2 97.4 %all-gather.4.cloned.1.call-start = ((), (), s32[]{:S(2)}) async-start(), calls=%async_computation.2 | async-start | bytes 7077888 | tf_op jit(solution)/shard_map/all_gather | solution.py:758
  9.3 3.0 copy-start.33
  11.5 1.1 copy-start.5
  11.6 127.2 %all-gather.6.cloned.1.call-start = ((), (), s32[]{:S(2)}) async-start(), calls=%async_computation.5 | async-start | bytes 7077888 | tf_op jit(solution)/shard_map/all_gather | solution.py:760
  12.3 262.1 %reduce-scatter.3.cloned.1.call-start = ((), (), s32[]{:S(2)}) async-start(), calls=%async_computation.3 | async-start | bytes 7077888 | tf_op jit(solution)/shard_map/reduce_scatter | solution.py:815
  14.2 64.6 %copy-start.41 = (f32[3,48]{1,0:T(4,128)S(1)}, f32[3,48]{1,0:T(4,128)}, u32[]{:S(2)}) copy-start(f32[3,48]{1,0:T(4,128)} %param.31) | copy-start | bytes 1732
  14.2 66.0 %copy-start.25 = (f32[5,256]{1,0:T(8,128)S(1)}, f32[5,256]{1,0:T(8,128)}, u32[]{:S(2)}) copy-start(f32[5,256]{1,0:T(8,128)} %param.30) | copy-start | bytes 15364
  72.7 31.9 %copy-start.1 = (bf16[8,4,48,1152]{3,2,1,0:T(8,128)(2,1)S(1)}, bf16[8,4,48,1152]{3,2,1,0:T(8,128)(2,1)}, u32[]{:S(2)}) copy-start(bf16[8,4,48,1152]{3,2,1,0:T(8,128)(2,1)} %spread_weights.1) | copy-start | bytes 10616836
  72.8 30.2 %collective-permute-start.2 = (bf16[96,1536]{1,0:T(8,128)(2,1)}, bf16[96,1536]{1,0:T(8,128)(2,1)}, u32[]{:S(2)}, u32[]{:S(2)}) collective-permute-start(bf16[96,1536]{1,0:T(8,128)(2,1)} %convert_element_type.93), channel_id=1, source_target_pairs={{0,3},{1,0},{2,1},{3,2},{4,7},{5,4},{6,5},{7,6},{8,11},{9,8},{10,9... | collective-permute-start | bytes 884744 | tf_op jit(solution)/shard_map/ppermute | solution.py:685
  76.1 25.1 %collective-permute-start.1 = (bf16[96,1536]{1,0:T(8,128)(2,1)}, bf16[96,1536]{1,0:T(8,128)(2,1)}, u32[]{:S(2)}, u32[]{:S(2)}) collective-permute-start(bf16[96,1536]{1,0:T(8,128)(2,1)} %convert_element_type.93), channel_id=1, source_target_pairs={{0,2},{1,3},{2,0},{3,1},{4,6},{5,7},{6,4},{7,5},{8,10},{9,11},{10,... | collective-permute-start | bytes 884744 | tf_op jit(solution)/shard_map/ppermute | solution.py:685
  76.1 20.7 %collective-permute-start = (bf16[96,1536]{1,0:T(8,128)(2,1)}, bf16[96,1536]{1,0:T(8,128)(2,1)}, u32[]{:S(2)}, u32[]{:S(2)}) collective-permute-start(bf16[96,1536]{1,0:T(8,128)(2,1)} %convert_element_type.93), channel_id=1, source_target_pairs={{0,1},{1,2},{2,3},{3,0},{4,5},{5,6},{6,7},{7,4},{8,9},{9,10},{10,1... | collective-permute-start | bytes 884744 | tf_op jit(solution)/shard_map/ppermute | solution.py:685
  76.8 0.6 copy-start.17
  78.8 59.9 %copy-start.36 = (f32[384]{0:T(512)}, f32[384]{0:T(512)S(1)}, u32[]{:S(2)}) copy-start(f32[384]{0:T(512)S(1)} %dynamic_slice.36) | copy-start | bytes 4612
  165.3 4.8 %copy-start.9 = (bf16[2048,384]{1,0:T(8,128)(2,1)S(1)}, bf16[2048,384]{1,0:T(8,128)(2,1)}, u32[]{:S(2)}) copy-start(bf16[2048,384]{1,0:T(8,128)(2,1)} %get-tuple-element.71) | copy-start | bytes 4718596
  165.3 4.8 %copy-start.37 = (f32[384]{0:T(512)S(1)}, f32[384]{0:T(512)}, u32[]{:S(2)}) copy-start(f32[384]{0:T(512)} %copy-done.36) | copy-start | bytes 4612
  176.9 271.7 %reduce-scatter.5.cloned.1.call-start = ((), (), s32[]{:S(2)}) async-start(), calls=%async_computation.4 | async-start | bytes 7077888 | tf_op jit(solution)/shard_map/reduce_scatter | solution.py:846
  252.6 7.2 %copy-start.10 = (bf16[32,2048]{1,0:T(8,128)(2,1)S(1)}, bf16[32,2048]{1,0:T(8,128)(2,1)}, u32[]{:S(2)}) copy-start(bf16[32,2048]{1,0:T(8,128)(2,1)} %reduce_sum.128) | copy-start | bytes 393220
  252.6 7.2 %copy-start.15 = (bf16[1536,48]{0,1:T(8,128)(2,1)S(1)}, bf16[1536,48]{0,1:T(8,128)(2,1)}, u32[]{:S(2)}) copy-start(bf16[1536,48]{0,1:T(8,128)(2,1)} %convolution_convert_fusion.2) | copy-start | bytes 442372
  252.6 7.2 %copy-start.19 = (bf16[16,2048]{1,0:T(8,128)(2,1)S(1)}, bf16[16,2048]{1,0:T(8,128)(2,1)}, u32[]{:S(2)}) copy-start(bf16[16,2048]{1,0:T(8,128)(2,1)} %get-tuple-element.76) | copy-start | bytes 196612
  283.0 14.5 %slice-start = ((s8[6291456]{0:T(1024)(128)(4,1)}), s8[4194304]{0:T(1024)(128)(4,1)S(1)}, s32[]{:S(2)}) async-start(s8[6291456]{0:T(1024)(128)(4,1)} %bitcast.106), calls=%async_computation.6 | async-start | bytes 8388608
  286.6 114.2 %collective-permute-start.5 = (f32[96,1536]{1,0:T(8,128)}, f32[96,1536]{1,0:T(8,128)}, u32[]{:S(2)}, u32[]{:S(2)}) collective-permute-start(f32[96,1536]{1,0:T(8,128)} %get-tuple-element.133), channel_id=1, source_target_pairs={{0,3},{1,0},{2,1},{3,2},{4,7},{5,4},{6,5},{7,6},{8,11},{9,8},{10,9... | collective-permute-start | bytes 1769480 | tf_op jit(solution)/shard_map/ppermute | solution.py:685
  286.6 115.1 %collective-permute-start.4 = (f32[96,1536]{1,0:T(8,128)}, f32[96,1536]{1,0:T(8,128)}, u32[]{:S(2)}, u32[]{:S(2)}) collective-permute-start(f32[96,1536]{1,0:T(8,128)} %get-tuple-element.134), channel_id=1, source_target_pairs={{0,2},{1,3},{2,0},{3,1},{4,6},{5,7},{6,4},{7,5},{8,10},{9,11},{10,... | collective-permute-start | bytes 1769480 | tf_op jit(solution)/shard_map/ppermute | solution.py:685
  289.8 111.9 %collective-permute-start.3 = (f32[96,1536]{1,0:T(8,128)}, f32[96,1536]{1,0:T(8,128)}, u32[]{:S(2)}, u32[]{:S(2)}) collective-permute-start(f32[96,1536]{1,0:T(8,128)} %get-tuple-element.135), channel_id=1, source_target_pairs={{0,1},{1,2},{2,3},{3,0},{4,5},{5,6},{6,7},{7,4},{8,9},{9,10},{10,1... | collective-permute-start | bytes 1769480 | tf_op jit(solution)/shard_map/ppermute | solution.py:685
  291.3 5.6 %copy-start.3 = (f32[1536,768]{1,0:T(8,128)S(1)}, f32[1536,768]{1,0:T(8,128)}, u32[]{:S(2)}) copy-start(f32[1536,768]{1,0:T(8,128)} %get-tuple-element.81) | copy-start | bytes 14155780
  291.3 6.2 %slice-start.1 = ((s8[6291456]{0:T(1024)(128)(4,1)}), s8[2097152]{0:T(1024)(128)(4,1)S(1)}, s32[]{:S(2)}) async-start(s8[6291456]{0:T(1024)(128)(4,1)} %bitcast.106), calls=%async_computation.7 | async-start | bytes 4194304
  294.4 110.5 %collective-permute-start.8 = (bf16[8,48,768]{2,1,0:T(8,128)(2,1)}, bf16[8,48,768]{2,1,0:T(8,128)(2,1)}, u32[]{:S(2)}, u32[]{:S(2)}) collective-permute-start(bf16[8,48,768]{2,1,0:T(8,128)(2,1)} %get-tuple-element.129), channel_id=1, source_target_pairs={{0,3},{1,0},{2,1},{3,2},{4,7},{5,4},{6,5},{7,6},{8,11},{9,8},{10,9... | collective-permute-start | bytes 1769480 | tf_op jit(solution)/shard_map/ppermute | solution.py:685
  296.9 0.9 copy-start.11
  296.9 1.0 copy-start.16
  296.9 108.1 %collective-permute-start.7 = (bf16[8,48,768]{2,1,0:T(8,128)(2,1)}, bf16[8,48,768]{2,1,0:T(8,128)(2,1)}, u32[]{:S(2)}, u32[]{:S(2)}) collective-permute-start(bf16[8,48,768]{2,1,0:T(8,128)(2,1)} %get-tuple-element.130), channel_id=1, source_target_pairs={{0,2},{1,3},{2,0},{3,1},{4,6},{5,7},{6,4},{7,5},{8,10},{9,11},{10,... | collective-permute-start | bytes 1769480 | tf_op jit(solution)/shard_map/ppermute | solution.py:685
  297.9 1.2 copy-start.29
  297.9 2.3 copy-start.35
  297.9 2.3 copy-start.28
  297.9 2.4 copy-start.48
  299.1 102.6 %copy-start.6 = (f32[96,1536]{1,0:T(8,128)S(1)}, f32[96,1536]{1,0:T(8,128)}, u32[]{:S(2)}) copy-start(f32[96,1536]{1,0:T(8,128)} %param.26) | copy-start | bytes 1769476
  299.1 102.6 %copy-start.7 = (f32[96,1536]{1,0:T(8,128)S(1)}, f32[96,1536]{1,0:T(8,128)}, u32[]{:S(2)}) copy-start(f32[96,1536]{1,0:T(8,128)} %get-tuple-element.86) | copy-start | bytes 1769476
  299.1 102.6 %copy-start.13 = (f32[96,1536]{1,0:T(8,128)S(1)}, f32[96,1536]{1,0:T(8,128)}, u32[]{:S(2)}) copy-start(f32[96,1536]{1,0:T(8,128)} %param.33) | copy-start | bytes 1769476
  299.1 102.6 %copy-start.14 = (f32[96,1536]{1,0:T(8,128)S(1)}, f32[96,1536]{1,0:T(8,128)}, u32[]{:S(2)}) copy-start(f32[96,1536]{1,0:T(8,128)} %param.40) | copy-start | bytes 1769476
  400.8 17.5 %collective-permute-start.6 = (bf16[8,48,768]{2,1,0:T(8,128)(2,1)}, bf16[8,48,768]{2,1,0:T(8,128)(2,1)}, u32[]{:S(2)}, u32[]{:S(2)}) collective-permute-start(bf16[8,48,768]{2,1,0:T(8,128)(2,1)} %get-tuple-element.131), channel_id=1, source_target_pairs={{0,1},{1,2},{2,3},{3,0},{4,5},{5,6},{6,7},{7,4},{8,9},{9,10},{10,1... | collective-permute-start | bytes 1769480 | tf_op jit(solution)/shard_map/ppermute | solution.py:685
  401.7 16.8 %copy-start.42 = (f32[3,48]{1,0:T(4,128)S(1)}, f32[3,48]{1,0:T(4,128)}, u32[]{:S(2)}) copy-start(f32[3,48]{1,0:T(4,128)} %param.31) | copy-start | bytes 1732
  401.7 16.8 %copy-start.46 = (f32[3,48]{1,0:T(4,128)S(1)}, f32[3,48]{1,0:T(4,128)}, u32[]{:S(2)}) copy-start(f32[3,48]{1,0:T(4,128)} %param.38) | copy-start | bytes 1732
  401.7 16.8 %copy-start.47 = (f32[3,48]{1,0:T(4,128)S(1)}, f32[3,48]{1,0:T(4,128)}, u32[]{:S(2)}) copy-start(f32[3,48]{1,0:T(4,128)} %param.45) | copy-start | bytes 1732
  401.8 18.0 %copy-start.8 = (bf16[8,48,768]{2,1,0:T(8,128)(2,1)S(1)}, bf16[8,48,768]{2,1,0:T(8,128)(2,1)}, u32[]{:S(2)}) copy-start(bf16[8,48,768]{2,1,0:T(8,128)(2,1)} %get-tuple-element.90) | copy-start | bytes 1769476
  418.3 27.6 %copy-start.27 = (f32[5,256]{1,0:T(8,128)}, f32[5,256]{1,0:T(8,128)S(1)}, u32[]{:S(2)}) copy-start(f32[5,256]{1,0:T(8,128)S(1)} %reduce_sum.138) | copy-start | bytes 15364
  418.5 26.8 %copy-start.40 = (f32[3,48]{1,0:T(4,128)}, f32[3,48]{1,0:T(4,128)S(1)}, u32[]{:S(2)}) copy-start(f32[3,48]{1,0:T(4,128)S(1)} %reshape.192) | copy-start | bytes 1732
  419.7 27.5 %copy-start.24 = (f32[3072]{0:T(1024)}, f32[3072]{0:T(1024)S(1)}, u32[]{:S(2)}) copy-start(f32[3072]{0:T(1024)S(1)} %reshape.188) | copy-start | bytes 36868
  419.7 28.1 %copy-start.18 = (f32[1,5,8,384]{3,1,2,0:T(8,128)}, f32[1,5,8,384]{3,1,2,0:T(8,128)S(1)}, u32[]{:S(2)}) copy-start(f32[1,5,8,384]{3,1,2,0:T(8,128)S(1)} %copy.105) | copy-start | bytes 184324
  436.1 9.8 %copy-start.26 = (f32[5,256]{1,0:T(8,128)S(1)}, f32[5,256]{1,0:T(8,128)}, u32[]{:S(2)}) copy-start(f32[5,256]{1,0:T(8,128)} %param.30) | copy-start | bytes 15364
  436.1 9.8 %copy-start.38 = (f32[5,256]{1,0:T(8,128)S(1)}, f32[5,256]{1,0:T(8,128)}, u32[]{:S(2)}) copy-start(f32[5,256]{1,0:T(8,128)} %param.37) | copy-start | bytes 15364
  436.1 9.8 %copy-start.39 = (f32[5,256]{1,0:T(8,128)S(1)}, f32[5,256]{1,0:T(8,128)}, u32[]{:S(2)}) copy-start(f32[5,256]{1,0:T(8,128)} %param.44) | copy-start | bytes 15364
  436.3 10.3 %copy-start.20 = (f32[1536]{0:T(1024)S(1)}, f32[1536]{0:T(1024)}, u32[]{:S(2)}) copy-start(f32[1536]{0:T(1024)} %param.27) | copy-start | bytes 18436
  436.3 10.3 %copy-start.43 = (f32[1536]{0:T(1024)S(1)}, f32[1536]{0:T(1024)}, u32[]{:S(2)}) copy-start(f32[1536]{0:T(1024)} %param.34) | copy-start | bytes 18436
  436.3 10.3 %copy-start.44 = (f32[1536]{0:T(1024)S(1)}, f32[1536]{0:T(1024)}, u32[]{:S(2)}) copy-start(f32[1536]{0:T(1024)} %param.41) | copy-start | bytes 18436
  436.4 10.8 %copy-start.30 = (f32[3072]{0:T(1024)S(1)}, f32[3072]{0:T(1024)}, u32[]{:S(2)}) copy-start(f32[3072]{0:T(1024)} %param.28) | copy-start | bytes 36868
  436.4 10.8 %copy-start.31 = (f32[3072]{0:T(1024)S(1)}, f32[3072]{0:T(1024)}, u32[]{:S(2)}) copy-start(f32[3072]{0:T(1024)} %param.35) | copy-start | bytes 36868
  436.4 10.8 %copy-start.32 = (f32[3072]{0:T(1024)S(1)}, f32[3072]{0:T(1024)}, u32[]{:S(2)}) copy-start(f32[3072]{0:T(1024)} %param.42) | copy-start | bytes 36868
  437.1 10.8 %copy-start.21 = (f32[5,3072]{1,0:T(8,128)S(1)}, f32[5,3072]{1,0:T(8,128)}, u32[]{:S(2)}) copy-start(f32[5,3072]{1,0:T(8,128)} %param.29) | copy-start | bytes 184324
  437.1 10.8 %copy-start.22 = (f32[5,3072]{1,0:T(8,128)S(1)}, f32[5,3072]{1,0:T(8,128)}, u32[]{:S(2)}) copy-start(f32[5,3072]{1,0:T(8,128)} %param.36) | copy-start | bytes 184324
  437.1 10.8 %copy-start.23 = (f32[5,3072]{1,0:T(8,128)S(1)}, f32[5,3072]{1,0:T(8,128)}, u32[]{:S(2)}) copy-start(f32[5,3072]{1,0:T(8,128)} %param.43) | copy-start | bytes 184324
  437.1 11.5 %copy-start = (bf16[1,256,1536]{2,1,0:T(8,128)(2,1)S(1)}, bf16[1,256,1536]{2,1,0:T(8,128)(2,1)}, u32[]{:S(2)}) copy-start(bf16[1,256,1536]{2,1,0:T(8,128)(2,1)} %param.23) | copy-start | bytes 2359300
  445.3 4.8 %copy-start.4 = (bf16[1,256,1536]{2,1,0:T(8,128)(2,1)S(1)}, bf16[1,256,1536]{2,1,0:T(8,128)(2,1)}, u32[]{:S(2)}) copy-start(bf16[1,256,1536]{2,1,0:T(8,128)(2,1)} %param.24) | copy-start | bytes 2359300
  445.4 4.8 %copy-start.12 = (bf16[256,1536]{1,0:T(8,128)(2,1)S(1)}, bf16[256,1536]{1,0:T(8,128)(2,1)}, u32[]{:S(2)}) copy-start(bf16[256,1536]{1,0:T(8,128)(2,1)} %reduce-scatter.3.cloned.1.call-done) | copy-start | bytes 2359300
  445.4 4.8 %copy-start.34 = (f32[256]{0:T(256)S(1)}, f32[256]{0:T(256)}, u32[]{:S(2)}) copy-start(f32[256]{0:T(256)} %copy-done.33) | copy-start | bytes 3076
  445.4 4.8 %copy-start.45 = (f32[256]{0:T(256)S(1)}, f32[256]{0:T(256)}, u32[]{:S(2)}) copy-start(f32[256]{0:T(256)} %get-tuple-element.143) | copy-start | bytes 3076
Sparse Core Ops, SparseCore 0:
  11.7 61.2 all-gather.3
  74.9 45.3 all-gather.5
  177.1 75.0 reduce-scatter.2
  274.5 62.4 reduce-scatter.4

commit v6 on v5

--- a/solution.py
+++ b/solution.py
@@ -823,8 +823,9 @@
     )
 
     g_main = mm(normed_all, dmain, TN)
-    g_full = g_main
-    g_main = g_main.astype(bf16).reshape(n_seq, n_wsh, rows_in, 2 * width)
+    d_gain_part = jnp.sum(g_main * w_main.astype(f32), axis=1)
+    g_main, dmain = lax.optimization_barrier((g_main.astype(bf16), dmain))
+    g_main = g_main.reshape(n_seq, n_wsh, rows_in, 2 * width)
     g_parts = [lax.dynamic_index_in_dim(g_main, wsh_index, 1, keepdims=False)]
     for j in range(1, n_wsh):
         to = lax.rem(wsh_index + j, n_wsh)
@@ -839,9 +840,7 @@
     d_normed = mm(dmain, w_main, NT) + lax.dot_general(
         d_ext, w_ext, (((0,), (1,)), ((), ())), preferred_element_type=f32
     )
-    d_normed, mixed, g_full, d_ext = lax.optimization_barrier(
-        (d_normed.astype(bf16), mixed, g_full, d_ext)
-    )
+    d_normed, mixed = lax.optimization_barrier((d_normed.astype(bf16), mixed))
     block_out = (inputs + mixed.astype(f32))[None]
     d_normed = lax.psum_scatter(d_normed, "seq", scatter_dimension=0, tiled=True)
     d_normed = d_normed.astype(f32)
@@ -855,9 +854,7 @@
     g_ext = lax.dot_general(
         normed_all, d_ext, (((0,), (1,)), ((), ())), preferred_element_type=f32
     )
-    d_gain_part = jnp.sum(g_full * w_main.astype(f32), axis=1) + jnp.sum(
-        g_ext * w_ext.astype(f32), axis=1
-    )
+    d_gain_part = d_gain_part + jnp.sum(g_ext * w_ext.astype(f32), axis=1)
     g_ext = jnp.pad(g_ext.astype(bf16), ((0, 0), (0, -g_ext.shape[1] % LANES)))
     g_ext = g_ext.reshape(n_seq, n_wsh, rows_in, LANES)
 

time: 462 us -> 452 us (0.978)
  Pallas kernels: 273 us -> 195 us
  waiting for transfers between devices: 29.9 us -> 104 us
  other arithmetic: 36.1 us -> 31.2 us
    pallas_call x4, Pallas kernels: 129 us -> 51.8 us  [swap(): pl.pallas_call(functools.partial(swap_kernel, plan, n_seq, n_wsh), in_spe...]
    ppermute x9, waiting for transfers between devices: 29.2 us -> 103 us  [shift(): lax.ppermute(x, 'wshard', [(i, (i + j) % n_wsh) for i in range(n_wsh)])]
    unnamed x108 -> x102, local copies, waits for them, and re-layouts: 2.58 us -> 9.23 us
  transfers between devices with their start and end apart: 13 -> 13, of which waited for: 3 -> 5; matrix products, arithmetic and copies ran while one was open for 19% -> 18% of each run, Pallas kernels for 58% -> 42%
where the time goes in v6:
time: 452 us; the launch traced here: 451 us
  Pallas kernels  195 us (43%)
  waiting for transfers between devices  104 us (23%)
  matrix products  60.1 us (13%)
  local copies, waits for them, and re-layouts  33.2 us (7%)
  other arithmetic  31.2 us (7%)
  between operations  14.5 us (3%)
  starting transfers between devices  12.5 us (3%)
    ppermute x9, waiting for transfers between devices, shift(): lax.ppermute(x, 'wshard', [(i, (i + j) % n_wsh) for i in range(n_wsh)])  103 us
    pallas_call x1, Pallas kernels, spread_weights(): pl.pallas_call(functools.partial(weights_kernel, n_seq, n_wsh), in_specs=...  57.9 us
    pallas_call x4, Pallas kernels, swap(): pl.pallas_call(functools.partial(swap_kernel, plan, n_seq, n_wsh), in_spe...  51.8 us
    dot_general x7, matrix products, mm(): return lax.dot_general(a, b, dims, preferred_element_type=f32)  51.7 us
    pallas_call x1, Pallas kernels, mixer_backward(): pl.pallas_call(functools.partial(bwd_kernel, heads, count), grid=(count,)...  47.8 us
    pallas_call x1, Pallas kernels, mixer_forward(): pl.pallas_call(functools.partial(fwd_kernel, heads), grid=(count,), in_sp...  22.3 us
    ppermute x9, starting transfers between devices, shift(): lax.ppermute(x, 'wshard', [(i, (i + j) % n_wsh) for i in range(n_wsh)])  12.3 us
    unnamed x102, local copies, waits for them, and re-layouts  9.23 us
  transfers between devices with their start and end apart: 13, of which 5 were waited for; matrix products, arithmetic and copies ran while one was open for 18% of the time, Pallas kernels for 42%

profile of v6, /device:TPU:0, one launch (start us, length us, event | category | flops | bytes accessed | tf_op | source)
XLA Modules:
  0.0 450.9 jit_solution(16034183719545636508)
XLA Ops:
  7.3 1.5 fusion.13
  9.8 2.3 fusion.15
  12.1 0.7 all-gather.6.cloned.1.call-update
  13.1 0.7 convert_element_type.93
  13.9 0.9 copy.100
  15.3 57.9 %spread_weights.1 = bf16[8,4,48,1152]{3,2,1,0:T(8,128)(2,1)} custom-call(bf16[8,48,768]{2,1,0:T(8,128)(2,1)} %bitcast.98, bf16[48,384]{1,0:T(8,128)(2,1)} %pad.24.small), custom_call_target="tpu_custom_call" | custom-call | bytes 200000000 | tf_op jit(solution)/shard_map/spread_weights/pallas_call | solution.py:517
  73.3 3.3 collective-permute-start.2
  76.6 0.6 collective-permute-start
  78.6 0.8 dynamic_slice.36
  80.0 0.7 constant_dynamic-slice_fusion.4
  81.3 1.1 broadcast_in_dim.51
  82.4 1.7 bitcast_dynamic-update-slice_fusion.3
  84.2 13.1 %collective-permute-done = bf16[96,1536]{1,0:T(8,128)(2,1)} collective-permute-done((bf16[96,1536]{1,0:T(8,128)(2,1)}, bf16[96,1536]{1,0:T(8,128)(2,1)}, u32[]{:S(2)}, u32[]{:S(2)}) %collective-permute-start) | collective-permute-done | bytes 294944 | tf_op jit(solution)/shard_map/ppermute | solution.py:685
  97.3 1.7 bitcast_dynamic-update-slice_fusion.2
  99.0 2.7 collective-permute-done.1
  101.7 1.7 bitcast_dynamic-update-slice_fusion.1
  103.4 1.7 bitcast_dynamic-update-slice_fusion
  105.1 11.8 %convolution_convert_fusion.1.main_ref.small_ref.main_prev.small_prev = bf16[2048,1152]{1,0:T(8,128)(2,1)} fusion(bf16[2048,1536]{1,0:T(8,128)(2,1)} %all-gather.4.cloned.1.call-done, bf16[1536,1152]{1,0:T(8,128)(2,1)S(1)} %bitcast.93), kind=kOutput, calls=%fused_computation.2 | convolution fusion | flops 7250116608 | bytes 14548992 | tf_op jit(solution)/shard_map/dot_general | solution.py:35
  116.9 22.3 %mixer_forward.1 = (bf16[2048,384]{1,0:T(8,128)(2,1)}, f32[2048,384]{1,0:T(8,128)}, f32[16,128,384]{2,1,0:T(8,128)}) custom-call(bf16[2048,1152]{1,0:T(8,128)(2,1)} %convolution_convert_fusion.1.main_ref.small_ref.main_prev.small_prev, bf16[2048,1152]{1,0:T(8,128)(2,1)} %convolution_convert_fusion.1.main_ref.small_ref.main_prev.small_prev, ...), custom_call_target="tpu_custom_call" | custom-call | bytes 70000000 | tf_op jit(solution)/shard_map/mixer_forward/pallas_call | solution.py:193
  139.2 8.7 %fusion.4 = (f32[2048]{0:T(1024)S(1)}, f32[2048]{0:T(1024)S(1)}, f32[384,2048]{0,1:T(8,128)}) fusion(bf16[2048,384]{1,0:T(8,128)(2,1)} %get-tuple-element.71, f32[384]{0:T(512)S(1)} %dynamic_slice.36, bf16[384,1536]{1,0:T(8,128)(2,1)} %bitcast.9, bf16[1,2048,1536]{2,1,0:T(8,128)(2,1)} %all-gather.6.cloned.1.call-done), kind=kOutput, calls=%fused_computation.13 | convolution fusion | flops 2420633600 | bytes 12207616 | tf_op jit(solution)/shard_map/dot_general | solution.py:35
  148.5 7.3 %sum_over_seq.1 = f32[32,128]{1,0:T(8,128)} custom-call(f32[32,128]{1,0:T(8,128)} %reshape.177.x_ref), custom_call_target="tpu_custom_call" | custom-call | tf_op jit(solution)/shard_map/sum_over_seq/pallas_call | solution.py:658
  155.9 0.7 multiply_multiply_fusion.5
  156.6 1.3 multiply_bitcast_fusion
  157.9 7.9 %convolution_convert_fusion = bf16[2048,1536]{1,0:T(8,128)(2,1)} fusion(bf16[384,1536]{1,0:T(8,128)(2,1)} %bitcast.9, bf16[2048,384]{1,0:T(8,128)(2,1)} %get-tuple-element.71, f32[2048]{0:T(1024)S(1)} %get-tuple-element.144, f32[384]{0:T(512)} %copy-done.34), kind=kOutput, calls=%fused_computation.1 | convolution fusion | flops 2422210560 | bytes 9053696 | tf_op jit(solution)/shard_map/dot_general | solution.py:35
  165.8 4.8 %fusion.12 = (f32[384]{0:T(512)}, bf16[2048,384]{1,0:T(8,128)(2,1)}) fusion(bf16[2048,384]{1,0:T(8,128)(2,1)} %get-tuple-element.71, f32[384,2048]{0,1:T(8,128)} %get-tuple-element.147, f32[2048]{0:T(1024)S(1)} %get-tuple-element.144, f32[2048]{0:T(1024)} %get-tuple-element.143, f32[2048]{0:T(1024)S(1)} %multiply_multiply_fusion.5, f32[384]{0:T(512)} %copy-done.34), kind=kLoop, calls=%fused_computation.21 | loop fusion | flops 7863936 | bytes 6319104 | tf_op jit(solution)/shard_map/reduce_sum | solution.py:810
  170.5 6.9 %fusion = f32[384,1536]{1,0:T(8,128)} fusion(bf16[1,2048,1536]{2,1,0:T(8,128)(2,1)} %all-gather.6.cloned.1.call-done, bf16[2048,384]{1,0:T(8,128)(2,1)S(1)} %copy-done.7, f32[2048]{0:T(1024)S(1)} %get-tuple-element.144, f32[384]{0:T(512)S(1)} %copy-done.35), kind=kOutput, calls=%fused_computation.3 | convolution fusion | flops 2419064832 | bytes 10233344 | tf_op jit(solution)/shard_map/dot_general | solution.py:35
  177.5 1.6 slice.91
  179.1 1.0 copy.85
  180.1 4.3 copy.93
  184.5 1.1 convolution_convert_fusion.2
  185.6 47.8 %mixer_backward.1 = (bf16[2048,768]{1,0:T(8,128)(2,1)}, bf16[256,2048]{1,0:T(8,128)(2,1)}, bf16[16,2048]{1,0:T(8,128)(2,1)}, f32[8,640]{1,0:T(8,128)}, f32[8,128]{1,0:T(8,128)}) custom-call(bf16[2048,1152]{1,0:T(8,128)(2,1)} %convolution_convert_fusion.1.main_ref.small_ref.main_prev.small_prev, ...), custom_call_target="tpu_custom_call" | custom-call | bytes 160000000 | tf_op jit(solution)/shard_map/mixer_backward/pallas_call | solution.py:377
  233.5 16.0 %shard_map.462 = bf16[8,32,2048]{2,1,0:T(8,128)(2,1)} custom-call(bf16[8,32,2048]{2,1,0:T(8,128)(2,1)} %bitcast.101), custom_call_target="tpu_custom_call" | custom-call | tf_op jit(solution)/shard_map/pallas_call | solution.py:623
  249.5 2.1 reduce_sum.128
  251.5 10.2 %multiply_reduce_fusion = (f32[1536]{0:T(1024)S(1)}, bf16[1536,768]{0,1:T(8,128)(2,1)}) fusion(bf16[1536,768]{0,1:T(8,128)(2,1)} %copy.93, bf16[2048,1536]{1,0:T(8,128)(2,1)} %all-gather.4.cloned.1.call-done, bf16[2048,768]{1,0:T(8,128)(2,1)} %get-tuple-element.75), kind=kOutput, calls=%fused_computation.12 | convolution fusion | flops 4836555264 | bytes 14161920 | tf_op jit(solution)/shard_map/dot_general | solution.py:35
  261.8 5.1 %fusion.42 = f32[2048,1536]{1,0:T(8,128)S(1)} fusion(bf16[2048,768]{1,0:T(8,128)(2,1)S(1)} %copy-done.46, bf16[1536,1152]{1,0:T(8,128)(2,1)S(1)} %bitcast.96), kind=kOutput, calls=%fused_computation.125 | convolution fusion | flops 4831838208 | bytes 18087936 | tf_op jit(solution)/shard_map/dot_general | solution.py:35
  266.9 4.5 add_convert_fusion
  272.1 0.7 slice.77
  273.2 3.9 multiply_reduce_fusion.1
  277.4 0.8 pad.27.clone
  278.9 15.3 %shard_map.463 = (bf16[4,8,48,128]{3,2,1,0:T(8,128)(2,1)}, f32[4,48,128]{2,1,0:T(8,128)}) custom-call(bf16[8,4,48,128]{3,2,1,0:T(8,128)(2,1)} %bitcast.100, f32[48,128]{1,0:T(8,128)} %pad_bitcast_fusion.refs_1_), custom_call_target="tpu_custom_call" | custom-call | tf_op jit(solution)/shard_map/pallas_call | solution.py:623
  294.2 1.5 reduce_sum.134.refs_0_
  295.7 8.9 %shard_map.464 = f32[8,48,128]{2,1,0:T(8,128)} custom-call(f32[48,128]{1,0:T(8,128)} %reduce_sum.134.refs_0_), custom_call_target="tpu_custom_call" | custom-call | tf_op jit(solution)/shard_map/pallas_call | solution.py:623
  304.7 1.0 copy.101
  305.7 1.7 reduce_sum.135.refs_1_
  308.9 1.3 constant_dynamic-slice_fusion
  310.2 2.7 collective-permute-start.5
  313.5 2.9 copy.87
  316.7 3.2 collective-permute-start.8
  320.0 1.1 collective-permute-start.7
  322.3 0.6 multiply_subtract_fusion.4
  323.6 0.8 multiply_subtract_fusion.1
  324.4 2.6 collective-permute-done.5
  327.0 0.7 collective-permute-start.6
  327.7 37.4 %collective-permute-done.4 = f32[96,1536]{1,0:T(8,128)} collective-permute-done((f32[96,1536]{1,0:T(8,128)}, f32[96,1536]{1,0:T(8,128)}, u32[]{:S(2)}, u32[]{:S(2)}) %collective-permute-start.4) | collective-permute-done | bytes 589856 | tf_op jit(solution)/shard_map/ppermute | solution.py:685
  365.0 3.1 multiply_subtract_fusion
  368.2 47.3 %collective-permute-done.7 = bf16[8,48,768]{2,1,0:T(8,128)(2,1)S(1)} collective-permute-done((bf16[8,48,768]{2,1,0:T(8,128)(2,1)S(1)}, bf16[8,48,768]{2,1,0:T(8,128)(2,1)S(1)}, u32[]{:S(2)}, u32[]{:S(2)}) %collective-permute-start.7) | collective-permute-done | bytes 589856 | tf_op jit(solution)/shard_map/ppermute | solution.py:685
  415.5 1.1 add_convert_fusion.1.refs_0_
  416.6 11.6 %shard_map.465 = (bf16[8,48,768]{2,1,0:T(8,128)(2,1)}, bf16[8,48,128]{2,1,0:T(8,128)(2,1)}) custom-call(bf16[8,48,768]{2,1,0:T(8,128)(2,1)} %add_convert_fusion.1.refs_0_, bf16[8,48,128]{2,1,0:T(8,128)(2,1)} %reduce_sum.135.refs_1_), custom_call_target="tpu_custom_call" | custom-call | tf_op jit(solution)/shard_map/pallas_call | solution.py:623
  428.2 1.0 slice.95
  429.1 0.9 copy.88
  430.4 0.7 fusion.30.ext_ref
  431.1 8.3 %adam_in.1 = (f32[48,6448]{1,0:T(8,128)}, f32[48,6448]{1,0:T(8,128)}, f32[48,6448]{1,0:T(8,128)}, f32[48,6448]{1,0:T(8,128)}) custom-call(bf16[8,48,768]{2,1,0:T(8,128)(2,1)} %get-tuple-element.95.g_ref, bf16[48,768]{1,0:T(8,128)(2,1)} %fusion.30.ext_ref, f32[48,6448]{1,0:T(8,128)} %p_ref.1, f32[48,6448]{1,0:T(8,128)} %m_ref.1, f32[48,6448]{1,0:T(8,128)} %v_ref.1), custom_call_target="tpu_custom_call" | custom-call | tf_op jit(solution)/shard_map/adam_in/pallas_call | solution.py:702
  439.4 1.5 fusion.20
  440.9 3.4 fusion.19
  (168 shorter events, 11.8 us)
Async XLA Ops:
  7.2 5.7 %copy-start.2 = (f32[48,6448]{1,0:T(8,128)S(1)}, f32[48,6448]{1,0:T(8,128)}, u32[]{:S(2)}) copy-start(f32[48,6448]{1,0:T(8,128)} %p_ref.1) | copy-start | bytes 3714052
  7.2 97.9 %all-gather.4.cloned.1.call-start = ((), (), s32[]{:S(2)}) async-start(), calls=%async_computation.2 | async-start | bytes 7077888 | tf_op jit(solution)/shard_map/all_gather | solution.py:758
  9.3 0.5 copy-start.31
  12.0 1.1 copy-start.4
  12.1 127.1 %all-gather.6.cloned.1.call-start = ((), (), s32[]{:S(2)}) async-start(), calls=%async_computation.5 | async-start | bytes 7077888 | tf_op jit(solution)/shard_map/all_gather | solution.py:760
  12.8 258.6 %reduce-scatter.3.cloned.1.call-start = ((), (), s32[]{:S(2)}) async-start(), calls=%async_computation.3 | async-start | bytes 7077888 | tf_op jit(solution)/shard_map/reduce_scatter | solution.py:815
  14.7 64.6 %copy-start.39 = (f32[3,48]{1,0:T(4,128)S(1)}, f32[3,48]{1,0:T(4,128)}, u32[]{:S(2)}) copy-start(f32[3,48]{1,0:T(4,128)} %param.31) | copy-start | bytes 1732
  14.7 66.0 %copy-start.24 = (f32[5,256]{1,0:T(8,128)S(1)}, f32[5,256]{1,0:T(8,128)}, u32[]{:S(2)}) copy-start(f32[5,256]{1,0:T(8,128)} %param.30) | copy-start | bytes 15364
  73.3 31.9 %copy-start.1 = (bf16[8,4,48,1152]{3,2,1,0:T(8,128)(2,1)S(1)}, bf16[8,4,48,1152]{3,2,1,0:T(8,128)(2,1)}, u32[]{:S(2)}) copy-start(bf16[8,4,48,1152]{3,2,1,0:T(8,128)(2,1)} %spread_weights.1) | copy-start | bytes 10616836
  73.3 30.2 %collective-permute-start.2 = (bf16[96,1536]{1,0:T(8,128)(2,1)}, bf16[96,1536]{1,0:T(8,128)(2,1)}, u32[]{:S(2)}, u32[]{:S(2)}) collective-permute-start(bf16[96,1536]{1,0:T(8,128)(2,1)} %convert_element_type.93), channel_id=1, source_target_pairs={{0,3},{1,0},{2,1},{3,2},{4,7},{5,4},{6,5},{7,6},{8,11},{9,8},{10,9... | collective-permute-start | bytes 884744 | tf_op jit(solution)/shard_map/ppermute | solution.py:685
  76.6 25.1 %collective-permute-start.1 = (bf16[96,1536]{1,0:T(8,128)(2,1)}, bf16[96,1536]{1,0:T(8,128)(2,1)}, u32[]{:S(2)}, u32[]{:S(2)}) collective-permute-start(bf16[96,1536]{1,0:T(8,128)(2,1)} %convert_element_type.93), channel_id=1, source_target_pairs={{0,2},{1,3},{2,0},{3,1},{4,6},{5,7},{6,4},{7,5},{8,10},{9,11},{10,... | collective-permute-start | bytes 884744 | tf_op jit(solution)/shard_map/ppermute | solution.py:685
  76.6 20.7 %collective-permute-start = (bf16[96,1536]{1,0:T(8,128)(2,1)}, bf16[96,1536]{1,0:T(8,128)(2,1)}, u32[]{:S(2)}, u32[]{:S(2)}) collective-permute-start(bf16[96,1536]{1,0:T(8,128)(2,1)} %convert_element_type.93), channel_id=1, source_target_pairs={{0,1},{1,2},{2,3},{3,0},{4,5},{5,6},{6,7},{7,4},{8,9},{9,10},{10,1... | collective-permute-start | bytes 884744 | tf_op jit(solution)/shard_map/ppermute | solution.py:685
  77.3 0.6 copy-start.15
  79.3 59.9 %copy-start.34 = (f32[384]{0:T(512)}, f32[384]{0:T(512)S(1)}, u32[]{:S(2)}) copy-start(f32[384]{0:T(512)S(1)} %dynamic_slice.36) | copy-start | bytes 4612
  165.8 4.8 %copy-start.7 = (bf16[2048,384]{1,0:T(8,128)(2,1)S(1)}, bf16[2048,384]{1,0:T(8,128)(2,1)}, u32[]{:S(2)}) copy-start(bf16[2048,384]{1,0:T(8,128)(2,1)} %get-tuple-element.71) | copy-start | bytes 4718596
  165.8 4.8 %copy-start.35 = (f32[384]{0:T(512)S(1)}, f32[384]{0:T(512)}, u32[]{:S(2)}) copy-start(f32[384]{0:T(512)} %copy-done.34) | copy-start | bytes 4612
  177.5 261.9 %reduce-scatter.5.cloned.1.call-start = ((), (), s32[]{:S(2)}) async-start(), calls=%async_computation.4 | async-start | bytes 7077888 | tf_op jit(solution)/shard_map/reduce_scatter | solution.py:845
  251.5 10.2 %copy-start.46 = (bf16[2048,768]{1,0:T(8,128)(2,1)S(1)}, bf16[2048,768]{1,0:T(8,128)(2,1)}, u32[]{:S(2)}) copy-start(bf16[2048,768]{1,0:T(8,128)(2,1)} %get-tuple-element.75) | copy-start | bytes 9437188
  261.7 5.2 %copy-start.8 = (bf16[32,2048]{1,0:T(8,128)(2,1)S(1)}, bf16[32,2048]{1,0:T(8,128)(2,1)}, u32[]{:S(2)}) copy-start(bf16[32,2048]{1,0:T(8,128)(2,1)} %reduce_sum.128) | copy-start | bytes 393220
  261.7 5.2 %copy-start.13 = (bf16[1536,48]{0,1:T(8,128)(2,1)S(1)}, bf16[1536,48]{0,1:T(8,128)(2,1)}, u32[]{:S(2)}) copy-start(bf16[1536,48]{0,1:T(8,128)(2,1)} %convolution_convert_fusion.2) | copy-start | bytes 442372
  261.7 5.2 %copy-start.17 = (bf16[16,2048]{1,0:T(8,128)(2,1)S(1)}, bf16[16,2048]{1,0:T(8,128)(2,1)}, u32[]{:S(2)}) copy-start(bf16[16,2048]{1,0:T(8,128)(2,1)} %get-tuple-element.77) | copy-start | bytes 196612
  271.4 0.7 copy-start.27
  271.4 1.7 copy-start.9
  271.4 1.7 copy-start.14
  271.4 1.7 copy-start.18
  273.2 5.1 %copy-start.33 = (f32[384]{0:T(512)S(1)}, f32[384]{0:T(512)}, u32[]{:S(2)}) copy-start(f32[384]{0:T(512)} %get-tuple-element.127) | copy-start | bytes 4612
  277.1 30.5 %copy-start.40 = (f32[3,48]{1,0:T(4,128)S(1)}, f32[3,48]{1,0:T(4,128)}, u32[]{:S(2)}) copy-start(f32[3,48]{1,0:T(4,128)} %param.31) | copy-start | bytes 1732
  277.1 30.5 %copy-start.44 = (f32[3,48]{1,0:T(4,128)S(1)}, f32[3,48]{1,0:T(4,128)}, u32[]{:S(2)}) copy-start(f32[3,48]{1,0:T(4,128)} %param.38) | copy-start | bytes 1732
  277.2 30.5 %copy-start.45 = (f32[3,48]{1,0:T(4,128)S(1)}, f32[3,48]{1,0:T(4,128)}, u32[]{:S(2)}) copy-start(f32[3,48]{1,0:T(4,128)} %param.45) | copy-start | bytes 1732
  277.2 31.7 %copy-start.6 = (f32[384,1536]{1,0:T(8,128)S(1)}, f32[384,1536]{1,0:T(8,128)}, u32[]{:S(2)}) copy-start(f32[384,1536]{1,0:T(8,128)} %fusion) | copy-start | bytes 7077892
  307.5 14.2 %copy-start.26 = (f32[5,256]{1,0:T(8,128)}, f32[5,256]{1,0:T(8,128)S(1)}, u32[]{:S(2)}) copy-start(f32[5,256]{1,0:T(8,128)S(1)} %reduce_sum.138) | copy-start | bytes 15364
  307.7 2.5 copy-start.38
  308.8 14.1 %copy-start.23 = (f32[3072]{0:T(1024)}, f32[3072]{0:T(1024)S(1)}, u32[]{:S(2)}) copy-start(f32[3072]{0:T(1024)S(1)} %reshape.188) | copy-start | bytes 36868
  308.9 14.7 %copy-start.16 = (f32[1,5,8,384]{3,1,2,0:T(8,128)}, f32[1,5,8,384]{3,1,2,0:T(8,128)S(1)}, u32[]{:S(2)}) copy-start(f32[1,5,8,384]{3,1,2,0:T(8,128)S(1)} %copy.97) | copy-start | bytes 184324
  310.2 16.8 %collective-permute-start.5 = (f32[96,1536]{1,0:T(8,128)}, f32[96,1536]{1,0:T(8,128)}, u32[]{:S(2)}, u32[]{:S(2)}) collective-permute-start(f32[96,1536]{1,0:T(8,128)} %get-tuple-element.135), channel_id=1, source_target_pairs={{0,3},{1,0},{2,1},{3,2},{4,7},{5,4},{6,5},{7,6},{8,11},{9,8},{10,9... | collective-permute-start | bytes 1769480 | tf_op jit(solution)/shard_map/ppermute | solution.py:685
  312.9 52.1 %collective-permute-start.4 = (f32[96,1536]{1,0:T(8,128)}, f32[96,1536]{1,0:T(8,128)}, u32[]{:S(2)}, u32[]{:S(2)}) collective-permute-start(f32[96,1536]{1,0:T(8,128)} %get-tuple-element.136), channel_id=1, source_target_pairs={{0,2},{1,3},{2,0},{3,1},{4,6},{5,7},{6,4},{7,5},{8,10},{9,11},{10,... | collective-permute-start | bytes 1769480 | tf_op jit(solution)/shard_map/ppermute | solution.py:685
  312.9 52.1 %collective-permute-start.3 = (f32[96,1536]{1,0:T(8,128)}, f32[96,1536]{1,0:T(8,128)}, u32[]{:S(2)}, u32[]{:S(2)}) collective-permute-start(f32[96,1536]{1,0:T(8,128)} %get-tuple-element.137), channel_id=1, source_target_pairs={{0,1},{1,2},{2,3},{3,0},{4,5},{5,6},{6,7},{7,4},{8,9},{9,10},{10,1... | collective-permute-start | bytes 1769480 | tf_op jit(solution)/shard_map/ppermute | solution.py:685
  316.4 5.3 %copy-start.25 = (f32[5,256]{1,0:T(8,128)S(1)}, f32[5,256]{1,0:T(8,128)}, u32[]{:S(2)}) copy-start(f32[5,256]{1,0:T(8,128)} %param.30) | copy-start | bytes 15364
  316.4 5.3 %copy-start.36 = (f32[5,256]{1,0:T(8,128)S(1)}, f32[5,256]{1,0:T(8,128)}, u32[]{:S(2)}) copy-start(f32[5,256]{1,0:T(8,128)} %param.37) | copy-start | bytes 15364
  316.4 5.3 %copy-start.37 = (f32[5,256]{1,0:T(8,128)S(1)}, f32[5,256]{1,0:T(8,128)}, u32[]{:S(2)}) copy-start(f32[5,256]{1,0:T(8,128)} %param.44) | copy-start | bytes 15364
  316.4 5.9 %copy-start.19 = (f32[1536]{0:T(1024)S(1)}, f32[1536]{0:T(1024)}, u32[]{:S(2)}) copy-start(f32[1536]{0:T(1024)} %param.27) | copy-start | bytes 18436
  316.4 5.9 %copy-start.41 = (f32[1536]{0:T(1024)S(1)}, f32[1536]{0:T(1024)}, u32[]{:S(2)}) copy-start(f32[1536]{0:T(1024)} %param.34) | copy-start | bytes 18436
  316.4 5.9 %copy-start.42 = (f32[1536]{0:T(1024)S(1)}, f32[1536]{0:T(1024)}, u32[]{:S(2)}) copy-start(f32[1536]{0:T(1024)} %param.41) | copy-start | bytes 18436
  316.5 6.5 %copy-start.28 = (f32[3072]{0:T(1024)S(1)}, f32[3072]{0:T(1024)}, u32[]{:S(2)}) copy-start(f32[3072]{0:T(1024)} %param.28) | copy-start | bytes 36868
  316.5 6.5 %copy-start.29 = (f32[3072]{0:T(1024)S(1)}, f32[3072]{0:T(1024)}, u32[]{:S(2)}) copy-start(f32[3072]{0:T(1024)} %param.35) | copy-start | bytes 36868
  316.5 6.5 %copy-start.30 = (f32[3072]{0:T(1024)S(1)}, f32[3072]{0:T(1024)}, u32[]{:S(2)}) copy-start(f32[3072]{0:T(1024)} %param.42) | copy-start | bytes 36868
  316.5 7.1 %copy-start.20 = (f32[5,3072]{1,0:T(8,128)S(1)}, f32[5,3072]{1,0:T(8,128)}, u32[]{:S(2)}) copy-start(f32[5,3072]{1,0:T(8,128)} %param.29) | copy-start | bytes 184324
  316.5 7.1 %copy-start.21 = (f32[5,3072]{1,0:T(8,128)S(1)}, f32[5,3072]{1,0:T(8,128)}, u32[]{:S(2)}) copy-start(f32[5,3072]{1,0:T(8,128)} %param.36) | copy-start | bytes 184324
  316.5 7.1 %copy-start.22 = (f32[5,3072]{1,0:T(8,128)S(1)}, f32[5,3072]{1,0:T(8,128)}, u32[]{:S(2)}) copy-start(f32[5,3072]{1,0:T(8,128)} %param.43) | copy-start | bytes 184324
  316.5 48.5 %copy-start.5 = (f32[96,1536]{1,0:T(8,128)S(1)}, f32[96,1536]{1,0:T(8,128)}, u32[]{:S(2)}) copy-start(f32[96,1536]{1,0:T(8,128)} %param.26) | copy-start | bytes 1769476
  316.5 48.5 %copy-start.11 = (f32[96,1536]{1,0:T(8,128)S(1)}, f32[96,1536]{1,0:T(8,128)}, u32[]{:S(2)}) copy-start(f32[96,1536]{1,0:T(8,128)} %param.33) | copy-start | bytes 1769476
  316.6 48.5 %copy-start.12 = (f32[96,1536]{1,0:T(8,128)S(1)}, f32[96,1536]{1,0:T(8,128)}, u32[]{:S(2)}) copy-start(f32[96,1536]{1,0:T(8,128)} %param.40) | copy-start | bytes 1769476
  316.7 51.4 %collective-permute-start.8 = (bf16[8,48,768]{2,1,0:T(8,128)(2,1)S(1)}, bf16[8,48,768]{2,1,0:T(8,128)(2,1)S(1)}, u32[]{:S(2)}, u32[]{:S(2)}) collective-permute-start(bf16[8,48,768]{2,1,0:T(8,128)(2,1)S(1)} %get-tuple-element.131), channel_id=1, source_target_pairs={{0,3},{1,0},{2,1},{3,2},{4,7},{5,4},{6,5},{7,6},{8,11},{9,8},{10,9... | collective-permute-start | bytes 1769480 | tf_op jit(solution)/shard_map/ppermute | solution.py:685
  320.0 95.5 %collective-permute-start.7 = (bf16[8,48,768]{2,1,0:T(8,128)(2,1)S(1)}, bf16[8,48,768]{2,1,0:T(8,128)(2,1)S(1)}, u32[]{:S(2)}, u32[]{:S(2)}) collective-permute-start(bf16[8,48,768]{2,1,0:T(8,128)(2,1)S(1)} %get-tuple-element.132), channel_id=1, source_target_pairs={{0,2},{1,3},{2,0},{3,1},{4,6},{5,7},{6,4},{7,5},{8,10},{9,11},{10,... | collective-permute-start | bytes 1769480 | tf_op jit(solution)/shard_map/ppermute | solution.py:685
  327.0 88.5 %collective-permute-start.6 = (bf16[8,48,768]{2,1,0:T(8,128)(2,1)S(1)}, bf16[8,48,768]{2,1,0:T(8,128)(2,1)S(1)}, u32[]{:S(2)}, u32[]{:S(2)}) collective-permute-start(bf16[8,48,768]{2,1,0:T(8,128)(2,1)S(1)} %get-tuple-element.133), channel_id=1, source_target_pairs={{0,1},{1,2},{2,3},{3,0},{4,5},{5,6},{6,7},{7,4},{8,9},{9,10},{10,1... | collective-permute-start | bytes 1769480 | tf_op jit(solution)/shard_map/ppermute | solution.py:685
  430.2 9.2 %copy-start = (bf16[1,256,1536]{2,1,0:T(8,128)(2,1)S(1)}, bf16[1,256,1536]{2,1,0:T(8,128)(2,1)}, u32[]{:S(2)}) copy-start(bf16[1,256,1536]{2,1,0:T(8,128)(2,1)} %param.23) | copy-start | bytes 2359300
  431.1 9.8 %copy-start.3 = (bf16[1,256,1536]{2,1,0:T(8,128)(2,1)S(1)}, bf16[1,256,1536]{2,1,0:T(8,128)(2,1)}, u32[]{:S(2)}) copy-start(bf16[1,256,1536]{2,1,0:T(8,128)(2,1)} %param.24) | copy-start | bytes 2359300
  431.1 9.8 %copy-start.10 = (bf16[256,1536]{1,0:T(8,128)(2,1)S(1)}, bf16[256,1536]{1,0:T(8,128)(2,1)}, u32[]{:S(2)}) copy-start(bf16[256,1536]{1,0:T(8,128)(2,1)} %reduce-scatter.3.cloned.1.call-done) | copy-start | bytes 2359300
  431.1 9.8 %copy-start.32 = (f32[256]{0:T(256)S(1)}, f32[256]{0:T(256)}, u32[]{:S(2)}) copy-start(f32[256]{0:T(256)} %copy-done.31) | copy-start | bytes 3076
  431.1 9.8 %copy-start.43 = (f32[256]{0:T(256)S(1)}, f32[256]{0:T(256)}, u32[]{:S(2)}) copy-start(f32[256]{0:T(256)} %get-tuple-element.145) | copy-start | bytes 3076
Sparse Core Ops, SparseCore 0:
  12.2 61.2 all-gather.3
  75.4 45.4 all-gather.5
  177.6 71.9 reduce-scatter.2
  271.6 65.3 reduce-scatter.4
